TPU v7x, 32 devices: a whole 2x2x4 slice. The times are simulated.
32 devices in a mesh: dp: 4 (over x, core), seq: 8 (over z, y).
Axes of the slice: x: 2, y: 2, z: 4, core: 2. Of those that a mesh axis runs over, the one named last changes fastest.
Arguments:
- tokens: bfloat16 [8, 1024, 1024], P('dp', 'seq'), may hold values from -6 to 6
- segment_ids: int32 [8, 1024], P('dp', 'seq'), may hold values from 0 to 3, never falling along the last dimension, each value on 1 to 512 neighbouring positions
- variate_ids: int32 [8, 1024], P('dp', 'seq'), may hold values from 0 to 3
- time_ids: int32 [8, 1024], P('dp', 'seq'), may hold values from 0 to 2047
- pad_mask: int32 [8, 1024], P('dp', 'seq'), may hold values 0 or 1
- cotangent: bfloat16 [8, 1024, 1024], P('dp', 'seq'), may hold values from -6 to 6
- w_qkv: bfloat16 [1024, 3072], P('dp', 'seq'), may hold values from -0.1875 to 0.1875
- w_out: bfloat16 [1024, 1024], P('dp', 'seq'), may hold values from -4 to 4
- w_gate: bfloat16 [1024, 4096], P('dp', 'seq'), may hold values from -0.1875 to 0.1875
- w_up: bfloat16 [1024, 4096], P('dp', 'seq'), may hold values from -0.1875 to 0.1875
- w_down: bfloat16 [4096, 1024], P('dp', 'seq'), may hold values from -0.09375 to 0.09375
- gain_attn: bfloat16 [1024], replicated, may hold values from 0.5 to 1.5
- gain_ffn: bfloat16 [1024], replicated, may hold values from 0.5 to 1.5
- variate_bias: bfloat16 [16], replicated, may hold values from -3 to 3
Outputs:
- output: bfloat16 [8, 1024, 1024], P('dp', 'seq')
- input_grad: bfloat16 [8, 1024, 1024], P('dp', 'seq')
- grad_w_qkv: float32 [1024, 3072], P('dp', 'seq')
- grad_w_out: float32 [1024, 1024], P('dp', 'seq')
- grad_w_gate: float32 [1024, 4096], P('dp', 'seq')
- grad_w_up: float32 [1024, 4096], P('dp', 'seq')
- grad_w_down: float32 [4096, 1024], P('dp', 'seq')
- grad_gain_attn: float32 [1024], replicated
- grad_gain_ffn: float32 [1024], replicated
- grad_variate_bias: float32 [16], replicated
Inputs may be any that keep to these rules, and one draw needn't show every extreme that they name: `segment_ids`: along each sequence the ids never fall; a document spans 1 to 512 positions, and one spans exactly that many.
All inputs are finite; a program needn't handle non-finite values. No bound on the sum of `pad_mask` on one device may be relied on, other than what follows from the above.
Results may differ from a plain program's by a relative error of at most 0.015.
Values may be sent and summed in bfloat16 or wider, within the bound.
A program may use at most 256 MiB of HBM per device.

v0:
```python
import jax
import jax.numpy as jnp
from jax import lax
from jax.sharding import PartitionSpec as P

HEADS = 16
HEAD_DIM = 64
WINDOW = 512


EPSILON = 1e-06
NEGATIVE = -1e30


def passed_along(block, axis, distance):
    devices = range(lax.axis_size(axis))
    route = [(i - distance, i) for i in devices if i - distance in devices]
    return lax.ppermute(block, axis, route)


def norm_scale(hidden):
    return lax.rsqrt(jnp.mean(hidden * hidden, axis=-1, keepdims=True) + EPSILON)


def norm_back(grad_in, hidden, inv_rms):
    return inv_rms * grad_in - hidden * inv_rms * inv_rms * inv_rms * jnp.mean(
        grad_in * hidden, axis=-1, keepdims=True
    )


def rope_tables(time_row, half_dim):
    frequency = jnp.exp(-jnp.log(10000.0) * jnp.arange(half_dim, dtype=jnp.float32) / half_dim)
    angles = time_row.astype(jnp.float32)[:, None] * frequency[None, :]
    return (jnp.cos(angles)[:, None, :], jnp.sin(angles)[:, None, :])


def rotate(values_in, cos_table, sine_table):
    half_dim = cos_table.shape[-1]
    first_half = values_in[..., :half_dim]
    second_half = values_in[..., half_dim:]
    return jnp.concatenate(
        [
            first_half * cos_table - second_half * sine_table,
            second_half * cos_table + first_half * sine_table,
        ],
        axis=-1,
    )


def rotate_back(grad_in, cos_table, sine_table):
    half_dim = cos_table.shape[-1]
    first_half = grad_in[..., :half_dim]
    second_half = grad_in[..., half_dim:]
    return jnp.concatenate(
        [
            first_half * cos_table + second_half * sine_table,
            second_half * cos_table - first_half * sine_table,
        ],
        axis=-1,
    )


def masked_scores(query_rot, keys_all, labels_own, labels_keys, var_bias, hop_count):
    row_count = query_rot.shape[0]
    key_count = keys_all.shape[0]
    offsets = (
        jnp.arange(key_count)[None, :] - hop_count * row_count - jnp.arange(row_count)[:, None]
    )
    allowed = (
        (jnp.abs(offsets) <= WINDOW)
        & (labels_own[0][:, None] == labels_keys[0][None, :])
        & ((labels_keys[2][None, :] == 1) | (offsets == 0))
    )
    same_var = (labels_own[1][:, None] == labels_keys[1][None, :]).astype(jnp.float32)
    scores = jnp.einsum(
        "qhd,khd->hqk", query_rot, keys_all, preferred_element_type=jnp.float32
    ) * HEAD_DIM ** (-0.5)
    scores = scores + var_bias[:, None, None] * same_var[None]
    return (jnp.where(allowed[None], scores, NEGATIVE), same_var)


def fetch_weights(shards):
    row_blocks = (
        lax.all_gather(shards[0], "dp", axis=0, tiled=True),
        lax.all_gather(shards[1], "dp", axis=0, tiled=True),
        lax.all_gather(shards[2], "dp", axis=0, tiled=True),
        lax.all_gather(shards[3], "dp", axis=0, tiled=True),
        lax.all_gather(shards[4], "dp", axis=0, tiled=True),
    )
    return (
        lax.all_gather(row_blocks[0], "seq", axis=1, tiled=True),
        lax.all_gather(row_blocks[1], "seq", axis=1, tiled=True),
        lax.all_gather(row_blocks[2], "seq", axis=1, tiled=True),
        lax.all_gather(row_blocks[3], "seq", axis=1, tiled=True),
        lax.all_gather(row_blocks[4], "seq", axis=1, tiled=True),
    )


def fetch_keep(shards):
    row_blocks = (
        lax.all_gather(shards[0], "dp", axis=0, tiled=True),
        lax.all_gather(shards[1], "dp", axis=0, tiled=True),
        lax.all_gather(shards[2], "dp", axis=0, tiled=True),
        lax.all_gather(shards[3], "dp", axis=0, tiled=True),
        lax.all_gather(shards[4], "dp", axis=0, tiled=True),
    )
    return (
        lax.all_gather(row_blocks[0], "seq", axis=1, tiled=True),
        lax.all_gather(row_blocks[1], "seq", axis=1, tiled=True),
        lax.all_gather(row_blocks[2], "seq", axis=1, tiled=True),
        lax.all_gather(row_blocks[3], "seq", axis=1, tiled=True),
        lax.all_gather(row_blocks[4], "seq", axis=1, tiled=True),
    )


def reduce_last(grads_full):
    col_sums = (
        lax.psum_scatter(grads_full[0], "seq", scatter_dimension=1, tiled=True),
        lax.psum_scatter(grads_full[1], "seq", scatter_dimension=1, tiled=True),
        lax.psum_scatter(grads_full[2], "seq", scatter_dimension=1, tiled=True),
        lax.psum_scatter(grads_full[3], "seq", scatter_dimension=1, tiled=True),
        lax.psum_scatter(grads_full[4], "seq", scatter_dimension=1, tiled=True),
    )
    return (
        lax.psum_scatter(
            col_sums[0].astype(jnp.bfloat16), "dp", scatter_dimension=0, tiled=True
        ).astype(jnp.float32),
        lax.psum_scatter(
            col_sums[1].astype(jnp.bfloat16), "dp", scatter_dimension=0, tiled=True
        ).astype(jnp.float32),
        lax.psum_scatter(
            col_sums[2].astype(jnp.bfloat16), "dp", scatter_dimension=0, tiled=True
        ).astype(jnp.float32),
        lax.psum_scatter(
            col_sums[3].astype(jnp.bfloat16), "dp", scatter_dimension=0, tiled=True
        ).astype(jnp.float32),
        lax.psum_scatter(
            col_sums[4].astype(jnp.bfloat16), "dp", scatter_dimension=0, tiled=True
        ).astype(jnp.float32),
    )


def weight_grads(pieces):
    (
        normed_one,
        grad_qkv,
        attended,
        grad_branch,
        normed_two,
        grad_gate,
        grad_up,
        hidden,
        grad_ffn,
    ) = pieces
    grad_w_qkv = jnp.einsum("td,tf->df", normed_one, grad_qkv, preferred_element_type=jnp.float32)
    grad_w_out = jnp.einsum("ti,to->io", attended, grad_branch, preferred_element_type=jnp.float32)
    grad_w_gate = jnp.einsum("td,tf->df", normed_two, grad_gate, preferred_element_type=jnp.float32)
    grad_w_up = jnp.einsum("td,tf->df", normed_two, grad_up, preferred_element_type=jnp.float32)
    grad_w_down = jnp.einsum("tf,td->fd", hidden, grad_ffn, preferred_element_type=jnp.float32)
    return (grad_w_qkv, grad_w_out, grad_w_gate, grad_w_up, grad_w_down)


def on_device(
    tokens,
    segment_ids,
    variate_ids,
    time_ids,
    pad_mask,
    cotangent,
    w_qkv,
    w_out,
    w_gate,
    w_up,
    w_down,
    gain_attn,
    gain_ffn,
    variate_bias,
):
    micro_count, row_count, model_width = tokens.shape
    hop_count = -(-WINDOW // row_count)
    key_count = (2 * hop_count + 1) * row_count
    shards = (w_qkv, w_out, w_gate, w_up, w_down)
    var_bias = variate_bias.astype(jnp.float32)
    gain_one = gain_attn.astype(jnp.float32)
    gain_two = gain_ffn.astype(jnp.float32)
    bias_total = jnp.zeros(var_bias.shape, jnp.float32)
    gain_one_total = jnp.zeros(gain_one.shape, jnp.float32)
    gain_two_total = jnp.zeros(gain_two.shape, jnp.float32)
    grad_totals = None
    saved = []
    outputs = []
    input_grads = []
    held_weights = fetch_weights(shards)
    for micro_step in range(micro_count):
        if micro_step == 0:
            weights = held_weights
        else:
            weights = fetch_keep(shards)
        resid_in = tokens[micro_step].astype(jnp.float32)
        inv_one = norm_scale(resid_in)
        normed_one = (resid_in * inv_one * gain_one).astype(jnp.bfloat16)
        qkv_proj = jnp.dot(normed_one, weights[0], preferred_element_type=jnp.float32)
        cos_table, sine_table = rope_tables(time_ids[micro_step], HEAD_DIM // 2)
        query_rot = rotate(
            qkv_proj[:, :model_width].reshape(row_count, HEADS, HEAD_DIM), cos_table, sine_table
        ).astype(jnp.bfloat16)
        key_rot = rotate(
            qkv_proj[:, model_width : 2 * model_width].reshape(row_count, HEADS, HEAD_DIM),
            cos_table,
            sine_table,
        ).astype(jnp.bfloat16)
        value_own = qkv_proj[:, 2 * model_width :].astype(jnp.bfloat16)
        kv_own = jnp.stack([key_rot.reshape(row_count, model_width), value_own])
        labels_own = jnp.stack(
            [segment_ids[micro_step], variate_ids[micro_step], pad_mask[micro_step]]
        )
        kv_slots = []
        label_slots = []
        for slot_index in range(2 * hop_count + 1):
            offset = slot_index - hop_count
            if offset == 0:
                kv_slots.append(kv_own)
                label_slots.append(labels_own)
            else:
                kv_slots.append(passed_along(kv_own, "seq", -offset))
                label_slots.append(passed_along(labels_own, "seq", -offset))
        kv_all = jnp.concatenate(kv_slots, axis=1)
        labels_keys = jnp.concatenate(label_slots, axis=1)
        keys_all = kv_all[0].reshape(key_count, HEADS, HEAD_DIM)
        values_all = kv_all[1].reshape(key_count, HEADS, HEAD_DIM)
        scores, same_var = masked_scores(
            query_rot, keys_all, labels_own, labels_keys, var_bias, hop_count
        )
        maxima = jnp.max(scores, axis=-1, keepdims=True)
        exp_shift = jnp.exp(scores - maxima)
        denom_sum = jnp.sum(exp_shift, axis=-1, keepdims=True)
        log_norm = maxima + jnp.log(denom_sum)
        prob_low = (exp_shift / denom_sum).astype(jnp.bfloat16)
        attended = jnp.einsum(
            "hqk,khd->qhd", prob_low, values_all, preferred_element_type=jnp.float32
        )
        attended = attended.reshape(row_count, model_width).astype(jnp.bfloat16)
        resid_mid = resid_in + jnp.dot(attended, weights[1], preferred_element_type=jnp.float32)
        inv_two = norm_scale(resid_mid)
        normed_two = (resid_mid * inv_two * gain_two).astype(jnp.bfloat16)
        gate_proj = jnp.dot(normed_two, weights[2], preferred_element_type=jnp.float32)
        up_proj = jnp.dot(normed_two, weights[3], preferred_element_type=jnp.float32)
        gate_sig = jax.nn.sigmoid(gate_proj)
        hidden = (gate_proj * gate_sig * up_proj).astype(jnp.bfloat16)
        ffn_out = jnp.dot(hidden, weights[4], preferred_element_type=jnp.float32)
        outputs.append((resid_mid + ffn_out).astype(jnp.bfloat16))
        grad_out = cotangent[micro_step].astype(jnp.float32)
        grad_ffn = grad_out.astype(jnp.bfloat16)
        grad_hidden = jnp.einsum(
            "td,fd->tf", grad_ffn, weights[4], preferred_element_type=jnp.float32
        )
        grad_gate = (
            grad_hidden * up_proj * gate_sig * (1.0 + gate_proj * (1.0 - gate_sig))
        ).astype(jnp.bfloat16)
        grad_up = (grad_hidden * gate_proj * gate_sig).astype(jnp.bfloat16)
        grad_normed_two = jnp.einsum(
            "tf,df->td", grad_gate, weights[2], preferred_element_type=jnp.float32
        )
        grad_normed_two = grad_normed_two + jnp.einsum(
            "tf,df->td", grad_up, weights[3], preferred_element_type=jnp.float32
        )
        gain_two_total = gain_two_total + jnp.sum(grad_normed_two * resid_mid * inv_two, axis=0)
        grad_mid = grad_out + norm_back(grad_normed_two * gain_two, resid_mid, inv_two)
        grad_branch = grad_mid.astype(jnp.bfloat16)
        grad_attended = jnp.einsum(
            "to,io->ti", grad_branch, weights[1], preferred_element_type=jnp.float32
        )
        grad_attended = grad_attended.astype(jnp.bfloat16).reshape(row_count, HEADS, HEAD_DIM)
        scores, same_var = masked_scores(
            query_rot, keys_all, labels_own, labels_keys, var_bias, hop_count
        )
        prob_full = jnp.exp(scores - log_norm)
        prob_low = prob_full.astype(jnp.bfloat16)
        grad_values = jnp.einsum(
            "hqk,qhd->khd", prob_low, grad_attended, preferred_element_type=jnp.float32
        )
        grad_prob = jnp.einsum(
            "qhd,khd->hqk", grad_attended, values_all, preferred_element_type=jnp.float32
        )
        grad_scores = prob_full * (
            grad_prob - jnp.sum(prob_full * grad_prob, axis=-1, keepdims=True)
        )
        grad_scores = grad_scores.astype(jnp.bfloat16)
        bias_total = bias_total + jnp.sum(
            grad_scores.astype(jnp.float32) * same_var[None], axis=(1, 2)
        )
        grad_query = jnp.einsum(
            "hqk,khd->qhd", grad_scores, keys_all, preferred_element_type=jnp.float32
        ) * HEAD_DIM ** (-0.5)
        grad_keys = jnp.einsum(
            "hqk,qhd->khd", grad_scores, query_rot, preferred_element_type=jnp.float32
        ) * HEAD_DIM ** (-0.5)
        grad_kv = jnp.stack(
            [grad_keys.reshape(key_count, model_width), grad_values.reshape(key_count, model_width)]
        )
        grad_kv_own = grad_kv[:, hop_count * row_count : (hop_count + 1) * row_count]
        for slot_index in range(2 * hop_count + 1):
            offset = slot_index - hop_count
            if offset != 0:
                slot_grad = grad_kv[:, slot_index * row_count : (slot_index + 1) * row_count]
                grad_kv_own = grad_kv_own + passed_along(
                    slot_grad.astype(jnp.bfloat16), "seq", offset
                ).astype(slot_grad.dtype)
        grad_q_plain = rotate_back(grad_query, cos_table, sine_table).reshape(
            row_count, model_width
        )
        grad_k_plain = rotate_back(
            grad_kv_own[0].reshape(row_count, HEADS, HEAD_DIM), cos_table, sine_table
        ).reshape(row_count, model_width)
        grad_qkv = jnp.concatenate([grad_q_plain, grad_k_plain, grad_kv_own[1]], axis=1).astype(
            jnp.bfloat16
        )
        grad_normed_one = jnp.einsum(
            "tf,df->td", grad_qkv, weights[0], preferred_element_type=jnp.float32
        )
        gain_one_total = gain_one_total + jnp.sum(grad_normed_one * resid_in * inv_one, axis=0)
        grad_input = grad_mid + norm_back(grad_normed_one * gain_one, resid_in, inv_one)
        input_grads.append(grad_input.astype(jnp.bfloat16))
        pieces = (
            normed_one,
            grad_qkv,
            attended,
            grad_branch,
            normed_two,
            grad_gate,
            grad_up,
            hidden,
            grad_ffn,
        )
        saved.append(pieces)
    joined = tuple(
        (
            jnp.concatenate([entry[index] for entry in saved], axis=0)
            for index in range(len(saved[0]))
        )
    )
    grad_totals = reduce_last(weight_grads(joined))
    bias_sum, gain_one_sum, gain_two_sum = lax.psum(
        (bias_total, gain_one_total, gain_two_total), ("dp", "seq")
    )
    return (
        jnp.stack(outputs),
        jnp.stack(input_grads),
        grad_totals[0],
        grad_totals[1],
        grad_totals[2],
        grad_totals[3],
        grad_totals[4],
        gain_one_sum,
        gain_two_sum,
        bias_sum,
    )


def solution(mesh):
    in_specs = (
        P("dp", "seq", None),
        P("dp", "seq"),
        P("dp", "seq"),
        P("dp", "seq"),
        P("dp", "seq"),
        P("dp", "seq", None),
        P("dp", "seq"),
        P("dp", "seq"),
        P("dp", "seq"),
        P("dp", "seq"),
        P("dp", "seq"),
        P(),
        P(),
        P(),
    )
    out_specs = (
        P("dp", "seq", None),
        P("dp", "seq", None),
        P("dp", "seq"),
        P("dp", "seq"),
        P("dp", "seq"),
        P("dp", "seq"),
        P("dp", "seq"),
        P(),
        P(),
        P(),
    )
    return jax.shard_map(
        on_device, mesh=mesh, in_specs=in_specs, out_specs=out_specs, check_vma=False
    )
```

profile of v0, /device:TPU:0, one launch (start us, length us, event | category | flops | bytes accessed | tf_op | source)
XLA Modules:
  0.0 2215.0 jit_solution(10381712855684015665)
XLA Ops:
  9.5 11.7 all_gather.40
  30.6 18.2 all-gather.17.cloned.1.call-done
  111.2 57.5 %all-gather.9.cloned.1.call-done = bf16[1024,3072]{1,0:T(8,128)(2,1)} async-done(((bf16[1024,384]{1,0:T(8,128)(2,1)}), bf16[1024,3072]{1,0:T(8,128)(2,1)}) %all-gather.9.cloned.1.call-update) | async-done | bytes 6291472 | tf_op jit(solution)/shard_map/all_gather | solution.py:91
  218.7 15.6 collective-permute-done.2
  236.7 67.6 %collective-permute-start.16 = (bf16[2,128,1024]{2,1,0:T(8,128)(2,1)}, bf16[2,128,1024]{2,1,0:T(8,128)(2,1)S(1)}, u32[]{:S(2)}, u32[]{:S(2)}) collective-permute-start(bf16[2,128,1024]{2,1,0:T(8,128)(2,1)} %pad_maximum_fusion.3), channel_id=1, source_target_pairs={{0,4},{1,5},{2,6},{3,7},{8,12},{9,13},{10,14},{11,15},{16,20},{17,... | collective-permute-start | bytes 1572872 | tf_op jit(solution)/shard_map/ppermute | solution.py:18
  329.8 14.7 collective-permute-done.17
  346.6 17.1 collective-permute-done.18
  378.4 18.0 collective-permute-done.22
  398.2 52.5 %collective-permute-done.23 = bf16[2,128,1024]{2,1,0:T(8,128)(2,1)} collective-permute-done((bf16[2,128,1024]{2,1,0:T(8,128)(2,1)}, bf16[2,128,1024]{2,1,0:T(8,128)(2,1)}, u32[]{:S(2)}, u32[]{:S(2)}) %collective-permute-start.23) | collective-permute-done | bytes 524320 | tf_op jit(solution)/shard_map/ppermute | solution.py:18
  498.1 90.5 %all-gather.19.cloned.1.call-done = bf16[1024,4096]{1,0:T(8,128)(2,1)} async-done(((bf16[1024,512]{1,0:T(8,128)(2,1)}), bf16[1024,4096]{1,0:T(8,128)(2,1)}) %all-gather.19.cloned.1.call-update) | async-done | bytes 8388624 | tf_op jit(solution)/shard_map/all_gather | solution.py:94
  594.6 119.2 %all-gather.23.cloned.1.call-done = bf16[4096,1024]{1,0:T(8,128)(2,1)} async-done(((bf16[4096,128]{1,0:T(8,128)(2,1)}), bf16[4096,1024]{1,0:T(8,128)(2,1)}) %all-gather.23.cloned.1.call-update) | async-done | bytes 8388624 | tf_op jit(solution)/shard_map/all_gather | solution.py:95
  760.9 10.3 multiply_reduce_fusion.3
  826.7 27.9 %collective-permute-done.32 = bf16[2,128,1024]{1,2,0:T(8,128)(2,1)S(1)} collective-permute-done((bf16[2,128,1024]{1,2,0:T(8,128)(2,1)S(1)}, bf16[2,128,1024]{1,2,0:T(8,128)(2,1)S(1)}, u32[]{:S(2)}, u32[]{:S(2)}) %collective-permute-start.32) | collective-permute-done | bytes 524320 | tf_op jit(solution)/shard_map/ppermute | solution.py:18
  863.2 15.5 collective-permute-start.39
  893.4 49.4 %collective-permute-done.40 = bf16[2,128,1024]{1,2,0:T(8,128)(2,1)S(1)} collective-permute-done((bf16[2,128,1024]{1,2,0:T(8,128)(2,1)S(1)}, bf16[2,128,1024]{1,2,0:T(8,128)(2,1)S(1)}, u32[]{:S(2)}, u32[]{:S(2)}) %collective-permute-start.40) | collective-permute-done | bytes 524320 | tf_op jit(solution)/shard_map/ppermute | solution.py:18
  945.5 21.3 collective-permute-start.47
  1019.0 208.8 %reduce-scatter.11.cloned.1.call-done = f32[1024,384]{1,0:T(8,128)} async-done(((f32[1024,3072]{1,0:T(8,128)}), f32[1024,384]{1,0:T(8,128)}) %reduce-scatter.11.cloned.1.call-update) | async-done | bytes 1572880 | tf_op jit(solution)/shard_map/reduce_scatter | solution.py:118
  1230.2 280.7 %reduce-scatter.27.cloned.1.call-done = f32[4096,128]{1,0:T(8,128)} async-done(((f32[4096,1024]{1,0:T(8,128)}), f32[4096,128]{1,0:T(8,128)}) %reduce-scatter.27.cloned.1.call-update) | async-done | bytes 2097168 | tf_op jit(solution)/shard_map/reduce_scatter | solution.py:122
  1513.6 280.3 %reduce-scatter.23.cloned.1.call-done = f32[1024,512]{1,0:T(8,128)} async-done(((f32[1024,4096]{1,0:T(8,128)}), f32[1024,512]{1,0:T(8,128)}) %reduce-scatter.23.cloned.1.call-update) | async-done | bytes 2097168 | tf_op jit(solution)/shard_map/reduce_scatter | solution.py:121
  1801.5 275.6 %reduce-scatter.19.cloned.1.call-done = f32[1024,512]{1,0:T(8,128)} async-done(((f32[1024,4096]{1,0:T(8,128)}), f32[1024,512]{1,0:T(8,128)}) %reduce-scatter.19.cloned.1.call-update) | async-done | bytes 2097168 | tf_op jit(solution)/shard_map/reduce_scatter | solution.py:120
  2094.2 39.5 %all-reduce = (f32[1024]{0:T(1024)}, f32[1024]{0:T(1024)}, f32[16]{0:T(128)}) all-reduce(f32[1024]{0:T(1024)S(1)} %add.257, f32[1024]{0:T(1024)S(1)} %add.258, f32[16]{0:T(128)S(1)} %add.259), channel_id=1, replica_groups=mesh['dp'=4,'seq'=8] {'dp','seq'}, use_global_device_ids=true, to_apply=%region_26.27 | all-reduce | flops 2064 | bytes 16512 | tf_op jit(solution)/shard_map/psum | solution.py:343
  2139.6 12.0 reduce-scatter.29.cloned.1.call-done
  2153.3 25.4 %reduce-scatter.25.cloned.1.call-done = bf16[256,512]{1,0:T(8,128)(2,1)} async-done(((bf16[1024,512]{1,0:T(8,128)(2,1)}), bf16[256,512]{1,0:T(8,128)(2,1)}) %reduce-scatter.25.cloned.1.call-update) | async-done | bytes 262160 | tf_op jit(solution)/shard_map/reduce_scatter | solution.py:134
  2180.5 25.4 %reduce-scatter.21.cloned.1.call-done = bf16[256,512]{1,0:T(8,128)(2,1)} async-done(((bf16[1024,512]{1,0:T(8,128)(2,1)}), bf16[256,512]{1,0:T(8,128)(2,1)}) %reduce-scatter.21.cloned.1.call-update) | async-done | bytes 262160 | tf_op jit(solution)/shard_map/reduce_scatter | solution.py:131
  (510 shorter events, 443.4 us)
Async XLA Ops:
  8.7 101.2 %all-gather.21.cloned.1.call-start = ((), (), s32[]{:S(2)}) async-start(), calls=%async_computation.16 | async-start | bytes 1310720 | tf_op jit(solution)/shard_map/all_gather | solution.py:88
  9.5 159.2 %all-gather.9.cloned.1.call-start = ((), (), s32[]{:S(2)}) async-start(), calls=%async_computation.10 | async-start | bytes 7077888 | tf_op jit(solution)/shard_map/all_gather | solution.py:91
  21.2 456.5 %all-gather.11.cloned.1.call-start = ((), (), s32[]{:S(2)}) async-start(), calls=%async_computation.11 | async-start | bytes 2359296 | tf_op jit(solution)/shard_map/all_gather | solution.py:92
  29.7 462.4 %all-gather.15.cloned.1.call-start = ((), (), s32[]{:S(2)}) async-start(), calls=%async_computation.13 | async-start | bytes 9437184 | tf_op jit(solution)/shard_map/all_gather | solution.py:93
  30.5 558.1 %all-gather.19.cloned.1.call-start = ((), (), s32[]{:S(2)}) async-start(), calls=%async_computation.15 | async-start | bytes 9437184 | tf_op jit(solution)/shard_map/all_gather | solution.py:94
  48.8 665.0 %all-gather.23.cloned.1.call-start = ((), (), s32[]{:S(2)}) async-start(), calls=%async_computation.17 | async-start | bytes 9437184 | tf_op jit(solution)/shard_map/all_gather | solution.py:95
  110.0 907.2 %reduce-scatter.15.cloned.1.call-start = ((), (), s32[]{:S(2)}) async-start(), calls=%async_computation.20 | async-start | bytes 4718592 | tf_op jit(solution)/shard_map/reduce_scatter | solution.py:119
  193.4 112.9 %collective-permute-start.4 = (bf16[2,128,1024]{2,1,0:T(8,128)(2,1)}, bf16[2,128,1024]{2,1,0:T(8,128)(2,1)}, u32[]{:S(2)}, u32[]{:S(2)}) collective-permute-start(bf16[2,128,1024]{2,1,0:T(8,128)(2,1)} %pad_maximum_fusion.2), channel_id=1, source_target_pairs={{1,0},{2,1},{3,2},{4,3},{5,4},{6,5},{7,6},{9,8},{10,9},{11,10},{12... | collective-permute-start | bytes 1572872 | tf_op jit(solution)/shard_map/ppermute | solution.py:18
  205.8 102.9 %collective-permute-start.5 = (bf16[2,128,1024]{2,1,0:T(8,128)(2,1)}, bf16[2,128,1024]{2,1,0:T(8,128)(2,1)S(1)}, u32[]{:S(2)}, u32[]{:S(2)}) collective-permute-start(bf16[2,128,1024]{2,1,0:T(8,128)(2,1)} %pad_maximum_fusion.2), channel_id=1, source_target_pairs={{2,0},{3,1},{4,2},{5,3},{6,4},{7,5},{10,8},{11,9},{12,10},{13,11},... | collective-permute-start | bytes 1572872 | tf_op jit(solution)/shard_map/ppermute | solution.py:18
  216.3 93.8 %collective-permute-start.6 = (bf16[2,128,1024]{2,1,0:T(8,128)(2,1)}, bf16[2,128,1024]{2,1,0:T(8,128)(2,1)S(1)}, u32[]{:S(2)}, u32[]{:S(2)}) collective-permute-start(bf16[2,128,1024]{2,1,0:T(8,128)(2,1)} %pad_maximum_fusion.2), channel_id=1, source_target_pairs={{3,0},{4,1},{5,2},{6,3},{7,4},{11,8},{12,9},{13,10},{14,11},{15,12... | collective-permute-start | bytes 1572872 | tf_op jit(solution)/shard_map/ppermute | solution.py:18
  234.3 87.4 %collective-permute-start.7 = (bf16[2,128,1024]{2,1,0:T(8,128)(2,1)}, bf16[2,128,1024]{2,1,0:T(8,128)(2,1)S(1)}, u32[]{:S(2)}, u32[]{:S(2)}) collective-permute-start(bf16[2,128,1024]{2,1,0:T(8,128)(2,1)} %pad_maximum_fusion.2), channel_id=1, source_target_pairs={{4,0},{5,1},{6,2},{7,3},{12,8},{13,9},{14,10},{15,11},{20,16},{21,... | collective-permute-start | bytes 1572872 | tf_op jit(solution)/shard_map/ppermute | solution.py:18
  236.7 91.0 %collective-permute-start.16 = (bf16[2,128,1024]{2,1,0:T(8,128)(2,1)}, bf16[2,128,1024]{2,1,0:T(8,128)(2,1)S(1)}, u32[]{:S(2)}, u32[]{:S(2)}) collective-permute-start(bf16[2,128,1024]{2,1,0:T(8,128)(2,1)} %pad_maximum_fusion.3), channel_id=1, source_target_pairs={{0,4},{1,5},{2,6},{3,7},{8,12},{9,13},{10,14},{11,15},{16,20},{17,... | collective-permute-start | bytes 1572872 | tf_op jit(solution)/shard_map/ppermute | solution.py:18
  363.7 87.0 %collective-permute-start.23 = (bf16[2,128,1024]{2,1,0:T(8,128)(2,1)}, bf16[2,128,1024]{2,1,0:T(8,128)(2,1)}, u32[]{:S(2)}, u32[]{:S(2)}) collective-permute-start(bf16[2,128,1024]{2,1,0:T(8,128)(2,1)} %pad_maximum_fusion.3), channel_id=1, source_target_pairs={{4,0},{5,1},{6,2},{7,3},{12,8},{13,9},{14,10},{15,11},{20,16},{21,... | collective-permute-start | bytes 1572872 | tf_op jit(solution)/shard_map/ppermute | solution.py:18
  778.6 449.2 %reduce-scatter.11.cloned.1.call-start = ((), (), s32[]{:S(2)}) async-start(), calls=%async_computation.18 | async-start | bytes 14155776 | tf_op jit(solution)/shard_map/reduce_scatter | solution.py:118
  887.2 86.0 %collective-permute-start.43 = (bf16[2,128,1024]{1,2,0:T(8,128)(2,1)S(1)}, bf16[2,128,1024]{1,2,0:T(8,128)(2,1)S(1)}, u32[]{:S(2)}, u32[]{:S(2)}) collective-permute-start(bf16[2,128,1024]{1,2,0:T(8,128)(2,1)S(1)} %get-tuple-element.50), channel_id=1, source_target_pairs={{1,0},{2,1},{3,2},{4,3},{5,4},{6,5},{7,6},{9,8},{10,9},{11,10},{12... | collective-permute-start | bytes 1572872 | tf_op jit(solution)/shard_map/ppermute | solution.py:18
  891.9 81.4 %collective-permute-start.44 = (bf16[2,128,1024]{1,2,0:T(8,128)(2,1)S(1)}, bf16[2,128,1024]{1,2,0:T(8,128)(2,1)S(1)}, u32[]{:S(2)}, u32[]{:S(2)}) collective-permute-start(bf16[2,128,1024]{1,2,0:T(8,128)(2,1)S(1)} %get-tuple-element.49), channel_id=1, source_target_pairs={{0,1},{1,2},{2,3},{3,4},{4,5},{5,6},{6,7},{8,9},{9,10},{10,11},{11... | collective-permute-start | bytes 1572872 | tf_op jit(solution)/shard_map/ppermute | solution.py:18
  985.8 525.1 %reduce-scatter.27.cloned.1.call-start = ((), (), s32[]{:S(2)}) async-start(), calls=%async_computation.26 | async-start | bytes 18874368 | tf_op jit(solution)/shard_map/reduce_scatter | solution.py:122
  995.7 798.2 %reduce-scatter.23.cloned.1.call-start = ((), (), s32[]{:S(2)}) async-start(), calls=%async_computation.24 | async-start | bytes 18874368 | tf_op jit(solution)/shard_map/reduce_scatter | solution.py:121
  1006.4 1070.7 %reduce-scatter.19.cloned.1.call-start = ((), (), s32[]{:S(2)}) async-start(), calls=%async_computation.22 | async-start | bytes 18874368 | tf_op jit(solution)/shard_map/reduce_scatter | solution.py:120
  1017.1 1119.3 %reduce-scatter.17.cloned.1.call-start = ((), (), s32[]{:S(2)}) async-start(), calls=%async_computation.21 | async-start | bytes 327680 | tf_op jit(solution)/shard_map/reduce_scatter | solution.py:128
  1019.0 1118.9 %reduce-scatter.13.cloned.1.call-start = ((), (), s32[]{:S(2)}) async-start(), calls=%async_computation.19 | async-start | bytes 983040 | tf_op jit(solution)/shard_map/reduce_scatter | solution.py:125
  1230.2 921.4 %reduce-scatter.29.cloned.1.call-start = ((), (), s32[]{:S(2)}) async-start(), calls=%async_computation.27 | async-start | bytes 1310720 | tf_op jit(solution)/shard_map/reduce_scatter | solution.py:137
  1513.6 665.1 %reduce-scatter.25.cloned.1.call-start = ((), (), s32[]{:S(2)}) async-start(), calls=%async_computation.25 | async-start | bytes 1310720 | tf_op jit(solution)/shard_map/reduce_scatter | solution.py:134
  1796.7 409.2 %reduce-scatter.21.cloned.1.call-start = ((), (), s32[]{:S(2)}) async-start(), calls=%async_computation.23 | async-start | bytes 1310720 | tf_op jit(solution)/shard_map/reduce_scatter | solution.py:131
  (147 other events, 5867.6 us)
Sparse Core Ops, SparseCore 0:
  9.6 20.8 all-gather.12
  32.0 16.6 all-gather.16
  50.3 16.6 all-gather.20
  69.0 99.6 all-gather.8
  170.6 80.9 all-gather.10
  253.5 208.6 all-gather.14
  464.3 124.3 all-gather.18
  590.7 123.1 all-gather.22
  778.7 147.9 reduce-scatter.14
  985.9 241.8 reduce-scatter.10
  1231.6 279.2 reduce-scatter.26
  1514.5 279.3 reduce-scatter.22
  1797.7 279.3 reduce-scatter.18
  2079.4 19.1 reduce-scatter.16
  2101.0 23.3 reduce-scatter.12
  2126.7 24.7 reduce-scatter.28
  2153.9 24.7 reduce-scatter.24
  2181.1 24.7 reduce-scatter.20
where the time goes:
time: 2230 us; the launch traced here: 2220 us
  waiting for transfers between devices  1630 us (73%)
  starting transfers between devices  201 us (9%)
  matrix products  168 us (8%)
  local copies, waits for them, and re-layouts  70.1 us (3%)
  other arithmetic  65.9 us (3%)
  blocking collectives  59.5 us (3%)
    reduce_scatter x1, waiting for transfers between devices, reduce_last(): lax.psum_scatter(grads_full[4], 'seq', scatter_dimension=1, tiled=True)  281 us
    reduce_scatter x1, waiting for transfers between devices, reduce_last(): lax.psum_scatter(grads_full[3], 'seq', scatter_dimension=1, tiled=True)  280 us
    reduce_scatter x1, waiting for transfers between devices, reduce_last(): lax.psum_scatter(grads_full[2], 'seq', scatter_dimension=1, tiled=True)  276 us
    ppermute x48, waiting for transfers between devices, passed_along(): return lax.ppermute(block, axis, route)  236 us
    reduce_scatter x1, waiting for transfers between devices, reduce_last(): lax.psum_scatter(grads_full[0], 'seq', scatter_dimension=1, tiled=True)  209 us
    ppermute x48, starting transfers between devices, passed_along(): return lax.ppermute(block, axis, route)  200 us
    all_gather x1, waiting for transfers between devices, fetch_weights(): lax.all_gather(row_blocks[4], 'seq', axis=1, tiled=True)  119 us
    all_gather x1, waiting for transfers between devices, fetch_weights(): lax.all_gather(row_blocks[3], 'seq', axis=1, tiled=True)  90.5 us
  transfers between devices with their start and end apart: 66, of which 32 were waited for; matrix products, arithmetic and copies ran while one was open for 10% of the time, Pallas kernels for 0%

commit v1 on v0

--- a/solution.py
+++ b/solution.py
@@ -1,7 +1,12 @@
+import functools
+
 import jax
 import jax.numpy as jnp
 from jax import lax
+from jax.experimental import pallas as pl
+from jax.experimental.pallas import tpu as pltpu
 from jax.sharding import PartitionSpec as P
+
 
 HEADS = 16
 HEAD_DIM = 64
@@ -357,6 +362,801 @@
     )
 
 
+MESH = pl.DeviceIdType.MESH
+VM = pl.BlockSpec(memory_space=pltpu.VMEM)
+DMA = pltpu.SemaphoreType.DMA
+
+
+def at(dp, seq):
+    return {"dp": dp, "seq": seq}
+
+
+def ring(i):
+    return i + 1 - 2 * lax.rem(i, 2), lax.rem(i + 2, 4)
+
+
+def meet(peers):
+    barrier = pltpu.get_barrier_semaphore()
+    for peer in peers:
+        pl.semaphore_signal(barrier, inc=1, device_id=peer, device_id_type=MESH)
+    pl.semaphore_wait(barrier, len(peers))
+
+
+def send(src, dst, send_sem, recv_sem, peer):
+    return pltpu.make_async_remote_copy(
+        src_ref=src,
+        dst_ref=dst,
+        send_sem=send_sem,
+        recv_sem=recv_sem,
+        device_id=peer,
+        device_id_type=MESH,
+    )
+
+
+def comm_call(kernel, outs, scratch, collective_id, in_count, vmem=None):
+    return pl.pallas_call(
+        kernel,
+        out_shape=outs,
+        in_specs=[VM] * in_count,
+        out_specs=[VM] * len(outs),
+        scratch_shapes=scratch,
+        compiler_params=pltpu.CompilerParams(
+            collective_id=collective_id, has_side_effects=True, vmem_limit_bytes=vmem
+        ),
+    )
+
+
+def bf16(*shape):
+    return jax.ShapeDtypeStruct(shape, jnp.bfloat16)
+
+
+def f32(*shape):
+    return jax.ShapeDtypeStruct(shape, jnp.float32)
+
+
+def weight_pieces(kind, refs, dst, me, other, seq):
+    if kind == "attention":
+        w_qkv, w_out = refs
+        place = lax.rem(other + 2 * lax.rem(seq, 2), 4)
+        return [
+            (w_qkv.at[place], dst.at[pl.ds(256 * me, 256)]),
+            (w_out.at[pl.ds(64 * other, 64)], dst.at[pl.ds(1024 + 64 * me, 64)]),
+        ]
+    w_gate, w_up, w_down = refs
+    columns = pl.ds(pl.multiple_of(128 * other, 128), 128)
+    pairs = [
+        (w_gate.at[:, columns], dst.at[pl.ds(256 * me, 256)]),
+        (w_up.at[:, columns], dst.at[pl.ds(1024 + 256 * me, 256)]),
+    ]
+    for half in (0, 1):
+        pairs.append(
+            (
+                w_down.at[pl.ds(512 * half + 128 * other, 128)],
+                dst.at[pl.ds(2048 + 256 * me + 128 * half, 128)],
+            )
+        )
+    return pairs
+
+
+def grad_pieces(kind, src, dst, me, other, seq):
+    if kind == "attention":
+        g_qkv, g_out = dst
+        place = lax.rem(me + 2 * lax.rem(seq, 2), 4)
+        return [
+            (src.at[pl.ds(256 * other, 256)], g_qkv.at[place]),
+            (src.at[pl.ds(1024 + 64 * other, 64)], g_out.at[pl.ds(64 * me, 64)]),
+        ]
+    g_gate, g_up, g_down = dst
+    columns = pl.ds(pl.multiple_of(128 * me, 128), 128)
+    pairs = [
+        (src.at[pl.ds(256 * other, 256)], g_gate.at[:, columns]),
+        (src.at[pl.ds(1024 + 256 * other, 256)], g_up.at[:, columns]),
+    ]
+    for half in (0, 1):
+        pairs.append(
+            (
+                src.at[pl.ds(2048 + 256 * other + 128 * half, 128)],
+                g_down.at[pl.ds(512 * half + 128 * me, 128)],
+            )
+        )
+    return pairs
+
+
+def exchange_kernel(pieces, n_in, n_out, *refs):
+    ins, outs = refs[:n_in], refs[n_in : n_in + n_out]
+    send_sem, recv_sem, own_sem = refs[n_in + n_out :]
+    me, seq = lax.axis_index("dp"), lax.axis_index("seq")
+    others = [lax.rem(me + step, 4) for step in (1, 2, 3)]
+    meet([at(other, seq) for other in others])
+    copies = []
+    for step, other in enumerate(others):
+        for index, (src, dst) in enumerate(pieces(ins, outs, me, other, seq)):
+            copy = send(
+                src, dst, send_sem.at[step, index], recv_sem.at[step, index], at(other, seq)
+            )
+            copy.start()
+            copies.append(copy)
+    own = [
+        pltpu.make_async_copy(src, dst, own_sem.at[index])
+        for index, (src, dst) in enumerate(pieces(ins, outs, me, me, seq))
+    ]
+    for copy in own:
+        copy.start()
+    for copy in own:
+        copy.wait()
+    for copy in copies:
+        copy.wait()
+
+
+def exchange(pieces, ins, outs, count, collective_id):
+    kernel = functools.partial(exchange_kernel, pieces, len(ins), len(outs))
+    return comm_call(
+        kernel, outs, [DMA((3, count)), DMA((3, count)), DMA((count,))], collective_id, len(ins)
+    )(*ins)
+
+
+def home_meet(peers):
+    i, j = lax.axis_index("dp"), lax.axis_index("seq")
+    target, stays = j // 2, j // 2 == i
+    barrier = pltpu.get_barrier_semaphore()
+    for peer in peers:
+        pl.semaphore_signal(barrier, inc=1, device_id=peer, device_id_type=MESH)
+    for s in (0, 1):
+
+        @pl.when(jnp.logical_not(stays & (2 * i + s == j)))
+        def _():
+            pl.semaphore_signal(
+                barrier, inc=1, device_id=at(target, 2 * i + s), device_id_type=MESH
+            )
+
+    pl.semaphore_wait(barrier, len(peers) + jnp.where(stays, 1, 2))
+
+
+def home_start(ins, outs, send_sem, recv_sem):
+    i, j = lax.axis_index("dp"), lax.axis_index("seq")
+    target, stays = j // 2, j // 2 == i
+    slot = lax.rem(j, 2)
+    for a in range(len(ins)):
+        for s in (0, 1):
+            here = stays & (2 * i + s == j)
+
+            @pl.when(jnp.logical_not(here))
+            def _():
+                send(
+                    ins[a].at[s],
+                    outs[a].at[slot],
+                    send_sem.at[a, s],
+                    recv_sem.at[a, slot],
+                    at(target, 2 * i + s),
+                ).start()
+
+            @pl.when(here)
+            def _():
+                pltpu.make_async_copy(ins[a].at[s], outs[a].at[slot], recv_sem.at[a, slot]).start()
+
+
+def home_finish(ins, outs, send_sem, recv_sem):
+    i, j = lax.axis_index("dp"), lax.axis_index("seq")
+    stays = j // 2 == i
+    for a in range(len(ins)):
+        for s in (0, 1):
+            pltpu.make_async_copy(ins[a].at[s], outs[a].at[s], recv_sem.at[a, s]).wait()
+
+            @pl.when(jnp.logical_not(stays & (2 * i + s == j)))
+            def _():
+                pltpu.make_async_copy(ins[a].at[s], outs[a].at[s], send_sem.at[a, s]).wait()
+
+
+def home_kernel(count, *refs):
+    ins, outs = refs[:count], refs[count : 2 * count]
+    send_sem, recv_sem = refs[2 * count :]
+    home_meet([])
+    home_start(ins, outs, send_sem, recv_sem)
+    home_finish(ins, outs, send_sem, recv_sem)
+
+
+def front_kernel(*refs):
+    (tok, cot, ids, packed, w_out, w_gate, w_up, w_down), refs = refs[:8], refs[8:]
+    (tok_o, cot_o, ids_o, attn_o, ffn_o), refs = refs[:5], refs[5:]
+    h_send, h_recv, a_send, a_recv, a_own, f_send, f_recv, f_own = refs
+    i, j = lax.axis_index("dp"), lax.axis_index("seq")
+    others = [lax.rem(i + step, 4) for step in (1, 2, 3)]
+    home_meet([at(other, j) for other in others])
+    home_start((tok, cot, ids), (tok_o, cot_o, ids_o), h_send, h_recv)
+    copies = []
+    for kind, ins, out, sems in (
+        ("attention", (packed, w_out), attn_o, (a_send, a_recv, a_own)),
+        ("ffn", (w_gate, w_up, w_down), ffn_o, (f_send, f_recv, f_own)),
+    ):
+        for step, other in enumerate(others):
+            for index, (src, dst) in enumerate(weight_pieces(kind, ins, out, i, other, j)):
+                copy = send(
+                    src, dst, sems[0].at[step, index], sems[1].at[step, index], at(other, j)
+                )
+                copy.start()
+                copies.append(copy)
+        for index, (src, dst) in enumerate(weight_pieces(kind, ins, out, i, i, j)):
+            copy = pltpu.make_async_copy(src, dst, sems[2].at[index])
+            copy.start()
+            copies.append(copy)
+    for copy in copies:
+        copy.wait()
+    home_finish((tok, cot, ids), (tok_o, cot_o, ids_o), h_send, h_recv)
+
+
+def front(arrays, collective_id):
+    return comm_call(
+        front_kernel,
+        [jax.ShapeDtypeStruct(v.shape, v.dtype) for v in arrays[:3]]
+        + [bf16(1280, 128), bf16(3072, 128)],
+        [DMA((3, 2)), DMA((3, 2)), DMA((3, 2)), DMA((3, 2)), DMA((2,)), DMA((3, 4)), DMA((3, 4)), DMA((4,))],
+        collective_id,
+        8,
+    )(*arrays)
+
+
+def send_home(arrays, collective_id):
+    count = len(arrays)
+    return comm_call(
+        functools.partial(home_kernel, count),
+        [jax.ShapeDtypeStruct(v.shape, v.dtype) for v in arrays],
+        [DMA((count, 2)), DMA((count, 2))],
+        collective_id,
+        count,
+    )(*arrays)
+
+
+def gather_kernel(count, *refs):
+    ins, outs = refs[:count], refs[count : 2 * count]
+    own_sem, s_core, r_core, s_x, r_x, s_on, r_on = refs[2 * count :]
+    i, j = lax.axis_index("dp"), lax.axis_index("seq")
+    core, across = ring(i)
+    diagonal = lax.rem(core + 2, 4)
+    meet([at(core, j), at(across, j)])
+    pending = []
+    for a in range(count):
+        for s in (0, 1):
+            for sems, peer in (((s_x, r_x), across), ((s_core, r_core), core)):
+                copy = send(
+                    ins[a].at[s],
+                    outs[a].at[2 * i + s],
+                    sems[0].at[a, s],
+                    sems[1].at[a, s],
+                    at(peer, j),
+                )
+                copy.start()
+                pending.append(copy)
+            copy = pltpu.make_async_copy(ins[a].at[s], outs[a].at[2 * i + s], own_sem.at[a, s])
+            copy.start()
+            pending.append(copy)
+    onward = []
+    for a in range(count):
+        for s in (0, 1):
+            block = outs[a].at[2 * across + s]
+            pltpu.make_async_copy(ins[a].at[s], block, r_x.at[a, s]).wait()
+            copy = send(block, block, s_on.at[a, s], r_on.at[a, s], at(core, j))
+            copy.start()
+            onward.append(copy)
+    for a in range(count):
+        for s in (0, 1):
+            pltpu.make_async_copy(ins[a].at[s], outs[a].at[2 * core + s], r_core.at[a, s]).wait()
+            pltpu.make_async_copy(ins[a].at[s], outs[a].at[2 * diagonal + s], r_on.at[a, s]).wait()
+    for index, copy in enumerate(pending):
+        if index % 3 == 2:
+            copy.wait()
+        else:
+            copy.wait_send()
+    for copy in onward:
+        copy.wait_send()
+
+
+def gather_group(arrays, collective_id):
+    count = len(arrays)
+    return comm_call(
+        functools.partial(gather_kernel, count),
+        [jax.ShapeDtypeStruct((8,) + v.shape[1:], v.dtype) for v in arrays],
+        [DMA((count, 2))] * 7,
+        collective_id,
+        count,
+    )(*arrays)
+
+
+def reduce_kernel(count, *refs):
+    ins, outs = refs[:count], refs[count : 2 * count]
+    from_core, to_x, from_x, s_core, r_core, s_x, r_x = refs[2 * count :]
+    i, j = lax.axis_index("dp"), lax.axis_index("seq")
+    core, across = ring(i)
+    diagonal = lax.rem(core + 2, 4)
+    meet([at(core, j), at(across, j)])
+    pending = []
+    for a in range(count):
+        for side, owner in ((0, diagonal), (1, core)):
+            for s in (0, 1):
+                copy = send(
+                    ins[a].at[2 * owner + s],
+                    from_core.at[a, side, s],
+                    s_core.at[a, side, s],
+                    r_core.at[a, side, s],
+                    at(core, j),
+                )
+                copy.start()
+                pending.append(copy)
+    across_copies = []
+    for a in range(count):
+        for s in (0, 1):
+            pltpu.make_async_copy(
+                ins[a].at[s], from_core.at[a, 0, s], r_core.at[a, 0, s]
+            ).wait()
+            both = ins[a][2 * across + s].astype(jnp.float32) + from_core[a, 0, s].astype(
+                jnp.float32
+            )
+            to_x[a, s] = both.astype(jnp.bfloat16)
+            copy = send(
+                to_x.at[a, s], from_x.at[a, s], s_x.at[a, s], r_x.at[a, s], at(across, j)
+            )
+            copy.start()
+            across_copies.append(copy)
+    for a in range(count):
+        for s in (0, 1):
+            pltpu.make_async_copy(
+                ins[a].at[s], from_core.at[a, 1, s], r_core.at[a, 1, s]
+            ).wait()
+            outs[a][s] = ins[a][2 * i + s].astype(jnp.float32) + from_core[a, 1, s].astype(
+                jnp.float32
+            )
+    for a in range(count):
+        for s in (0, 1):
+            pltpu.make_async_copy(ins[a].at[s], from_x.at[a, s], r_x.at[a, s]).wait()
+            outs[a][s] = outs[a][s] + from_x[a, s].astype(jnp.float32)
+    for copy in pending + across_copies:
+        copy.wait_send()
+
+
+def reduce_group(arrays, collective_id):
+    count = len(arrays)
+    _, rows, width = arrays[0].shape
+    block = (rows, width)
+    return comm_call(
+        functools.partial(reduce_kernel, count),
+        [f32(2, rows, width) for _ in arrays],
+        [
+            pltpu.VMEM((count, 2, 2) + block, jnp.bfloat16),
+            pltpu.VMEM((count, 2) + block, jnp.bfloat16),
+            pltpu.VMEM((count, 2) + block, jnp.bfloat16),
+            DMA((count, 2, 2)),
+            DMA((count, 2, 2)),
+            DMA((count, 2)),
+            DMA((count, 2)),
+        ],
+        collective_id,
+        count,
+    )(*arrays)
+
+
+def small_sum_kernel(x_ref, o_ref, first, second, s_sem, r_sem, s_sem2, r_sem2):
+    i, j = lax.axis_index("dp"), lax.axis_index("seq")
+    groups = [at(lax.rem(i + step, 4), j) for step in (1, 2, 3)]
+    chains = [at(i, lax.rem(j + step, 8)) for step in range(1, 8)]
+    meet(groups + chains)
+    copies = []
+    for step, peer in enumerate(groups):
+        copy = send(x_ref, first.at[i], s_sem.at[step], r_sem.at[step], peer)
+        copy.start()
+        copies.append(copy)
+    first[i] = x_ref[...]
+    for copy in copies:
+        copy.wait()
+    second[j] = (first[0] + first[1]) + (first[2] + first[3])
+    copies = []
+    for step, peer in enumerate(chains):
+        copy = send(second.at[j], second.at[j], s_sem2.at[step], r_sem2.at[step], peer)
+        copy.start()
+        copies.append(copy)
+    for copy in copies:
+        copy.wait()
+    total = second[0]
+    for step in range(1, 8):
+        total = total + second[step]
+    o_ref[...] = total
+
+
+def small_sum(x, collective_id):
+    return comm_call(
+        small_sum_kernel,
+        [jax.ShapeDtypeStruct(x.shape, x.dtype)],
+        [
+            pltpu.VMEM((4,) + x.shape, x.dtype),
+            pltpu.VMEM((8,) + x.shape, x.dtype),
+            DMA((3,)),
+            DMA((3,)),
+            DMA((7,)),
+            DMA((7,)),
+        ],
+        collective_id,
+        1,
+    )(x)[0]
+
+
+NT = (((1,), (1,)), ((), ()))
+TN = (((0,), (0,)), ((), ()))
+
+
+def swap_halves(x):
+    lane = lax.broadcasted_iota(jnp.int32, x.shape, 1)
+    width = x.shape[1]
+    return jnp.where(lane % 64 < 32, pltpu.roll(x, width - 32, 1), pltpu.roll(x, 32, 1))
+
+
+def attention_kernel(p_ref, cos_ref, sin_ref, idc_ref, idr_ref, bias_ref, q_ref, k_ref, v_ref, o_ref, lse_ref):
+    @pl.loop(0, 4)
+    def _(block):
+        rows = pl.ds(block * 256, 256)
+        cos_t, sin_t = cos_ref[rows, :], sin_ref[rows, :]
+        for pair in (0, 1):
+            cols = slice(128 * pair, 128 * pair + 128)
+            for base, out in ((0, q_ref), (256, k_ref)):
+                x = p_ref[rows, base + 128 * pair : base + 128 * pair + 128]
+                out[rows, cols] = (x * cos_t + swap_halves(x) * sin_t).astype(jnp.bfloat16)
+        v_ref[rows, :] = p_ref[rows, 512:768].astype(jnp.bfloat16)
+
+    @pl.loop(0, 4)
+    def _(block):
+        start = block * 256
+        rows = pl.ds(start, 256)
+        seg_q, var_q = idc_ref[rows, 0:1], idc_ref[rows, 1:2]
+        code_k, var_k = idr_ref[0:1, :], idr_ref[1:2, :]
+        row = start + lax.broadcasted_iota(jnp.int32, (256, 1024), 0)
+        col = lax.broadcasted_iota(jnp.int32, (256, 1024), 1)
+        allowed = ((seg_q == code_k) & (jnp.abs(row - col) <= WINDOW)) | (row == col)
+        masked = jnp.where(allowed, 0.0, NEGATIVE)
+        same = jnp.where(var_q == var_k, 1.0, 0.0)
+        stats = jnp.zeros((256, 128), jnp.float32)
+        lane = lax.broadcasted_iota(jnp.int32, (256, 128), 1)
+        for h in range(4):
+            cols = slice(64 * h, 64 * h + 64)
+            scores = lax.dot_general(
+                q_ref[rows, cols] * 0.125, k_ref[:, cols], NT, preferred_element_type=jnp.float32
+            )
+            scores = scores + bias_ref[h] * same + masked
+            top = jnp.max(scores, axis=1, keepdims=True)
+            weight = jnp.exp(scores - top)
+            total = jnp.sum(weight, axis=1, keepdims=True)
+            mixed = jnp.dot(
+                weight.astype(jnp.bfloat16), v_ref[:, cols], preferred_element_type=jnp.float32
+            )
+            o_ref[rows, cols] = (mixed / total).astype(jnp.bfloat16)
+            stats = jnp.where(lane == h, top + jnp.log(total), stats)
+        lse_ref[rows, :] = stats
+
+
+def attention_back_kernel(
+    q_ref, k_ref, v_ref, do_ref, lse_ref, cos_ref, sin_ref, idc_ref, idr_ref, bias_ref,
+    dqkv_ref, dbias_ref, dq_acc, dk_acc, dv_acc,
+):
+    dk_acc[...] = jnp.zeros_like(dk_acc)
+    dv_acc[...] = jnp.zeros_like(dv_acc)
+    dbias_ref[...] = jnp.zeros_like(dbias_ref)
+
+    @pl.loop(0, 4)
+    def _(block):
+        start = pl.multiple_of(block * 256, 256)
+        rows = pl.ds(start, 256)
+        code_k, var_k = idc_ref[:, 2:3], idc_ref[:, 1:2]
+        seg_q, var_q = idr_ref[2:3, rows], idr_ref[1:2, rows]
+        row = lax.broadcasted_iota(jnp.int32, (1024, 256), 0)
+        col = start + lax.broadcasted_iota(jnp.int32, (1024, 256), 1)
+        allowed = ((seg_q == code_k) & (jnp.abs(row - col) <= WINDOW)) | (row == col)
+        masked = jnp.where(allowed, 0.0, NEGATIVE)
+        same = jnp.where(var_q == var_k, 1.0, 0.0)
+        for h in range(4):
+            cols = slice(64 * h, 64 * h + 64)
+            q_h, k_h, v_h = q_ref[rows, cols] * 0.125, k_ref[:, cols], v_ref[:, cols]
+            do_h = do_ref[rows, cols]
+            scores = lax.dot_general(k_h, q_h, NT, preferred_element_type=jnp.float32)
+            scores = scores + bias_ref[h] * same + masked
+            prob = jnp.exp(scores - lse_ref[h : h + 1, rows])
+            dv_acc[:, cols] += jnp.dot(
+                prob.astype(jnp.bfloat16), do_h, preferred_element_type=jnp.float32
+            )
+            dprob = lax.dot_general(v_h, do_h, NT, preferred_element_type=jnp.float32)
+            mean = jnp.sum(prob * dprob, axis=0, keepdims=True)
+            dscore = (prob * (dprob - mean)).astype(jnp.bfloat16)
+            dbias_ref[h : h + 1, :] += jnp.sum(
+                dscore.astype(jnp.float32) * same, axis=0, keepdims=True
+            )
+            dk_acc[:, cols] += jnp.dot(dscore, q_h, preferred_element_type=jnp.float32)
+            dq_acc[rows, cols] = lax.dot_general(
+                dscore, k_h, TN, preferred_element_type=jnp.float32
+            ) * 0.125
+
+    @pl.loop(0, 4)
+    def _(block):
+        rows = pl.ds(pl.multiple_of(block * 256, 256), 256)
+        cos_t, sin_t = cos_ref[rows, :], sin_ref[rows, :]
+        for pair in (0, 1):
+            cols = slice(128 * pair, 128 * pair + 128)
+            for base, acc in ((0, dq_acc), (256, dk_acc)):
+                g = acc[rows, cols]
+                dqkv_ref[rows, base + 128 * pair : base + 128 * pair + 128] = (
+                    g * cos_t - swap_halves(g) * sin_t
+                ).astype(jnp.bfloat16)
+        dqkv_ref[rows, 512:768] = dv_acc[rows, :].astype(jnp.bfloat16)
+
+
+def local_call(kernel, outs, scratch, specs, vmem):
+    return pl.pallas_call(
+        kernel,
+        out_shape=outs,
+        in_specs=specs,
+        out_specs=[VM] * len(outs),
+        scratch_shapes=scratch,
+        compiler_params=pltpu.CompilerParams(vmem_limit_bytes=vmem),
+    )
+
+
+SM = pl.BlockSpec(memory_space=pltpu.SMEM)
+
+
+def wide(ref, first, rows):
+    return jnp.concatenate([ref[first, rows, :], ref[first + 1, rows, :]], axis=1)
+
+
+def store_wide(ref, first, rows, value):
+    ref[first, rows, :] = value[:, :128]
+    ref[first + 1, rows, :] = value[:, 128:]
+
+
+EVERY = slice(None)
+
+
+def ffn_kernel(
+    a_ref, g_ref, wg_ref, wu_ref, wd_ref,
+    da_ref, out_ref, gg_ref, gu_ref, gd_ref,
+    turned, da_acc, out_acc, hidden_s, dgate_s, dup_s,
+):
+    step, last = pl.program_id(0), pl.num_programs(0) - 1
+
+    @pl.when(step == 0)
+    def _():
+        @pl.loop(0, 4)
+        def _(t):
+            rows = pl.ds(pl.multiple_of(t * 256, 256), 256)
+            for d in range(4):
+                cols = slice(256 * d, 256 * d + 256)
+                turned[cols, rows] = a_ref[rows, cols].T
+
+    wg, wu = wide(wg_ref, 0, EVERY), wide(wu_ref, 0, EVERY)
+    wd = jnp.concatenate([wd_ref[b] for b in range(8)], axis=1)
+
+    @pl.loop(0, 4)
+    def _(t):
+        rows = pl.ds(pl.multiple_of(t * 256, 256), 256)
+        a, g = a_ref[rows, :], g_ref[rows, :]
+        gate, up, dh = dot(a, wg), dot(a, wu), dot(g, wd, NT)
+        sig = 1.0 / (1.0 + jnp.exp(-gate))
+        gate_sig = gate * sig
+        hidden = (gate_sig * up).astype(jnp.bfloat16)
+        dgate = (dh * up * (sig + gate_sig * (1.0 - sig))).astype(jnp.bfloat16)
+        dup = (dh * gate_sig).astype(jnp.bfloat16)
+        hidden_s[rows, :] = hidden
+        dgate_s[rows, :] = dgate
+        dup_s[rows, :] = dup
+        da = dot(dgate, wg, NT) + dot(dup, wu, NT)
+        out = dot(hidden, wd)
+
+        @pl.when(step == 0)
+        def _():
+            da_acc[rows, :] = da
+            out_acc[rows, :] = out
+
+        @pl.when(step > 0)
+        def _():
+            da_acc[rows, :] += da
+            out_acc[rows, :] += out
+
+    @pl.loop(0, 4)
+    def _(d):
+        rows = pl.ds(pl.multiple_of(d * 256, 256), 256)
+        a_t = turned[rows, :]
+        store_wide(gg_ref, 0, rows, dot(a_t, dgate_s[...], out=jnp.bfloat16))
+        store_wide(gu_ref, 0, rows, dot(a_t, dup_s[...], out=jnp.bfloat16))
+
+    h_t = hidden_s[...].T
+    for d in range(4):
+        store_wide(gd_ref, 2 * d, EVERY, dot(h_t, g_ref[:, 256 * d : 256 * d + 256], out=jnp.bfloat16))
+
+    @pl.when(step == last)
+    def _():
+        da_ref[...] = da_acc[...].astype(jnp.bfloat16)
+        out_ref[...] = out_acc[...].astype(jnp.bfloat16)
+
+
+def ffn(a2, g_low, weights):
+    tile = (2, 1024, 128)
+    grads = [
+        pl.BlockSpec(tile, lambda f: (f, 0, 0)),
+        pl.BlockSpec(tile, lambda f: (f, 0, 0)),
+        pl.BlockSpec((8, 256, 128), lambda f: (0, f, 0)),
+    ]
+    whole = pl.BlockSpec((1024, 1024), lambda f: (0, 0))
+    return pl.pallas_call(
+        ffn_kernel,
+        grid=(4,),
+        out_shape=[bf16(1024, 1024)] * 2 + [bf16(8, 1024, 128)] * 3,
+        in_specs=[
+            whole,
+            whole,
+            pl.BlockSpec(tile, lambda f: (f, 0, 0)),
+            pl.BlockSpec(tile, lambda f: (f, 1, 0)),
+            pl.BlockSpec((8, 256, 128), lambda f: (0, 8 + f, 0)),
+        ],
+        out_specs=[whole, whole] + grads,
+        scratch_shapes=[pltpu.VMEM((1024, 1024), jnp.bfloat16)]
+        + [pltpu.VMEM((1024, 1024), jnp.float32)] * 2
+        + [pltpu.VMEM((1024, 256), jnp.bfloat16)] * 3,
+        compiler_params=pltpu.CompilerParams(vmem_limit_bytes=52 << 20),
+        name="ffn",
+    )(a2, g_low, weights, weights, weights)
+
+
+def attention(proj, cos_t, sin_t, id_cols, id_rows, bias):
+    return local_call(
+        attention_kernel, [bf16(1024, 256)] * 4 + [f32(1024, 128)], [], [VM] * 5 + [SM], 48 << 20
+    )(proj, cos_t, sin_t, id_cols, id_rows, bias)
+
+
+def attention_back(q, k, v, do, lse, cos_t, sin_t, id_cols, id_rows, bias):
+    return local_call(
+        attention_back_kernel,
+        [bf16(1024, 768), f32(8, 256)],
+        [pltpu.VMEM((1024, 256), jnp.float32)] * 3,
+        [VM] * 9 + [SM],
+        48 << 20,
+    )(q, k, v, do, lse, cos_t, sin_t, id_cols, id_rows, bias)
+
+
+SLOTS = (
+    (0, 1, 2, 4, 5, 6, 8, 9, 10, 12, 13, 14),
+    (0, 2, 3, 4, 6, 7, 8, 10, 11, 12, 14, 15),
+)
+
+
+def dot(a, b, dims=None, out=jnp.float32):
+    dims = (((1,), (0,)), ((), ())) if dims is None else dims
+    return lax.dot_general(a, b, dims, preferred_element_type=jnp.float32).astype(out)
+
+
+def on_group(
+    tokens, segment_ids, variate_ids, time_ids, pad_mask, cotangent,
+    w_qkv, w_out, w_gate, w_up, w_down, gain_attn, gain_ffn, variate_bias,
+):
+    i = lax.axis_index("dp")
+    low_half = i < 2
+    gain_one, gain_two = gain_attn.astype(jnp.float32), gain_ffn.astype(jnp.float32)
+
+    packed = jnp.pad(w_qkv, ((0, 0), (0, 128))).reshape(256, 2, 4, 64)
+    packed = packed.transpose(2, 0, 1, 3).reshape(4, 256, 128)
+    ids = jnp.stack([segment_ids, variate_ids, time_ids, pad_mask], axis=1)
+    ids = jnp.pad(ids, ((0, 0), (0, 4), (0, 0)))
+    own_tok, own_cot, own_ids, attn_block, ffn_block = front(
+        [tokens, cotangent, ids, packed, w_out, w_gate, w_up, w_down], 1
+    )
+    attn_w = lax.all_gather(attn_block, "seq")
+    ffn_w = lax.all_gather(ffn_block, "seq")
+    all_tok, all_cot, all_ids = gather_group([own_tok, own_cot, own_ids], 4)
+    all_tok = all_tok.reshape(1024, 1024)
+    g_low = all_cot.reshape(1024, 1024)
+    id_seq = all_ids.transpose(1, 0, 2).reshape(8, 1024)
+    seg, var, time, pad = id_seq[0], id_seq[1], id_seq[2], id_seq[3]
+    code = jnp.where(pad == 1, seg, -1)
+    id_rows = jnp.stack([code, var, seg] + [seg] * 5)
+    id_cols = jnp.pad(jnp.stack([seg, var, code], axis=1), ((0, 0), (0, 125)))
+    frequency = jnp.exp(-jnp.log(10000.0) * jnp.arange(32, dtype=jnp.float32) / 32)
+    angles = time.astype(jnp.float32)[:, None] * frequency[None, :]
+    cos_h, sin_h = jnp.cos(angles), jnp.sin(angles)
+    cos_t = jnp.concatenate([cos_h] * 4, axis=1)
+    sin_t = jnp.concatenate([-sin_h, sin_h] * 2, axis=1)
+    bias = jnp.where(
+        jnp.arange(4)[None, :] == i, variate_bias.astype(jnp.float32).reshape(4, 4), 0.0
+    ).sum(axis=1)
+
+    resid = all_tok.astype(jnp.float32)
+    a1 = (resid * norm_scale(resid) * gain_one).astype(jnp.bfloat16)
+
+    slots = attn_w[:, :1024].reshape(8, 1024, 2, 64)
+
+    def column(m):
+        first, second = SLOTS[0][m], SLOTS[1][m]
+        return jnp.where(
+            low_half, slots[first // 2, :, first % 2], slots[second // 2, :, second % 2]
+        )
+
+    w_heads = jnp.concatenate([column(m) for m in range(12)], axis=1)
+    w_mix = attn_w[:, 1024:].transpose(1, 0, 2).reshape(256, 1024)
+    proj = dot(a1, w_heads)
+    q, k, v, attended, lse = attention(proj, cos_t, sin_t, id_cols, id_rows, bias)
+    lse_rows = lse[:, :8].T
+    part = dot(attended, w_mix, out=jnp.bfloat16).reshape(8, 128, 1024)
+    (branch,) = reduce_group([part], 5)
+
+    own = own_tok.reshape(256, 1024).astype(jnp.float32)
+    inv_one = norm_scale(own)
+    mid = own + branch.reshape(256, 1024)
+    inv_two = norm_scale(mid)
+    a2_own = (mid * inv_two * gain_two).astype(jnp.bfloat16)
+    (a2,) = gather_group([a2_own.reshape(2, 128, 1024)], 6)
+    a2 = a2.reshape(1024, 1024)
+
+    da2_part, out_part, g_gate, g_up, g_down = ffn(a2, g_low, ffn_w)
+    ffn_grads = jnp.concatenate([g_gate, g_up, g_down], axis=1)
+    ffn_sum = lax.psum_scatter(ffn_grads, "seq", scatter_dimension=0)
+    da2, ffn_out = reduce_group([da2_part.reshape(8, 128, 1024), out_part.reshape(8, 128, 1024)], 7)
+
+    def blocks(g):
+        return g.astype(jnp.bfloat16).reshape(-1, 8, 128).transpose(1, 0, 2)
+
+    da2 = da2.reshape(256, 1024)
+    output = (mid + ffn_out.reshape(256, 1024)).astype(jnp.bfloat16)
+    grad_gain_two = jnp.sum(da2 * mid * inv_two, axis=0)
+    own_cot = own_cot.reshape(256, 1024).astype(jnp.float32)
+    e2 = own_cot + norm_back(da2 * gain_two, mid, inv_two)
+    (ez,) = gather_group([e2.astype(jnp.bfloat16).reshape(2, 128, 1024)], 8)
+    ez = ez.reshape(1024, 1024)
+    do = dot(ez, w_mix, NT, jnp.bfloat16)
+    dqkv, dbias = attention_back(q, k, v, do, lse_rows, cos_t, sin_t, id_cols, id_rows, bias)
+    da1_part = dot(dqkv, w_heads, NT, jnp.bfloat16).reshape(8, 128, 1024)
+    (da1,) = reduce_group([da1_part], 9)
+    da1 = da1.reshape(256, 1024)
+    grad_gain_one = jnp.sum(da1 * own * inv_one, axis=0)
+    input_grad = (e2 + norm_back(da1 * gain_one, own, inv_one)).astype(jnp.bfloat16)
+    output, input_grad = send_home(
+        [output.reshape(2, 128, 1024), input_grad.reshape(2, 128, 1024)], 10
+    )
+
+    grad_heads = dot(a1, dqkv, TN, jnp.bfloat16).reshape(1024, 12, 64)
+    grad_mix = dot(attended, ez, TN)
+    nothing = jnp.zeros((1024, 64), jnp.bfloat16)
+
+    def slot_grad(slot):
+        picks = [
+            grad_heads[:, SLOTS[half].index(slot)] if slot in SLOTS[half] else nothing
+            for half in (0, 1)
+        ]
+        return jnp.where(low_half, picks[0], picks[1])
+
+    grad_slots = jnp.stack(
+        [
+            jnp.concatenate([slot_grad(2 * b), slot_grad(2 * b + 1)], axis=1)
+            for b in range(8)
+        ]
+    )
+    attn_grads = jnp.concatenate([grad_slots, blocks(grad_mix)], axis=1)
+    attn_sum = lax.psum_scatter(attn_grads, "seq", scatter_dimension=0)
+
+    bias_grads = jnp.where(
+        jnp.arange(4)[None, :] == i, jnp.sum(dbias[:4], axis=1)[:, None], 0.0
+    ).reshape(16)
+    small = jnp.concatenate(
+        [grad_gain_one, grad_gain_two, jnp.pad(bias_grads, (0, 1024 - 16))]
+    ).reshape(24, 128)
+    small = small_sum(small, 11).reshape(3, 1024)
+
+    g_gate, g_up, g_down = exchange(
+        lambda ins, outs, me, other, seq: grad_pieces("ffn", ins[0], outs, me, other, seq),
+        [ffn_sum], [bf16(256, 512), bf16(256, 512), bf16(1024, 128)], 4, 12,
+    )
+    g_qkv, g_out = exchange(
+        lambda ins, outs, me, other, seq: grad_pieces("attention", ins[0], outs, me, other, seq),
+        [attn_sum], [bf16(4, 256, 128), bf16(256, 128)], 2, 13,
+    )
+    g_qkv = g_qkv.reshape(4, 256, 2, 64).transpose(1, 2, 0, 3).reshape(256, 512)[:, :384]
+    up32 = lambda g: g.astype(jnp.float32)
+    return (
+        output, input_grad, up32(g_qkv), up32(g_out), up32(g_gate), up32(g_up), up32(g_down),
+        small[0], small[1], small[2, :16],
+    )
+
+
 def solution(mesh):
     in_specs = (
         P("dp", "seq", None),
@@ -386,6 +1186,7 @@
         P(),
         P(),
     )
+    grouped = mesh.shape["dp"] == 4 and mesh.shape["seq"] == 8
     return jax.shard_map(
-        on_device, mesh=mesh, in_specs=in_specs, out_specs=out_specs, check_vma=False
-    )
+        on_group if grouped else on_device, mesh=mesh, in_specs=in_specs, out_specs=out_specs, check_vma=False
+    )

time: 2230 us -> 593 us (0.27)
  waiting for transfers between devices: 1630 us -> 159 us
  Pallas kernels: 0 us -> 328 us
  starting transfers between devices: 201 us -> 0.16 us
  matrix products: 168 us -> 14.8 us
  blocking collectives: 59.5 us -> 0 us
  local copies, waits for them, and re-layouts: 70.1 us -> 33.4 us
  other arithmetic: 65.9 us -> 41.8 us
    reduce_scatter x10 -> x2, waiting for transfers between devices: 1110 us -> 127 us  [the longest x1 101 us: on_group(): ffn_sum = lax.psum_scatter(ffn_grads, 'seq', scatter_dimension=0)]
    pallas_call x0 -> x14, Pallas kernels: none -> 328 us  [the longest x3 93.8 us: gather_group(): comm_call(functools.partial(gather_kernel, count), [jax.ShapeDtypeStruct(...]
    all_gather x8 -> x2, waiting for transfers between devices: 286 us -> 31.4 us  [the longest x1 17.7 us: on_group(): ffn_w = lax.all_gather(ffn_block, 'seq')]
    ppermute x48 -> x0, waiting for transfers between devices: 236 us -> none  [passed_along(): return lax.ppermute(block, axis, route)]
    ppermute x48 -> x0, starting transfers between devices: 200 us -> none  [passed_along(): return lax.ppermute(block, axis, route)]
    dot_general x37 -> x6, matrix products: 168 us -> 14.8 us  [dot(): lax.dot_general(a, b, dims, preferred_element_type=jnp.float32).astype(out)]
    psum x1 -> x0, blocking collectives: 39.5 us -> none  [on_device(): lax.psum((bias_total, gain_one_total, gain_two_total), ('dp', 'seq'))]
    slice x19 -> x3, local copies, waits for them, and re-layouts: 38.1 us -> 4.97 us  [the longest x1 3.07 us: on_group(): slots = attn_w[:, :1024].reshape(8, 1024, 2, 64)]
  transfers between devices with their start and end apart: 66 -> 4, of which waited for: 32 -> 4; matrix products, arithmetic and copies ran while one was open for 10% -> 9% of each run, Pallas kernels for 0% -> 30%
where the time goes in v1:
time: 593 us; the launch traced here: 592 us
  Pallas kernels  328 us (55%)
  waiting for transfers between devices  159 us (27%)
  other arithmetic  41.8 us (7%)
  local copies, waits for them, and re-layouts  33.4 us (6%)
  matrix products  14.8 us (2%)
  between operations  14.6 us (2%)
    reduce_scatter x1, waiting for transfers between devices, on_group(): ffn_sum = lax.psum_scatter(ffn_grads, 'seq', scatter_dimension=0)  101 us
    pallas_call x3, Pallas kernels, gather_group(): comm_call(functools.partial(gather_kernel, count), [jax.ShapeDtypeStruct(...  93.8 us
    pallas_call x3, Pallas kernels, reduce_group(): comm_call(functools.partial(reduce_kernel, count), [f32(2, rows, width) f...  68.1 us
    pallas_call x1, Pallas kernels, ffn(): pl.pallas_call(ffn_kernel, grid=(4,), out_shape=[bf16(1024, 1024)] * 2 +...  41 us
    pallas_call x2, Pallas kernels, exchange(): comm_call(kernel, outs, [DMA((3, count)), DMA((3, count)), DMA((count,))]...  33.9 us
    pallas_call x1, Pallas kernels, front(): comm_call(front_kernel, [jax.ShapeDtypeStruct(v.shape, v.dtype) for v in...  27.5 us
    reduce_scatter x1, waiting for transfers between devices, on_group(): attn_sum = lax.psum_scatter(attn_grads, 'seq', scatter_dimension=0)  26.1 us
    unnamed x102, local copies, waits for them, and re-layouts  21.9 us
  transfers between devices with their start and end apart: 4, of which 4 were waited for; matrix products, arithmetic and copies ran while one was open for 9% of the time, Pallas kernels for 30%

profile of v1, /device:TPU:0, one launch (start us, length us, event | category | flops | bytes accessed | tf_op | source)
XLA Modules:
  0.0 591.5 jit_solution(9940065663927519029)
XLA Ops:
  10.6 27.5 %shard_map.213 = (bf16[2,128,1024]{2,1,0:T(8,128)(2,1)}, bf16[2,128,1024]{2,1,0:T(8,128)(2,1)}, s32[2,8,128]{2,1,0:T(8,128)}, bf16[1280,128]{1,0:T(8,128)(2,1)}, bf16[3072,128]{1,0:T(8,128)(2,1)}) custom-call(bf16[2,128,1024]{2,1,0:T(8,128)(2,1)} %refs_0_.1, bf16[2,128,1024]{2,1,0:T(8,128)(2,1)} %refs_1_.1, s32[2,8,128]{2,1,0:T(8,128)} %pad.16.refs_2_, ...), custom_call_target="tpu_custom_call" | custom-call | tf_op jit(solution)/shard_map/pallas_call | solution.py:588
  39.1 58.8 %shard_map.214 = (bf16[8,128,1024]{2,1,0:T(8,128)(2,1)}, bf16[8,128,1024]{2,1,0:T(8,128)(2,1)}, s32[8,8,128]{2,1,0:T(8,128)}) custom-call(bf16[2,128,1024]{2,1,0:T(8,128)(2,1)} %get-tuple-element.39.refs_0_, bf16[2,128,1024]{2,1,0:T(8,128)(2,1)} %get-tuple-element.40.refs_1_, s32[2,8,128]{2,1,0:T(8,128)} %get-tuple-element.41.refs_2_), custom_call_target="tpu_custom_call" | custom-call | tf_op jit(solution)/shard_map/pallas_call | solution.py:655
  106.2 13.7 %all-gather.5.cloned.1.call-done = bf16[10240,128]{1,0:T(8,128)(2,1)} async-done(((bf16[1280,128]{1,0:T(8,128)(2,1)}), bf16[10240,128]{1,0:T(8,128)(2,1)}) %all-gather.5.cloned.1.call-update) | async-done | bytes 2621456 | tf_op jit(solution)/shard_map/all_gather | solution.py:1044
  124.0 3.9 copy.120
  137.0 3.5 fusion.43.p_ref
  140.5 14.6 %shard_map.215 = (bf16[1024,256]{1,0:T(8,128)(2,1)S(1)}, bf16[1024,256]{1,0:T(8,128)(2,1)S(1)}, bf16[1024,256]{1,0:T(8,128)(2,1)S(1)}, bf16[1024,256]{1,0:T(8,128)(2,1)S(1)}, f32[1024,128]{1,0:T(8,128)S(1)}) custom-call(f32[1024,768]{1,0:T(8,128)} %fusion.43.p_ref, f32[1024,128]{1,0:T(8,128)S(1)} %pad_maximum_fusion.2.cos_ref, ...), custom_call_target="tpu_custom_call" | custom-call | tf_op jit(solution)/shard_map/pallas_call | solution.py:1003
  157.7 3.2 convolution_convert_fusion
  160.9 18.5 %shard_map.216 = f32[2,128,1024]{2,1,0:T(8,128)} custom-call(bf16[8,128,1024]{2,1,0:T(8,128)(2,1)} %bitcast.205), custom_call_target="tpu_custom_call" | custom-call | tf_op jit(solution)/shard_map/pallas_call | solution.py:719
  183.4 17.5 %shard_map.217 = bf16[8,128,1024]{2,1,0:T(8,128)(2,1)} custom-call(bf16[2,128,1024]{2,1,0:T(8,128)(2,1)} %multiply_convert_fusion.refs_0_), custom_call_target="tpu_custom_call" | custom-call | tf_op jit(solution)/shard_map/pallas_call | solution.py:655
  201.7 17.7 %all-gather.7.cloned.1.call-done = bf16[24576,128]{1,0:T(8,128)(2,1)} async-done(((bf16[3072,128]{1,0:T(8,128)(2,1)}), bf16[24576,128]{1,0:T(8,128)(2,1)}) %all-gather.7.cloned.1.call-update) | async-done | bytes 6291472 | tf_op jit(solution)/shard_map/all_gather | solution.py:1045
  219.3 41.0 %ffn.1 = (bf16[1024,1024]{1,0:T(8,128)(2,1)}, bf16[1024,1024]{1,0:T(8,128)(2,1)}, bf16[8,1024,128]{2,1,0:T(8,128)(2,1)}, bf16[8,1024,128]{2,1,0:T(8,128)(2,1)}, bf16[8,1024,128]{2,1,0:T(8,128)(2,1)}) custom-call(bf16[1024,1024]{1,0:T(8,128)(2,1)} %bitcast.206, bf16[1024,1024]{1,0:T(8,128)(2,1)} %bitcast.216, bf16[8,3072,128]{2,1,0:T(8,128)(2,1)} %bitcast.188, ...), custom_call_target="tpu_custom_call" | custom-call | tf_op jit(solution)/shard_map/ffn/pallas_call | solution.py:982
  260.4 30.8 %shard_map.218 = (f32[2,128,1024]{2,1,0:T(8,128)}, f32[2,128,1024]{2,1,0:T(8,128)}) custom-call(bf16[8,128,1024]{2,1,0:T(8,128)(2,1)} %bitcast.211, bf16[8,128,1024]{2,1,0:T(8,128)(2,1)} %bitcast.212), custom_call_target="tpu_custom_call" | custom-call | tf_op jit(solution)/shard_map/pallas_call | solution.py:719
  295.0 17.5 %shard_map.219 = bf16[8,128,1024]{2,1,0:T(8,128)(2,1)} custom-call(bf16[2,128,1024]{2,1,0:T(8,128)(2,1)} %fusion.41.refs_0_), custom_call_target="tpu_custom_call" | custom-call | tf_op jit(solution)/shard_map/pallas_call | solution.py:655
  316.3 21.0 %shard_map.220 = (bf16[1024,768]{1,0:T(8,128)(2,1)S(1)}, f32[8,256]{1,0:T(8,128)S(1)}) custom-call(bf16[1024,256]{1,0:T(8,128)(2,1)S(1)} %get-tuple-element.52.q_ref, bf16[1024,256]{1,0:T(8,128)(2,1)S(1)} %copy-done.1, bf16[1024,256]{1,0:T(8,128)(2,1)S(1)} %copy-done.3, bf16[1024,256]{1,0:T(8,128)(2,1)S(1)} %convolution_convert_fusion.4.do_ref, ...), custom_call_target="tpu_custom_call" | custom-call | tf_op jit(solution)/shard_map/pallas_call | solution.py:1009
  350.5 5.5 pad_maximum_fusion
  357.8 3.1 convolution_convert_fusion.1
  361.0 18.7 %shard_map.221 = f32[2,128,1024]{2,1,0:T(8,128)} custom-call(bf16[8,128,1024]{2,1,0:T(8,128)(2,1)} %bitcast.210), custom_call_target="tpu_custom_call" | custom-call | tf_op jit(solution)/shard_map/pallas_call | solution.py:719
  382.1 10.4 %shard_map.225 = f32[24,128]{1,0:T(8,128)} custom-call(f32[24,128]{1,0:T(8,128)} %pad_maximum_fusion.4.x_ref), custom_call_target="tpu_custom_call" | custom-call | tf_op jit(solution)/shard_map/pallas_call | solution.py:764
  392.6 3.2 fusion.8
  395.8 17.5 %shard_map.222 = (bf16[2,128,1024]{2,1,0:T(8,128)(2,1)}, bf16[2,128,1024]{2,1,0:T(8,128)(2,1)}) custom-call(bf16[2,128,1024]{2,1,0:T(8,128)(2,1)} %get-tuple-element.117.refs_0_, bf16[2,128,1024]{2,1,0:T(8,128)(2,1)} %get-tuple-element.116.refs_1_), custom_call_target="tpu_custom_call" | custom-call | tf_op jit(solution)/shard_map/pallas_call | solution.py:600
  414.4 26.1 %reduce-scatter.3.cloned.1.call-done = bf16[1,1280,128]{2,1,0:T(8,128)(2,1)} async-done(((bf16[8,1280,128]{2,1,0:T(8,128)(2,1)}), bf16[1,1280,128]{2,1,0:T(8,128)(2,1)}) %reduce-scatter.3.cloned.1.call-update) | async-done | bytes 327696 | tf_op jit(solution)/shard_map/reduce_scatter | solution.py:1134
  440.4 21.1 %shard_map.223 = (bf16[4,256,128]{2,1,0:T(8,128)(2,1)}, bf16[256,128]{1,0:T(8,128)(2,1)}) custom-call(bf16[1280,128]{1,0:T(8,128)(2,1)} %bitcast.227), custom_call_target="tpu_custom_call" | custom-call | tf_op jit(solution)/shard_map/pallas_call | solution.py:493
  464.4 100.9 %reduce-scatter.5.cloned.1.call-done = bf16[1,3072,128]{2,1,0:T(8,128)(2,1)} async-done(((bf16[8,3072,128]{2,1,0:T(8,128)(2,1)}), bf16[1,3072,128]{2,1,0:T(8,128)(2,1)}) %reduce-scatter.5.cloned.1.call-update) | async-done | bytes 786448 | tf_op jit(solution)/shard_map/reduce_scatter | solution.py:1092
  565.3 12.7 %shard_map.224 = (bf16[256,512]{1,0:T(8,128)(2,1)}, bf16[256,512]{1,0:T(8,128)(2,1)}, bf16[1024,128]{1,0:T(8,128)(2,1)}) custom-call(bf16[3072,128]{1,0:T(8,128)(2,1)} %bitcast.226), custom_call_target="tpu_custom_call" | custom-call | tf_op jit(solution)/shard_map/pallas_call | solution.py:493
  (186 shorter events, 68.5 us)
Async XLA Ops:
  7.2 112.7 %all-gather.5.cloned.1.call-start = ((), (), s32[]{:S(2)}) async-start(), calls=%async_computation.4 | async-start | bytes 2949120 | tf_op jit(solution)/shard_map/all_gather | solution.py:1044
  8.3 30.6 %copy-start.39 = (bf16[16]{0:T(256)(128)(2,1)S(1)}, bf16[16]{0:T(256)(128)(2,1)}, u32[]{:S(2)}) copy-start(bf16[16]{0:T(256)(128)(2,1)} %param.27) | copy-start | bytes 100
  8.3 30.7 %copy-start.35 = (bf16[1024]{0:T(1024)(128)(2,1)S(1)}, bf16[1024]{0:T(1024)(128)(2,1)}, u32[]{:S(2)}) copy-start(bf16[1024]{0:T(1024)(128)(2,1)} %param.26) | copy-start | bytes 6148
  8.3 30.7 %copy-start.36 = (bf16[1024]{0:T(1024)(128)(2,1)S(1)}, bf16[1024]{0:T(1024)(128)(2,1)}, u32[]{:S(2)}) copy-start(bf16[1024]{0:T(1024)(128)(2,1)} %param.25) | copy-start | bytes 6148
  38.1 181.2 %all-gather.7.cloned.1.call-start = ((), (), s32[]{:S(2)}) async-start(), calls=%async_computation.5 | async-start | bytes 7077888 | tf_op jit(solution)/shard_map/all_gather | solution.py:1045
  38.9 401.5 %reduce-scatter.3.cloned.1.call-start = ((), (), s32[]{:S(2)}) async-start(), calls=%async_computation.2 | async-start | bytes 2949120 | tf_op jit(solution)/shard_map/reduce_scatter | solution.py:1134
  100.9 2.9 copy-start.14
  129.0 6.5 %copy-start.9 = (bf16[8,1024,128]{1,2,0:T(8,128)(2,1)S(1)}, bf16[8,1024,128]{1,2,0:T(8,128)(2,1)}, u32[]{:S(2)}) copy-start(bf16[8,1024,128]{1,2,0:T(8,128)(2,1)} %copy.120) | copy-start | bytes 6291460
  129.0 8.0 %copy-start.17 = (bf16[1024,1024]{1,0:T(8,128)(2,1)S(1)}, bf16[1024,1024]{1,0:T(8,128)(2,1)}, u32[]{:S(2)}) copy-start(bf16[1024,1024]{1,0:T(8,128)(2,1)} %fusion.1) | copy-start | bytes 6291460
  160.9 18.5 %copy-start.15 = (bf16[2,128,1024]{2,1,0:T(8,128)(2,1)S(1)}, bf16[2,128,1024]{2,1,0:T(8,128)(2,1)}, u32[]{:S(2)}) copy-start(bf16[2,128,1024]{2,1,0:T(8,128)(2,1)} %get-tuple-element.39.refs_0_) | copy-start | bytes 1572868
  181.5 112.3 %copy-start.27 = (f32[2,128]{1,0:T(2,128)}, f32[2,128]{1,0:T(2,128)S(1)}, u32[]{:S(2)}) copy-start(f32[2,128]{1,0:T(2,128)S(1)} %add_rsqrt_fusion.1) | copy-start | bytes 3076
  260.3 33.4 %copy-start.16 = (bf16[2,128,1024]{2,1,0:T(8,128)(2,1)S(1)}, bf16[2,128,1024]{2,1,0:T(8,128)(2,1)}, u32[]{:S(2)}) copy-start(bf16[2,128,1024]{2,1,0:T(8,128)(2,1)} %get-tuple-element.40.refs_1_) | copy-start | bytes 1572868
  293.8 18.7 %copy-start.32 = (f32[2,128]{1,0:T(2,128)}, f32[2,128]{1,0:T(2,128)S(1)}, u32[]{:S(2)}) copy-start(f32[2,128]{1,0:T(2,128)S(1)} %broadcast_multiply_fusion.1) | copy-start | bytes 3076
  315.8 22.7 %copy-start.18 = (bf16[1024,1024]{1,0:T(8,128)(2,1)S(1)}, bf16[1024,1024]{1,0:T(8,128)(2,1)}, u32[]{:S(2)}) copy-start(bf16[1024,1024]{1,0:T(8,128)(2,1)} %fusion.1) | copy-start | bytes 6291460
  348.9 216.4 %reduce-scatter.5.cloned.1.call-start = ((), (), s32[]{:S(2)}) async-start(), calls=%async_computation.3 | async-start | bytes 7077888 | tf_op jit(solution)/shard_map/reduce_scatter | solution.py:1092
  361.0 20.6 %copy-start.29 = (f32[1024]{0:T(1024)S(1)}, f32[1024]{0:T(1024)}, u32[]{:S(2)}) copy-start(f32[1024]{0:T(1024)} %get-tuple-element.98) | copy-start | bytes 12292
  361.0 31.6 %copy-start.8 = (f32[2,128,1024]{2,1,0:T(8,128)S(1)}, f32[2,128,1024]{2,1,0:T(8,128)}, u32[]{:S(2)}) copy-start(f32[2,128,1024]{2,1,0:T(8,128)} %copy-done.6) | copy-start | bytes 3145732
  361.0 31.6 %copy-start.12 = (f32[2,128,1024]{2,1,0:T(8,128)S(1)}, f32[2,128,1024]{2,1,0:T(8,128)}, u32[]{:S(2)}) copy-start(f32[2,128,1024]{2,1,0:T(8,128)} %get-tuple-element.51) | copy-start | bytes 3145732
  361.0 31.6 %copy-start.28 = (f32[2,128]{1,0:T(2,128)S(1)}, f32[2,128]{1,0:T(2,128)}, u32[]{:S(2)}) copy-start(f32[2,128]{1,0:T(2,128)} %copy-done.27) | copy-start | bytes 3076
  361.0 31.6 %copy-start.33 = (f32[2,128]{1,0:T(2,128)S(1)}, f32[2,128]{1,0:T(2,128)}, u32[]{:S(2)}) copy-start(f32[2,128]{1,0:T(2,128)} %copy-done.32) | copy-start | bytes 3076
  379.7 12.9 %copy-start.10 = (f32[2,128,1024]{2,1,0:T(8,128)S(1)}, f32[2,128,1024]{2,1,0:T(8,128)}, u32[]{:S(2)}) copy-start(f32[2,128,1024]{2,1,0:T(8,128)} %shard_map.221) | copy-start | bytes 3145732
  392.6 20.6 %copy-start.25 = (f32[24,128]{1,0:T(8,128)S(1)}, f32[24,128]{1,0:T(8,128)}, u32[]{:S(2)}) copy-start(f32[24,128]{1,0:T(8,128)} %shard_map.225) | copy-start | bytes 36868
  462.8 120.6 %copy-start.24 = (bf16[2,128,1024]{2,1,0:T(8,128)(2,1)S(1)}, bf16[2,128,1024]{2,1,0:T(8,128)(2,1)}, u32[]{:S(2)}) copy-start(bf16[2,128,1024]{2,1,0:T(8,128)(2,1)} %get-tuple-element.157) | copy-start | bytes 1572868
  565.3 18.9 %copy-start.23 = (bf16[2,128,1024]{2,1,0:T(8,128)(2,1)S(1)}, bf16[2,128,1024]{2,1,0:T(8,128)(2,1)}, u32[]{:S(2)}) copy-start(bf16[2,128,1024]{2,1,0:T(8,128)(2,1)} %get-tuple-element.158) | copy-start | bytes 1572868
  (20 other events, 31.4 us)
Sparse Core Ops, SparseCore 0:
  38.3 81.5 all-gather.4
  122.0 97.2 all-gather.6
  349.0 91.3 reduce-scatter.2
  443.9 121.3 reduce-scatter.4

commit v2 on v1

--- a/solution.py
+++ b/solution.py
@@ -364,22 +364,45 @@
 
 MESH = pl.DeviceIdType.MESH
 VM = pl.BlockSpec(memory_space=pltpu.VMEM)
+HB = pl.BlockSpec(memory_space=pl.ANY)
+SM = pl.BlockSpec(memory_space=pltpu.SMEM)
 DMA = pltpu.SemaphoreType.DMA
+NT = (((1,), (1,)), ((), ()))
+TN = (((0,), (0,)), ((), ()))
+EVERY = slice(None)
+
+
+def bf16(*shape):
+    return jax.ShapeDtypeStruct(shape, jnp.bfloat16)
+
+
+def f32(*shape):
+    return jax.ShapeDtypeStruct(shape, jnp.float32)
+
+
+def dot(a, b, dims=None, out=jnp.float32):
+    dims = (((1,), (0,)), ((), ())) if dims is None else dims
+    return lax.dot_general(a, b, dims, preferred_element_type=jnp.float32).astype(out)
 
 
 def at(dp, seq):
     return {"dp": dp, "seq": seq}
 
 
+def place():
+    return lax.axis_index("dp"), lax.axis_index("seq")
+
+
 def ring(i):
     return i + 1 - 2 * lax.rem(i, 2), lax.rem(i + 2, 4)
 
 
-def meet(peers):
-    barrier = pltpu.get_barrier_semaphore()
-    for peer in peers:
-        pl.semaphore_signal(barrier, inc=1, device_id=peer, device_id_type=MESH)
-    pl.semaphore_wait(barrier, len(peers))
+def owned(i, s):
+    return 4 * lax.rem(i, 2) + 2 * s + i // 2
+
+
+def keeper(j):
+    return 2 * lax.rem(j, 2) + j // 4
 
 
 def send(src, dst, send_sem, recv_sem, peer):
@@ -391,6 +414,592 @@
         device_id=peer,
         device_id_type=MESH,
     )
+
+
+def landed(ref, sem):
+    pltpu.make_async_copy(ref, ref, sem).wait()
+
+
+def meet(peers, home=False):
+    i, j = place()
+    barrier = pltpu.get_barrier_semaphore()
+    for peer in peers:
+        pl.semaphore_signal(barrier, inc=1, device_id=peer, device_id_type=MESH)
+    if home:
+        target, stays = keeper(j), keeper(j) == i
+        for s in (0, 1):
+
+            @pl.when(jnp.logical_not(stays & (owned(i, s) == j)))
+            def _():
+                pl.semaphore_signal(
+                    barrier, inc=1, device_id=at(target, owned(i, s)), device_id_type=MESH
+                )
+
+        pl.semaphore_wait(barrier, len(peers) + jnp.where(stays, 1, 2))
+    else:
+        pl.semaphore_wait(barrier, len(peers))
+
+
+def dp_peers():
+    i, j = place()
+    return [at(lax.rem(i + step, 4), j) for step in (1, 2, 3)]
+
+
+def seq_peers():
+    i, j = place()
+    z, y = j // 2, lax.rem(j, 2)
+    return [at(i, 2 * lax.rem(z + step, 4) + y) for step in (1, 2, 3)] + [at(i, 2 * z + 1 - y)]
+
+
+class Home:
+    def __init__(self, ins, outs, sems, slotted):
+        self.ins, self.outs, self.slotted = ins, outs, slotted
+        self.send_sem, self.recv_sem = sems
+
+    @staticmethod
+    def sems(count):
+        return [DMA((count, 2)), DMA((count, 2))]
+
+    def target(self, a, s):
+        i, _ = place()
+        return self.outs[a].at[s if self.slotted else owned(i, s)]
+
+    def start(self, a, s):
+        i, j = place()
+        slot = lax.rem(j // 2, 2)
+        src, dst = self.ins[a].at[s], self.outs[a].at[slot if self.slotted else j]
+        here = (keeper(j) == i) & (owned(i, s) == j)
+
+        @pl.when(jnp.logical_not(here))
+        def _():
+            peer = at(keeper(j), owned(i, s))
+            send(src, dst, self.send_sem.at[a, s], self.recv_sem.at[a, slot], peer).start()
+
+        @pl.when(here)
+        def _():
+            pltpu.make_async_copy(src, dst, self.recv_sem.at[a, slot]).start()
+
+    def wait(self, a, s):
+        landed(self.target(a, s), self.recv_sem.at[a, s])
+
+    def finish(self, a):
+        i, j = place()
+        for s in (0, 1):
+
+            @pl.when(jnp.logical_not((keeper(j) == i) & (owned(i, s) == j)))
+            def _():
+                landed(self.ins[a].at[s], self.send_sem.at[a, s])
+
+
+class GroupGather:
+    def __init__(self, outs, sems):
+        self.outs = outs
+        self.s_core, self.r_core, self.s_x, self.r_x, self.s_on, self.r_on = sems
+
+    @staticmethod
+    def sems(count):
+        return [DMA((count, 2))] * 6
+
+    def push(self, a, s):
+        i, j = place()
+        core, across = ring(i)
+        block = self.outs[a].at[owned(i, s)]
+        send(block, block, self.s_x.at[a, s], self.r_x.at[a, s], at(across, j)).start()
+        send(block, block, self.s_core.at[a, s], self.r_core.at[a, s], at(core, j)).start()
+
+    def relay(self, a, s):
+        i, j = place()
+        core, across = ring(i)
+        block = self.outs[a].at[owned(across, s)]
+        landed(block, self.r_x.at[a, s])
+        send(block, block, self.s_on.at[a, s], self.r_on.at[a, s], at(core, j)).start()
+
+    def finish(self, a):
+        i, _ = place()
+        core, _ = ring(i)
+        for s in (0, 1):
+            landed(self.outs[a].at[owned(core, s)], self.r_core.at[a, s])
+            landed(self.outs[a].at[owned(lax.rem(core + 2, 4), s)], self.r_on.at[a, s])
+        for s in (0, 1):
+            for sem in (self.s_x, self.s_core, self.s_on):
+                landed(self.outs[a].at[s], sem.at[a, s])
+
+
+class GroupSum:
+    def __init__(self, parts, scratch):
+        self.parts = parts
+        self.near, self.out, self.far = scratch[:3]
+        self.s_core, self.r_core, self.s_x, self.r_x = scratch[3:]
+
+    @staticmethod
+    def scratch(count):
+        block = (128, 1024)
+        return [
+            pltpu.VMEM((count, 2, 2) + block, jnp.bfloat16),
+            pltpu.VMEM((count, 2) + block, jnp.bfloat16),
+            pltpu.VMEM((count, 2) + block, jnp.bfloat16),
+            DMA((count, 2, 2)),
+            DMA((count, 2, 2)),
+            DMA((count, 2)),
+            DMA((count, 2)),
+        ]
+
+    def start(self, a):
+        i, j = place()
+        core, _ = ring(i)
+        for side, owner in ((0, lax.rem(core + 2, 4)), (1, core)):
+            for s in (0, 1):
+                send(
+                    self.parts[a].at[owned(owner, s)],
+                    self.near.at[a, side, s],
+                    self.s_core.at[a, side, s],
+                    self.r_core.at[a, side, s],
+                    at(core, j),
+                ).start()
+
+    def cross(self, a, s):
+        i, j = place()
+        _, across = ring(i)
+        landed(self.near.at[a, 0, s], self.r_core.at[a, 0, s])
+        both = self.parts[a][owned(across, s)].astype(jnp.float32)
+        both = both + self.near[a, 0, s].astype(jnp.float32)
+        self.out[a, s] = both.astype(jnp.bfloat16)
+        send(
+            self.out.at[a, s], self.far.at[a, s], self.s_x.at[a, s], self.r_x.at[a, s], at(across, j)
+        ).start()
+
+    def total(self, a, s):
+        i, _ = place()
+        landed(self.near.at[a, 1, s], self.r_core.at[a, 1, s])
+        both = self.parts[a][owned(i, s)].astype(jnp.float32)
+        both = both + self.near[a, 1, s].astype(jnp.float32)
+        landed(self.far.at[a, s], self.r_x.at[a, s])
+        return both + self.far[a, s].astype(jnp.float32)
+
+    def finish(self, a):
+        for s in (0, 1):
+            landed(self.out.at[a, s], self.s_x.at[a, s])
+            for side in (0, 1):
+                landed(self.near.at[a, side, s], self.s_core.at[a, side, s])
+
+
+class Exchange:
+    def __init__(self, pieces, sems):
+        self.pieces = pieces
+        self.send_sem, self.recv_sem, self.own_sem = sems
+        self.copies = []
+
+    @staticmethod
+    def sems(count):
+        return [DMA((3, count)), DMA((3, count)), DMA((count,))]
+
+    def start(self):
+        i, j = place()
+        for step in (2, 3, 1):
+            other = lax.rem(i + step, 4)
+            for index, (src, dst) in enumerate(self.pieces(i, other)):
+                copy = send(
+                    src,
+                    dst,
+                    self.send_sem.at[step - 1, index],
+                    self.recv_sem.at[step - 1, index],
+                    at(other, j),
+                )
+                copy.start()
+                self.copies.append(copy)
+        for index, (src, dst) in enumerate(self.pieces(i, i)):
+            copy = pltpu.make_async_copy(src, dst, self.own_sem.at[index])
+            copy.start()
+            self.copies.append(copy)
+
+    def wait(self):
+        for copy in self.copies:
+            copy.wait()
+
+
+class SeqGather:
+    def __init__(self, full, chunks, sems):
+        self.full, self.chunks = full, chunks
+        self.s_z, self.r_z, self.s_y, self.r_y = sems
+
+    @staticmethod
+    def sems(count):
+        return [DMA((count, 3)), DMA((count, 3)), DMA((count, 4)), DMA((count, 4))]
+
+    def block(self, chunk, z, y):
+        start, size = self.chunks[chunk]
+        return self.full.at[2 * z + y, pl.ds(start, size)]
+
+    def start(self, chunk):
+        i, j = place()
+        z, y = j // 2, lax.rem(j, 2)
+        own = self.block(chunk, z, y)
+        for dz in (2, 1, 3):
+            peer = at(i, 2 * lax.rem(z + dz, 4) + y)
+            send(own, own, self.s_z.at[chunk, dz - 1], self.r_z.at[chunk, dz - 1], peer).start()
+        send(own, own, self.s_y.at[chunk, 0], self.r_y.at[chunk, 0], at(i, 2 * z + 1 - y)).start()
+
+    def forward(self, chunk, dz):
+        i, j = place()
+        z, y = j // 2, lax.rem(j, 2)
+        block = self.block(chunk, lax.rem(z + 4 - dz, 4), y)
+        landed(block, self.r_z.at[chunk, dz - 1])
+        peer = at(i, 2 * z + 1 - y)
+        send(block, block, self.s_y.at[chunk, dz], self.r_y.at[chunk, dz], peer).start()
+
+    def finish(self, chunk):
+        _, j = place()
+        z, y = j // 2, lax.rem(j, 2)
+        own = self.block(chunk, z, y)
+        for dz in (0, 1, 2, 3):
+            landed(self.block(chunk, lax.rem(z + 4 - dz, 4), 1 - y), self.r_y.at[chunk, dz])
+            landed(own, self.s_y.at[chunk, dz])
+            if dz:
+                landed(own, self.s_z.at[chunk, dz - 1])
+
+
+class SeqSum:
+    def __init__(self, parts, mine, chunks, scratch):
+        self.parts, self.mine, self.chunks = parts, mine, chunks
+        self.near, self.out, self.far = scratch[:3]
+        self.s_y, self.r_y, self.s_z, self.r_z = scratch[3:]
+
+    @staticmethod
+    def scratch(rows, count):
+        return [
+            pltpu.VMEM((4, rows, 128), jnp.bfloat16),
+            pltpu.VMEM((3, rows, 128), jnp.bfloat16),
+            pltpu.VMEM((3, rows, 128), jnp.bfloat16),
+            DMA((count, 4)),
+            DMA((count, 4)),
+            DMA((count, 3)),
+            DMA((count, 3)),
+        ]
+
+    def rows(self, chunk):
+        return pl.ds(*self.chunks[chunk])
+
+    def start(self, chunk):
+        i, j = place()
+        z, y = j // 2, lax.rem(j, 2)
+        rows = self.rows(chunk)
+        for dz in (2, 1, 3, 0):
+            send(
+                self.parts.at[2 * lax.rem(z + dz, 4) + 1 - y, rows],
+                self.near.at[dz, rows],
+                self.s_y.at[chunk, dz],
+                self.r_y.at[chunk, dz],
+                at(i, 2 * z + 1 - y),
+            ).start()
+
+    def cross(self, chunk, dz):
+        i, j = place()
+        z, y = j // 2, lax.rem(j, 2)
+        start, size = self.chunks[chunk]
+        rows = self.rows(chunk)
+        landed(self.near.at[dz, rows], self.r_y.at[chunk, dz])
+        self.add(2 * lax.rem(z + dz, 4) + y, dz, start, size)
+        send(
+            self.out.at[dz - 1, rows],
+            self.far.at[dz - 1, rows],
+            self.s_z.at[chunk, dz - 1],
+            self.r_z.at[chunk, dz - 1],
+            at(i, 2 * lax.rem(z + dz, 4) + y),
+        ).start()
+
+    def add(self, block, dz, start, size):
+        @pl.loop(0, size // 256)
+        def _(t):
+            rows = pl.ds(pl.multiple_of(start + t * 256, 256), 256)
+            both = self.mine[block // 2, rows, :].astype(jnp.float32)
+            both = both + self.near[dz, rows, :].astype(jnp.float32)
+            self.out[dz - 1, rows, :] = both.astype(jnp.bfloat16)
+
+    def finish(self, chunk, store):
+        _, j = place()
+        start, size = self.chunks[chunk]
+        rows = self.rows(chunk)
+        landed(self.near.at[0, rows], self.r_y.at[chunk, 0])
+        for dz in (1, 2, 3):
+            landed(self.far.at[dz - 1, rows], self.r_z.at[chunk, dz - 1])
+
+        @pl.loop(0, size // 256)
+        def _(t):
+            part = pl.ds(pl.multiple_of(start + t * 256, 256), 256)
+            total = self.mine[j // 2, part, :].astype(jnp.float32)
+            total = total + self.near[0, part, :].astype(jnp.float32)
+            for dz in (1, 2, 3):
+                total = total + self.far[dz - 1, part, :].astype(jnp.float32)
+            store(part, total)
+
+    def drain(self, chunk):
+        rows = self.rows(chunk)
+        for dz in (0, 1, 2, 3):
+            landed(self.near.at[dz, rows], self.s_y.at[chunk, dz])
+            if dz:
+                landed(self.out.at[dz - 1, rows], self.s_z.at[chunk, dz - 1])
+
+
+def swap_halves(x):
+    lane = lax.broadcasted_iota(jnp.int32, x.shape, 1)
+    width = x.shape[1]
+    return jnp.where(lane % 64 < 32, pltpu.roll(x, width - 32, 1), pltpu.roll(x, 32, 1))
+
+
+def angle_tables(table):
+    lane = lax.broadcasted_iota(jnp.int32, table.shape, 1)
+    by_32, by_64, by_96 = (pltpu.roll(table, shift, 1) for shift in (32, 64, 96))
+    first, second, third = lane < 32, lane < 64, lane < 96
+    cos_t = jnp.where(first, table, jnp.where(second, by_32, jnp.where(third, by_64, by_96)))
+    sin_t = jnp.where(first, -by_96, jnp.where(second, table, jnp.where(third, -by_32, by_64)))
+    return cos_t, sin_t
+
+
+SLOTS = (
+    (0, 1, 2, 4, 5, 6, 8, 9, 10, 12, 13, 14),
+    (0, 2, 3, 4, 6, 7, 8, 10, 11, 12, 14, 15),
+)
+
+
+def attention_pieces(packed, w_out, dst):
+    def pieces(me, other):
+        _, j = place()
+        spot = lax.rem(other + 2 * lax.rem(j, 2), 4)
+        return [
+            (packed.at[spot], dst.at[j, pl.ds(256 * me, 256)]),
+            (w_out.at[pl.ds(64 * other, 64)], dst.at[j, pl.ds(1024 + 64 * me, 64)]),
+        ]
+
+    return pieces
+
+
+def ffn_pieces(w_gate, w_up, w_down, dst):
+    def pieces(me, other):
+        _, j = place()
+        columns = pl.ds(pl.multiple_of(128 * other, 128), 128)
+        pairs = [
+            (w_gate.at[:, columns], dst.at[j, pl.ds(256 * me, 256)]),
+            (w_up.at[:, columns], dst.at[j, pl.ds(1024 + 256 * me, 256)]),
+        ]
+        for half in (0, 1):
+            pairs.append(
+                (
+                    w_down.at[pl.ds(512 * half + 128 * other, 128)],
+                    dst.at[j, pl.ds(2048 + 256 * me + 128 * half, 128)],
+                )
+            )
+        return pairs
+
+    return pieces
+
+
+def head_weights(full, wh_ref, wm_ref, low_half):
+    def column(m, rows):
+        first, second = SLOTS[0][m], SLOTS[1][m]
+        one = full[first // 2, rows, 64 * (first % 2) : 64 * (first % 2) + 64]
+        two = full[second // 2, rows, 64 * (second % 2) : 64 * (second % 2) + 64]
+        return jnp.where(low_half, one, two)
+
+    @pl.loop(0, 4)
+    def _(t):
+        rows = pl.ds(pl.multiple_of(t * 256, 256), 256)
+        for m in range(0, 12, 2):
+            wh_ref[rows, 64 * m : 64 * m + 128] = jnp.concatenate(
+                [column(m, rows), column(m + 1, rows)], axis=1
+            )
+
+    for b in range(8):
+        wm_ref[:, 128 * b : 128 * b + 128] = full[b, 1024:1280, :]
+
+
+def norm_rows(hidden):
+    return lax.rsqrt(jnp.mean(hidden * hidden, axis=1, keepdims=True) + EPSILON)
+
+
+FFN_CHUNKS = ((0, 1024), (1024, 1024), (2048, 1024))
+
+
+def open_kernel(*refs):
+    (tok, cot, tab, idr, packed, w_out, w_gate, w_up, w_down, gain_one, gain_two, bias), refs = (
+        refs[:12],
+        refs[12:],
+    )
+    (
+        tok_all, cot_all, tab_all, idr_all, a1_ref, q_ref, k_ref, v_ref, o_ref, lse_ref,
+        wh_ref, wm_ref, mid_ref, a2_all, ffn_all,
+    ), refs = refs[:15], refs[15:]
+    (attn_all, part, cos_ref, sin_ref, rows_ref), refs = refs[:5], refs[5:]
+    home_sems, refs = refs[:2], refs[2:]
+    gather_sems, refs = refs[:6], refs[6:]
+    a2_sems, refs = refs[:6], refs[6:]
+    sum_scratch, refs = refs[:7], refs[7:]
+    spread_a, spread_f, refs = refs[:3], refs[3:6], refs[6:]
+    chain_a, chain_f = refs[:4], refs[4:8]
+
+    i, _ = place()
+    home = Home((tok, tab, idr, cot), (tok_all, tab_all, idr_all, cot_all), home_sems, False)
+    group = GroupGather((tok_all, tab_all, idr_all, cot_all), gather_sems)
+    spread = Exchange(attention_pieces(packed, w_out, attn_all), spread_a)
+    spread_ffn = Exchange(ffn_pieces(w_gate, w_up, w_down, ffn_all), spread_f)
+    attn_w = SeqGather(attn_all, ((0, 1280),), chain_a)
+    ffn_w = SeqGather(ffn_all, FFN_CHUNKS, chain_f)
+    branch = GroupSum((part,), sum_scratch)
+    second = GroupGather((a2_all,), a2_sems)
+
+    meet(dp_peers() + seq_peers(), home=True)
+    for a in (0, 1, 2):
+        for s in (0, 1):
+            home.start(a, s)
+    spread.start()
+    spread_ffn.start()
+    spread.wait()
+    attn_w.start(0)
+    for a in (0, 1, 2):
+        for s in (0, 1):
+            home.wait(a, s)
+            group.push(a, s)
+    for s in (0, 1):
+        home.start(3, s)
+    spread_ffn.wait()
+    for chunk in range(3):
+        ffn_w.start(chunk)
+    for a in (0, 1, 2):
+        for s in (0, 1):
+            group.relay(a, s)
+    for a in (0, 1, 2):
+        group.finish(a)
+        home.finish(a)
+
+    for b in range(8):
+        rows_ref[:, 128 * b : 128 * b + 128] = idr_all[b]
+
+    @pl.loop(0, 8)
+    def _(b):
+        rows = pl.ds(pl.multiple_of(b * 128, 128), 128)
+        hidden = tok_all[b].astype(jnp.float32)
+        a1_ref[rows, :] = (hidden * norm_rows(hidden) * gain_one[...]).astype(jnp.bfloat16)
+        cos_t, sin_t = angle_tables(tab_all[b])
+        cos_ref[rows, :] = cos_t
+        sin_ref[rows, :] = sin_t
+
+    for dz in (1, 2, 3):
+        attn_w.forward(0, dz)
+    for s in (0, 1):
+        home.wait(3, s)
+        group.push(3, s)
+    attn_w.finish(0)
+    head_weights(attn_all, wh_ref, wm_ref, i < 2)
+
+    @pl.loop(0, 4)
+    def _(t):
+        rows = pl.ds(pl.multiple_of(t * 256, 256), 256)
+        proj = dot(a1_ref[rows, :], wh_ref[...])
+        cos_t, sin_t = cos_ref[rows, :], sin_ref[rows, :]
+        for pair in (0, 1):
+            cols = slice(128 * pair, 128 * pair + 128)
+            for base, out in ((0, q_ref), (256, k_ref)):
+                x = proj[:, base + 128 * pair : base + 128 * pair + 128]
+                out[rows, cols] = (x * cos_t + swap_halves(x) * sin_t).astype(jnp.bfloat16)
+        v_ref[rows, :] = proj[:, 512:768].astype(jnp.bfloat16)
+
+    for s in (0, 1):
+        group.relay(3, s)
+
+    @pl.loop(0, 4)
+    def _(t):
+        start = pl.multiple_of(t * 256, 256)
+        rows = pl.ds(start, 256)
+        columns = tab_all[pl.ds(2 * t, 2)].reshape(256, 128)
+        seg_q, var_q = columns[:, 64:65], columns[:, 65:66]
+        code_k, var_k = rows_ref[0:1, :], rows_ref[1:2, :]
+        row = start + lax.broadcasted_iota(jnp.int32, (256, 1024), 0)
+        col = lax.broadcasted_iota(jnp.int32, (256, 1024), 1)
+        allowed = ((seg_q == code_k) & (jnp.abs(row - col) <= WINDOW)) | (row == col)
+        masked = jnp.where(allowed, 0.0, NEGATIVE)
+        same = jnp.where(var_q == var_k, 1.0, 0.0)
+        stats = jnp.zeros((256, 128), jnp.float32)
+        lane = lax.broadcasted_iota(jnp.int32, (256, 128), 1)
+        for h in range(4):
+            cols = slice(64 * h, 64 * h + 64)
+            scores = dot(q_ref[rows, cols] * 0.125, k_ref[:, cols], NT)
+            scores = scores + bias[h] * same + masked
+            top = jnp.max(scores, axis=1, keepdims=True)
+            weight = jnp.exp(scores - top)
+            total = jnp.sum(weight, axis=1, keepdims=True)
+            mixed = dot(weight.astype(jnp.bfloat16), v_ref[:, cols])
+            o_ref[rows, cols] = (mixed / total).astype(jnp.bfloat16)
+            stats = jnp.where(lane == h, top + jnp.log(total), stats)
+        lse_ref[:, rows] = stats.T[:8]
+        part[pl.ds(2 * t, 2)] = dot(o_ref[rows, :], wm_ref[...], out=jnp.bfloat16).reshape(2, 128, 1024)
+
+    branch.start(0)
+    for dz in (1, 2, 3):
+        ffn_w.forward(0, dz)
+    for s in (0, 1):
+        branch.cross(0, s)
+    for s in (0, 1):
+        block = owned(i, s)
+        mid = tok_all[block].astype(jnp.float32) + branch.total(0, s)
+        mid_ref[s] = mid
+        a2_all[block] = (mid * norm_rows(mid) * gain_two[...]).astype(jnp.bfloat16)
+        second.push(0, s)
+    for dz in (1, 2, 3):
+        ffn_w.forward(1, dz)
+    for s in (0, 1):
+        second.relay(0, s)
+    branch.finish(0)
+    second.finish(0)
+    group.finish(3)
+    home.finish(3)
+    for dz in (1, 2, 3):
+        ffn_w.forward(2, dz)
+    for chunk in range(3):
+        ffn_w.finish(chunk)
+
+
+def open_phase(arrays):
+    f32_rows = pltpu.VMEM((1024, 128), jnp.float32)
+    return pl.pallas_call(
+        open_kernel,
+        out_shape=[
+            bf16(8, 128, 1024),
+            bf16(8, 128, 1024),
+            f32(8, 128, 128),
+            f32(8, 8, 128),
+            bf16(1024, 1024),
+            bf16(1024, 256),
+            bf16(1024, 256),
+            bf16(1024, 256),
+            bf16(1024, 256),
+            f32(8, 1024),
+            bf16(1024, 768),
+            bf16(256, 1024),
+            f32(2, 128, 1024),
+            bf16(8, 128, 1024),
+            bf16(8, 3072, 128),
+        ],
+        in_specs=[VM, HB, VM, VM, VM, VM, HB, HB, HB, VM, VM, SM],
+        out_specs=[VM, HB] + [VM] * 12 + [HB],
+        scratch_shapes=[
+            pltpu.VMEM((8, 1280, 128), jnp.bfloat16),
+            pltpu.VMEM((8, 128, 1024), jnp.bfloat16),
+            f32_rows,
+            f32_rows,
+            pltpu.VMEM((8, 1024), jnp.float32),
+        ]
+        + Home.sems(4)
+        + GroupGather.sems(4)
+        + GroupGather.sems(1)
+        + GroupSum.scratch(1)
+        + Exchange.sems(2)
+        + Exchange.sems(4)
+        + SeqGather.sems(1)
+        + SeqGather.sems(3),
+        compiler_params=pltpu.CompilerParams(
+            collective_id=1, has_side_effects=True, vmem_limit_bytes=56 << 20
+        ),
+        name="open_phase",
+    )(*arrays)
 
 
 def comm_call(kernel, outs, scratch, collective_id, in_count, vmem=None):
@@ -404,38 +1013,6 @@
             collective_id=collective_id, has_side_effects=True, vmem_limit_bytes=vmem
         ),
     )
-
-
-def bf16(*shape):
-    return jax.ShapeDtypeStruct(shape, jnp.bfloat16)
-
-
-def f32(*shape):
-    return jax.ShapeDtypeStruct(shape, jnp.float32)
-
-
-def weight_pieces(kind, refs, dst, me, other, seq):
-    if kind == "attention":
-        w_qkv, w_out = refs
-        place = lax.rem(other + 2 * lax.rem(seq, 2), 4)
-        return [
-            (w_qkv.at[place], dst.at[pl.ds(256 * me, 256)]),
-            (w_out.at[pl.ds(64 * other, 64)], dst.at[pl.ds(1024 + 64 * me, 64)]),
-        ]
-    w_gate, w_up, w_down = refs
-    columns = pl.ds(pl.multiple_of(128 * other, 128), 128)
-    pairs = [
-        (w_gate.at[:, columns], dst.at[pl.ds(256 * me, 256)]),
-        (w_up.at[:, columns], dst.at[pl.ds(1024 + 256 * me, 256)]),
-    ]
-    for half in (0, 1):
-        pairs.append(
-            (
-                w_down.at[pl.ds(512 * half + 128 * other, 128)],
-                dst.at[pl.ds(2048 + 256 * me + 128 * half, 128)],
-            )
-        )
-    return pairs
 
 
 def grad_pieces(kind, src, dst, me, other, seq):
@@ -495,104 +1072,17 @@
     )(*ins)
 
 
-def home_meet(peers):
-    i, j = lax.axis_index("dp"), lax.axis_index("seq")
-    target, stays = j // 2, j // 2 == i
-    barrier = pltpu.get_barrier_semaphore()
-    for peer in peers:
-        pl.semaphore_signal(barrier, inc=1, device_id=peer, device_id_type=MESH)
-    for s in (0, 1):
-
-        @pl.when(jnp.logical_not(stays & (2 * i + s == j)))
-        def _():
-            pl.semaphore_signal(
-                barrier, inc=1, device_id=at(target, 2 * i + s), device_id_type=MESH
-            )
-
-    pl.semaphore_wait(barrier, len(peers) + jnp.where(stays, 1, 2))
-
-
-def home_start(ins, outs, send_sem, recv_sem):
-    i, j = lax.axis_index("dp"), lax.axis_index("seq")
-    target, stays = j // 2, j // 2 == i
-    slot = lax.rem(j, 2)
-    for a in range(len(ins)):
-        for s in (0, 1):
-            here = stays & (2 * i + s == j)
-
-            @pl.when(jnp.logical_not(here))
-            def _():
-                send(
-                    ins[a].at[s],
-                    outs[a].at[slot],
-                    send_sem.at[a, s],
-                    recv_sem.at[a, slot],
-                    at(target, 2 * i + s),
-                ).start()
-
-            @pl.when(here)
-            def _():
-                pltpu.make_async_copy(ins[a].at[s], outs[a].at[slot], recv_sem.at[a, slot]).start()
-
-
-def home_finish(ins, outs, send_sem, recv_sem):
-    i, j = lax.axis_index("dp"), lax.axis_index("seq")
-    stays = j // 2 == i
-    for a in range(len(ins)):
-        for s in (0, 1):
-            pltpu.make_async_copy(ins[a].at[s], outs[a].at[s], recv_sem.at[a, s]).wait()
-
-            @pl.when(jnp.logical_not(stays & (2 * i + s == j)))
-            def _():
-                pltpu.make_async_copy(ins[a].at[s], outs[a].at[s], send_sem.at[a, s]).wait()
-
-
 def home_kernel(count, *refs):
     ins, outs = refs[:count], refs[count : 2 * count]
-    send_sem, recv_sem = refs[2 * count :]
-    home_meet([])
-    home_start(ins, outs, send_sem, recv_sem)
-    home_finish(ins, outs, send_sem, recv_sem)
-
-
-def front_kernel(*refs):
-    (tok, cot, ids, packed, w_out, w_gate, w_up, w_down), refs = refs[:8], refs[8:]
-    (tok_o, cot_o, ids_o, attn_o, ffn_o), refs = refs[:5], refs[5:]
-    h_send, h_recv, a_send, a_recv, a_own, f_send, f_recv, f_own = refs
-    i, j = lax.axis_index("dp"), lax.axis_index("seq")
-    others = [lax.rem(i + step, 4) for step in (1, 2, 3)]
-    home_meet([at(other, j) for other in others])
-    home_start((tok, cot, ids), (tok_o, cot_o, ids_o), h_send, h_recv)
-    copies = []
-    for kind, ins, out, sems in (
-        ("attention", (packed, w_out), attn_o, (a_send, a_recv, a_own)),
-        ("ffn", (w_gate, w_up, w_down), ffn_o, (f_send, f_recv, f_own)),
-    ):
-        for step, other in enumerate(others):
-            for index, (src, dst) in enumerate(weight_pieces(kind, ins, out, i, other, j)):
-                copy = send(
-                    src, dst, sems[0].at[step, index], sems[1].at[step, index], at(other, j)
-                )
-                copy.start()
-                copies.append(copy)
-        for index, (src, dst) in enumerate(weight_pieces(kind, ins, out, i, i, j)):
-            copy = pltpu.make_async_copy(src, dst, sems[2].at[index])
-            copy.start()
-            copies.append(copy)
-    for copy in copies:
-        copy.wait()
-    home_finish((tok, cot, ids), (tok_o, cot_o, ids_o), h_send, h_recv)
-
-
-def front(arrays, collective_id):
-    return comm_call(
-        front_kernel,
-        [jax.ShapeDtypeStruct(v.shape, v.dtype) for v in arrays[:3]]
-        + [bf16(1280, 128), bf16(3072, 128)],
-        [DMA((3, 2)), DMA((3, 2)), DMA((3, 2)), DMA((3, 2)), DMA((2,)), DMA((3, 4)), DMA((3, 4)), DMA((4,))],
-        collective_id,
-        8,
-    )(*arrays)
+    home = Home(ins, outs, refs[2 * count :], True)
+    meet([], home=True)
+    for a in range(count):
+        for s in (0, 1):
+            home.start(a, s)
+    for a in range(count):
+        for s in (0, 1):
+            home.wait(a, s)
+        home.finish(a)
 
 
 def send_home(arrays, collective_id):
@@ -600,10 +1090,21 @@
     return comm_call(
         functools.partial(home_kernel, count),
         [jax.ShapeDtypeStruct(v.shape, v.dtype) for v in arrays],
-        [DMA((count, 2)), DMA((count, 2))],
+        Home.sems(count),
         collective_id,
         count,
     )(*arrays)
+
+
+def local_call(kernel, outs, scratch, specs, vmem):
+    return pl.pallas_call(
+        kernel,
+        out_shape=outs,
+        in_specs=specs,
+        out_specs=[VM] * len(outs),
+        scratch_shapes=scratch,
+        compiler_params=pltpu.CompilerParams(vmem_limit_bytes=vmem),
+    )
 
 
 def gather_kernel(count, *refs):
@@ -619,28 +1120,28 @@
             for sems, peer in (((s_x, r_x), across), ((s_core, r_core), core)):
                 copy = send(
                     ins[a].at[s],
-                    outs[a].at[2 * i + s],
+                    outs[a].at[owned(i, s)],
                     sems[0].at[a, s],
                     sems[1].at[a, s],
                     at(peer, j),
                 )
                 copy.start()
                 pending.append(copy)
-            copy = pltpu.make_async_copy(ins[a].at[s], outs[a].at[2 * i + s], own_sem.at[a, s])
+            copy = pltpu.make_async_copy(ins[a].at[s], outs[a].at[owned(i, s)], own_sem.at[a, s])
             copy.start()
             pending.append(copy)
     onward = []
     for a in range(count):
         for s in (0, 1):
-            block = outs[a].at[2 * across + s]
+            block = outs[a].at[owned(across, s)]
             pltpu.make_async_copy(ins[a].at[s], block, r_x.at[a, s]).wait()
             copy = send(block, block, s_on.at[a, s], r_on.at[a, s], at(core, j))
             copy.start()
             onward.append(copy)
     for a in range(count):
         for s in (0, 1):
-            pltpu.make_async_copy(ins[a].at[s], outs[a].at[2 * core + s], r_core.at[a, s]).wait()
-            pltpu.make_async_copy(ins[a].at[s], outs[a].at[2 * diagonal + s], r_on.at[a, s]).wait()
+            pltpu.make_async_copy(ins[a].at[s], outs[a].at[owned(core, s)], r_core.at[a, s]).wait()
+            pltpu.make_async_copy(ins[a].at[s], outs[a].at[owned(diagonal, s)], r_on.at[a, s]).wait()
     for index, copy in enumerate(pending):
         if index % 3 == 2:
             copy.wait()
@@ -673,7 +1174,7 @@
         for side, owner in ((0, diagonal), (1, core)):
             for s in (0, 1):
                 copy = send(
-                    ins[a].at[2 * owner + s],
+                    ins[a].at[owned(owner, s)],
                     from_core.at[a, side, s],
                     s_core.at[a, side, s],
                     r_core.at[a, side, s],
@@ -687,7 +1188,7 @@
             pltpu.make_async_copy(
                 ins[a].at[s], from_core.at[a, 0, s], r_core.at[a, 0, s]
             ).wait()
-            both = ins[a][2 * across + s].astype(jnp.float32) + from_core[a, 0, s].astype(
+            both = ins[a][owned(across, s)].astype(jnp.float32) + from_core[a, 0, s].astype(
                 jnp.float32
             )
             to_x[a, s] = both.astype(jnp.bfloat16)
@@ -701,7 +1202,7 @@
             pltpu.make_async_copy(
                 ins[a].at[s], from_core.at[a, 1, s], r_core.at[a, 1, s]
             ).wait()
-            outs[a][s] = ins[a][2 * i + s].astype(jnp.float32) + from_core[a, 1, s].astype(
+            outs[a][s] = ins[a][owned(i, s)].astype(jnp.float32) + from_core[a, 1, s].astype(
                 jnp.float32
             )
     for a in range(count):
@@ -777,56 +1278,103 @@
     )(x)[0]
 
 
-NT = (((1,), (1,)), ((), ()))
-TN = (((0,), (0,)), ((), ()))
-
-
-def swap_halves(x):
-    lane = lax.broadcasted_iota(jnp.int32, x.shape, 1)
-    width = x.shape[1]
-    return jnp.where(lane % 64 < 32, pltpu.roll(x, width - 32, 1), pltpu.roll(x, 32, 1))
-
-
-def attention_kernel(p_ref, cos_ref, sin_ref, idc_ref, idr_ref, bias_ref, q_ref, k_ref, v_ref, o_ref, lse_ref):
+def wide(ref, first, rows):
+    return jnp.concatenate([ref[first, rows, :], ref[first + 1, rows, :]], axis=1)
+
+
+def store_wide(ref, first, rows, value):
+    ref[first, rows, :] = value[:, :128]
+    ref[first + 1, rows, :] = value[:, 128:]
+
+
+def ffn_kernel(
+    a_ref, g_ref, wg_ref, wu_ref, wd_ref,
+    da_ref, out_ref, gg_ref, gu_ref, gd_ref,
+    turned, da_acc, out_acc, hidden_s, dgate_s, dup_s,
+):
+    step, last = pl.program_id(0), pl.num_programs(0) - 1
+
+    @pl.when(step == 0)
+    def _():
+        @pl.loop(0, 4)
+        def _(t):
+            rows = pl.ds(pl.multiple_of(t * 256, 256), 256)
+            for d in range(4):
+                cols = slice(256 * d, 256 * d + 256)
+                turned[cols, rows] = a_ref[rows, cols].T
+
+    wg, wu = wide(wg_ref, 0, EVERY), wide(wu_ref, 0, EVERY)
+    wd = jnp.concatenate([wd_ref[b] for b in range(8)], axis=1)
+
     @pl.loop(0, 4)
-    def _(block):
-        rows = pl.ds(block * 256, 256)
-        cos_t, sin_t = cos_ref[rows, :], sin_ref[rows, :]
-        for pair in (0, 1):
-            cols = slice(128 * pair, 128 * pair + 128)
-            for base, out in ((0, q_ref), (256, k_ref)):
-                x = p_ref[rows, base + 128 * pair : base + 128 * pair + 128]
-                out[rows, cols] = (x * cos_t + swap_halves(x) * sin_t).astype(jnp.bfloat16)
-        v_ref[rows, :] = p_ref[rows, 512:768].astype(jnp.bfloat16)
+    def _(t):
+        rows = pl.ds(pl.multiple_of(t * 256, 256), 256)
+        a, g = a_ref[rows, :], g_ref[rows, :]
+        gate, up, dh = dot(a, wg), dot(a, wu), dot(g, wd, NT)
+        sig = 1.0 / (1.0 + jnp.exp(-gate))
+        gate_sig = gate * sig
+        hidden = (gate_sig * up).astype(jnp.bfloat16)
+        dgate = (dh * up * (sig + gate_sig * (1.0 - sig))).astype(jnp.bfloat16)
+        dup = (dh * gate_sig).astype(jnp.bfloat16)
+        hidden_s[rows, :] = hidden
+        dgate_s[rows, :] = dgate
+        dup_s[rows, :] = dup
+        da = dot(dgate, wg, NT) + dot(dup, wu, NT)
+        out = dot(hidden, wd)
+
+        @pl.when(step == 0)
+        def _():
+            da_acc[rows, :] = da
+            out_acc[rows, :] = out
+
+        @pl.when(step > 0)
+        def _():
+            da_acc[rows, :] += da
+            out_acc[rows, :] += out
 
     @pl.loop(0, 4)
-    def _(block):
-        start = block * 256
-        rows = pl.ds(start, 256)
-        seg_q, var_q = idc_ref[rows, 0:1], idc_ref[rows, 1:2]
-        code_k, var_k = idr_ref[0:1, :], idr_ref[1:2, :]
-        row = start + lax.broadcasted_iota(jnp.int32, (256, 1024), 0)
-        col = lax.broadcasted_iota(jnp.int32, (256, 1024), 1)
-        allowed = ((seg_q == code_k) & (jnp.abs(row - col) <= WINDOW)) | (row == col)
-        masked = jnp.where(allowed, 0.0, NEGATIVE)
-        same = jnp.where(var_q == var_k, 1.0, 0.0)
-        stats = jnp.zeros((256, 128), jnp.float32)
-        lane = lax.broadcasted_iota(jnp.int32, (256, 128), 1)
-        for h in range(4):
-            cols = slice(64 * h, 64 * h + 64)
-            scores = lax.dot_general(
-                q_ref[rows, cols] * 0.125, k_ref[:, cols], NT, preferred_element_type=jnp.float32
-            )
-            scores = scores + bias_ref[h] * same + masked
-            top = jnp.max(scores, axis=1, keepdims=True)
-            weight = jnp.exp(scores - top)
-            total = jnp.sum(weight, axis=1, keepdims=True)
-            mixed = jnp.dot(
-                weight.astype(jnp.bfloat16), v_ref[:, cols], preferred_element_type=jnp.float32
-            )
-            o_ref[rows, cols] = (mixed / total).astype(jnp.bfloat16)
-            stats = jnp.where(lane == h, top + jnp.log(total), stats)
-        lse_ref[rows, :] = stats
+    def _(d):
+        rows = pl.ds(pl.multiple_of(d * 256, 256), 256)
+        a_t = turned[rows, :]
+        store_wide(gg_ref, 0, rows, dot(a_t, dgate_s[...], out=jnp.bfloat16))
+        store_wide(gu_ref, 0, rows, dot(a_t, dup_s[...], out=jnp.bfloat16))
+
+    h_t = hidden_s[...].T
+    for d in range(4):
+        store_wide(gd_ref, 2 * d, EVERY, dot(h_t, g_ref[:, 256 * d : 256 * d + 256], out=jnp.bfloat16))
+
+    @pl.when(step == last)
+    def _():
+        da_ref[...] = da_acc[...].astype(jnp.bfloat16)
+        out_ref[...] = out_acc[...].astype(jnp.bfloat16)
+
+
+def ffn(a2, g_low, weights):
+    tile = (2, 1024, 128)
+    grads = [
+        pl.BlockSpec(tile, lambda f: (f, 0, 0)),
+        pl.BlockSpec(tile, lambda f: (f, 0, 0)),
+        pl.BlockSpec((8, 256, 128), lambda f: (0, f, 0)),
+    ]
+    whole = pl.BlockSpec((1024, 1024), lambda f: (0, 0))
+    return pl.pallas_call(
+        ffn_kernel,
+        grid=(4,),
+        out_shape=[bf16(1024, 1024)] * 2 + [bf16(8, 1024, 128)] * 3,
+        in_specs=[
+            whole,
+            whole,
+            pl.BlockSpec(tile, lambda f: (f, 0, 0)),
+            pl.BlockSpec(tile, lambda f: (f, 1, 0)),
+            pl.BlockSpec((8, 256, 128), lambda f: (0, 8 + f, 0)),
+        ],
+        out_specs=[whole, whole] + grads,
+        scratch_shapes=[pltpu.VMEM((1024, 1024), jnp.bfloat16)]
+        + [pltpu.VMEM((1024, 1024), jnp.float32)] * 2
+        + [pltpu.VMEM((1024, 256), jnp.bfloat16)] * 3,
+        compiler_params=pltpu.CompilerParams(vmem_limit_bytes=52 << 20),
+        name="ffn",
+    )(a2, g_low, weights, weights, weights)
 
 
 def attention_back_kernel(
@@ -883,128 +1431,6 @@
         dqkv_ref[rows, 512:768] = dv_acc[rows, :].astype(jnp.bfloat16)
 
 
-def local_call(kernel, outs, scratch, specs, vmem):
-    return pl.pallas_call(
-        kernel,
-        out_shape=outs,
-        in_specs=specs,
-        out_specs=[VM] * len(outs),
-        scratch_shapes=scratch,
-        compiler_params=pltpu.CompilerParams(vmem_limit_bytes=vmem),
-    )
-
-
-SM = pl.BlockSpec(memory_space=pltpu.SMEM)
-
-
-def wide(ref, first, rows):
-    return jnp.concatenate([ref[first, rows, :], ref[first + 1, rows, :]], axis=1)
-
-
-def store_wide(ref, first, rows, value):
-    ref[first, rows, :] = value[:, :128]
-    ref[first + 1, rows, :] = value[:, 128:]
-
-
-EVERY = slice(None)
-
-
-def ffn_kernel(
-    a_ref, g_ref, wg_ref, wu_ref, wd_ref,
-    da_ref, out_ref, gg_ref, gu_ref, gd_ref,
-    turned, da_acc, out_acc, hidden_s, dgate_s, dup_s,
-):
-    step, last = pl.program_id(0), pl.num_programs(0) - 1
-
-    @pl.when(step == 0)
-    def _():
-        @pl.loop(0, 4)
-        def _(t):
-            rows = pl.ds(pl.multiple_of(t * 256, 256), 256)
-            for d in range(4):
-                cols = slice(256 * d, 256 * d + 256)
-                turned[cols, rows] = a_ref[rows, cols].T
-
-    wg, wu = wide(wg_ref, 0, EVERY), wide(wu_ref, 0, EVERY)
-    wd = jnp.concatenate([wd_ref[b] for b in range(8)], axis=1)
-
-    @pl.loop(0, 4)
-    def _(t):
-        rows = pl.ds(pl.multiple_of(t * 256, 256), 256)
-        a, g = a_ref[rows, :], g_ref[rows, :]
-        gate, up, dh = dot(a, wg), dot(a, wu), dot(g, wd, NT)
-        sig = 1.0 / (1.0 + jnp.exp(-gate))
-        gate_sig = gate * sig
-        hidden = (gate_sig * up).astype(jnp.bfloat16)
-        dgate = (dh * up * (sig + gate_sig * (1.0 - sig))).astype(jnp.bfloat16)
-        dup = (dh * gate_sig).astype(jnp.bfloat16)
-        hidden_s[rows, :] = hidden
-        dgate_s[rows, :] = dgate
-        dup_s[rows, :] = dup
-        da = dot(dgate, wg, NT) + dot(dup, wu, NT)
-        out = dot(hidden, wd)
-
-        @pl.when(step == 0)
-        def _():
-            da_acc[rows, :] = da
-            out_acc[rows, :] = out
-
-        @pl.when(step > 0)
-        def _():
-            da_acc[rows, :] += da
-            out_acc[rows, :] += out
-
-    @pl.loop(0, 4)
-    def _(d):
-        rows = pl.ds(pl.multiple_of(d * 256, 256), 256)
-        a_t = turned[rows, :]
-        store_wide(gg_ref, 0, rows, dot(a_t, dgate_s[...], out=jnp.bfloat16))
-        store_wide(gu_ref, 0, rows, dot(a_t, dup_s[...], out=jnp.bfloat16))
-
-    h_t = hidden_s[...].T
-    for d in range(4):
-        store_wide(gd_ref, 2 * d, EVERY, dot(h_t, g_ref[:, 256 * d : 256 * d + 256], out=jnp.bfloat16))
-
-    @pl.when(step == last)
-    def _():
-        da_ref[...] = da_acc[...].astype(jnp.bfloat16)
-        out_ref[...] = out_acc[...].astype(jnp.bfloat16)
-
-
-def ffn(a2, g_low, weights):
-    tile = (2, 1024, 128)
-    grads = [
-        pl.BlockSpec(tile, lambda f: (f, 0, 0)),
-        pl.BlockSpec(tile, lambda f: (f, 0, 0)),
-        pl.BlockSpec((8, 256, 128), lambda f: (0, f, 0)),
-    ]
-    whole = pl.BlockSpec((1024, 1024), lambda f: (0, 0))
-    return pl.pallas_call(
-        ffn_kernel,
-        grid=(4,),
-        out_shape=[bf16(1024, 1024)] * 2 + [bf16(8, 1024, 128)] * 3,
-        in_specs=[
-            whole,
-            whole,
-            pl.BlockSpec(tile, lambda f: (f, 0, 0)),
-            pl.BlockSpec(tile, lambda f: (f, 1, 0)),
-            pl.BlockSpec((8, 256, 128), lambda f: (0, 8 + f, 0)),
-        ],
-        out_specs=[whole, whole] + grads,
-        scratch_shapes=[pltpu.VMEM((1024, 1024), jnp.bfloat16)]
-        + [pltpu.VMEM((1024, 1024), jnp.float32)] * 2
-        + [pltpu.VMEM((1024, 256), jnp.bfloat16)] * 3,
-        compiler_params=pltpu.CompilerParams(vmem_limit_bytes=52 << 20),
-        name="ffn",
-    )(a2, g_low, weights, weights, weights)
-
-
-def attention(proj, cos_t, sin_t, id_cols, id_rows, bias):
-    return local_call(
-        attention_kernel, [bf16(1024, 256)] * 4 + [f32(1024, 128)], [], [VM] * 5 + [SM], 48 << 20
-    )(proj, cos_t, sin_t, id_cols, id_rows, bias)
-
-
 def attention_back(q, k, v, do, lse, cos_t, sin_t, id_cols, id_rows, bias):
     return local_call(
         attention_back_kernel,
@@ -1015,17 +1441,6 @@
     )(q, k, v, do, lse, cos_t, sin_t, id_cols, id_rows, bias)
 
 
-SLOTS = (
-    (0, 1, 2, 4, 5, 6, 8, 9, 10, 12, 13, 14),
-    (0, 2, 3, 4, 6, 7, 8, 10, 11, 12, 14, 15),
-)
-
-
-def dot(a, b, dims=None, out=jnp.float32):
-    dims = (((1,), (0,)), ((), ())) if dims is None else dims
-    return lax.dot_general(a, b, dims, preferred_element_type=jnp.float32).astype(out)
-
-
 def on_group(
     tokens, segment_ids, variate_ids, time_ids, pad_mask, cotangent,
     w_qkv, w_out, w_gate, w_up, w_down, gain_attn, gain_ffn, variate_bias,
@@ -1036,57 +1451,43 @@
 
     packed = jnp.pad(w_qkv, ((0, 0), (0, 128))).reshape(256, 2, 4, 64)
     packed = packed.transpose(2, 0, 1, 3).reshape(4, 256, 128)
-    ids = jnp.stack([segment_ids, variate_ids, time_ids, pad_mask], axis=1)
-    ids = jnp.pad(ids, ((0, 0), (0, 4), (0, 0)))
-    own_tok, own_cot, own_ids, attn_block, ffn_block = front(
-        [tokens, cotangent, ids, packed, w_out, w_gate, w_up, w_down], 1
-    )
-    attn_w = lax.all_gather(attn_block, "seq")
-    ffn_w = lax.all_gather(ffn_block, "seq")
-    all_tok, all_cot, all_ids = gather_group([own_tok, own_cot, own_ids], 4)
-    all_tok = all_tok.reshape(1024, 1024)
-    g_low = all_cot.reshape(1024, 1024)
-    id_seq = all_ids.transpose(1, 0, 2).reshape(8, 1024)
-    seg, var, time, pad = id_seq[0], id_seq[1], id_seq[2], id_seq[3]
-    code = jnp.where(pad == 1, seg, -1)
-    id_rows = jnp.stack([code, var, seg] + [seg] * 5)
-    id_cols = jnp.pad(jnp.stack([seg, var, code], axis=1), ((0, 0), (0, 125)))
     frequency = jnp.exp(-jnp.log(10000.0) * jnp.arange(32, dtype=jnp.float32) / 32)
-    angles = time.astype(jnp.float32)[:, None] * frequency[None, :]
-    cos_h, sin_h = jnp.cos(angles), jnp.sin(angles)
-    cos_t = jnp.concatenate([cos_h] * 4, axis=1)
-    sin_t = jnp.concatenate([-sin_h, sin_h] * 2, axis=1)
+    angles = time_ids.astype(jnp.float32)[..., None] * frequency
+    code_ids = jnp.where(pad_mask == 1, segment_ids, -1)
+    labels = jnp.stack([segment_ids, variate_ids, code_ids], axis=-1).astype(jnp.float32)
+    tables = jnp.concatenate(
+        [jnp.cos(angles), jnp.sin(angles), labels, jnp.zeros((2, 128, 61), jnp.float32)], axis=-1
+    )
+    label_rows = jnp.stack([code_ids, variate_ids, segment_ids] + [segment_ids] * 5, axis=1)
     bias = jnp.where(
         jnp.arange(4)[None, :] == i, variate_bias.astype(jnp.float32).reshape(4, 4), 0.0
     ).sum(axis=1)
-
-    resid = all_tok.astype(jnp.float32)
-    a1 = (resid * norm_scale(resid) * gain_one).astype(jnp.bfloat16)
-
-    slots = attn_w[:, :1024].reshape(8, 1024, 2, 64)
-
-    def column(m):
-        first, second = SLOTS[0][m], SLOTS[1][m]
-        return jnp.where(
-            low_half, slots[first // 2, :, first % 2], slots[second // 2, :, second % 2]
-        )
-
-    w_heads = jnp.concatenate([column(m) for m in range(12)], axis=1)
-    w_mix = attn_w[:, 1024:].transpose(1, 0, 2).reshape(256, 1024)
-    proj = dot(a1, w_heads)
-    q, k, v, attended, lse = attention(proj, cos_t, sin_t, id_cols, id_rows, bias)
-    lse_rows = lse[:, :8].T
-    part = dot(attended, w_mix, out=jnp.bfloat16).reshape(8, 128, 1024)
-    (branch,) = reduce_group([part], 5)
-
-    own = own_tok.reshape(256, 1024).astype(jnp.float32)
+    (
+        tok_all, cot_all, tab_all, idr_all, a1, q, k, v, attended, lse_rows,
+        w_heads, w_mix, mid, a2, ffn_w,
+    ) = open_phase(
+        [
+            tokens, cotangent, tables, label_rows.astype(jnp.float32), packed, w_out, w_gate, w_up, w_down,
+            gain_one[None], gain_two[None], bias,
+        ]
+    )
+    g_low = cot_all.reshape(1024, 1024)
+    a2 = a2.reshape(1024, 1024)
+    mid = mid.reshape(256, 1024)
+    inv_two = norm_scale(mid)
+
+    def mine(blocks):
+        return jnp.concatenate(
+            [lax.dynamic_index_in_dim(blocks, owned(i, s), 0, False) for s in (0, 1)]
+        ).astype(jnp.float32)
+
+    own, own_cot = mine(tok_all), mine(cot_all)
     inv_one = norm_scale(own)
-    mid = own + branch.reshape(256, 1024)
-    inv_two = norm_scale(mid)
-    a2_own = (mid * inv_two * gain_two).astype(jnp.bfloat16)
-    (a2,) = gather_group([a2_own.reshape(2, 128, 1024)], 6)
-    a2 = a2.reshape(1024, 1024)
-
+    table = tab_all.reshape(1024, 128)
+    cos_t = jnp.concatenate([table[:, :32]] * 4, axis=1)
+    sin_t = jnp.concatenate([-table[:, 32:64], table[:, 32:64]] * 2, axis=1)
+    id_cols = jnp.pad(table[:, 64:67], ((0, 0), (0, 125)))
+    id_rows = idr_all.transpose(1, 0, 2).reshape(8, 1024)
     da2_part, out_part, g_gate, g_up, g_down = ffn(a2, g_low, ffn_w)
     ffn_grads = jnp.concatenate([g_gate, g_up, g_down], axis=1)
     ffn_sum = lax.psum_scatter(ffn_grads, "seq", scatter_dimension=0)
@@ -1098,7 +1499,6 @@
     da2 = da2.reshape(256, 1024)
     output = (mid + ffn_out.reshape(256, 1024)).astype(jnp.bfloat16)
     grad_gain_two = jnp.sum(da2 * mid * inv_two, axis=0)
-    own_cot = own_cot.reshape(256, 1024).astype(jnp.float32)
     e2 = own_cot + norm_back(da2 * gain_two, mid, inv_two)
     (ez,) = gather_group([e2.astype(jnp.bfloat16).reshape(2, 128, 1024)], 8)
     ez = ez.reshape(1024, 1024)

time: 593 us -> 575 us (0.970)
  Pallas kernels: 328 us -> 374 us
  waiting for transfers between devices: 159 us -> 119 us
  local copies, waits for them, and re-layouts: 33.4 us -> 22.6 us
  other arithmetic: 41.8 us -> 33.8 us
    pallas_call x2 -> x1, Pallas kernels: 42.1 us -> 173 us  [open_phase(): pl.pallas_call(open_kernel, out_shape=[bf16(8, 128, 1024), bf16(8, 128, 1...]
    pallas_call x3 -> x1, Pallas kernels: 93.8 us -> 18.3 us  [gather_group(): comm_call(functools.partial(gather_kernel, count), [jax.ShapeDtypeStruct(...]
    all_gather x2 -> x0, waiting for transfers between devices: 31.4 us -> none  [the longest x1 17.7 us: on_group(): ffn_w = lax.all_gather(ffn_block, 'seq')]
    pallas_call x3 -> x2, Pallas kernels: 68.1 us -> 47.6 us  [reduce_group(): comm_call(functools.partial(reduce_kernel, count), [f32(2, rows, width) f...]
    reduce_scatter x1, waiting for transfers between devices: 26.1 us -> 8.12 us  [on_group(): attn_sum = lax.psum_scatter(attn_grads, 'seq', scatter_dimension=0)]
    pallas_call x1, Pallas kernels: 10.4 us -> 28.1 us  [small_sum(): comm_call(small_sum_kernel, [jax.ShapeDtypeStruct(x.shape, x.dtype)], [pl...]
    pallas_call x2, Pallas kernels: 33.9 us -> 19.9 us  [exchange(): comm_call(kernel, outs, [DMA((3, count)), DMA((3, count)), DMA((count,))]...]
    unnamed x102 -> x92, local copies, waits for them, and re-layouts: 21.9 us -> 11.1 us
  transfers between devices with their start and end apart: 4 -> 2, of which waited for: 4 -> 2; matrix products, arithmetic and copies ran while one was open for 9% -> 3% of each run, Pallas kernels for 30% -> 13%
where the time goes in v2:
time: 575 us; the launch traced here: 573 us
  Pallas kernels  374 us (65%)
  waiting for transfers between devices  119 us (21%)
  other arithmetic  33.8 us (6%)
  local copies, waits for them, and re-layouts  22.6 us (4%)
  between operations  14.8 us (3%)
  matrix products  9.65 us (2%)
    pallas_call x1, Pallas kernels, open_phase(): pl.pallas_call(open_kernel, out_shape=[bf16(8, 128, 1024), bf16(8, 128, 1...  173 us
    reduce_scatter x1, waiting for transfers between devices, on_group(): ffn_sum = lax.psum_scatter(ffn_grads, 'seq', scatter_dimension=0)  111 us
    pallas_call x2, Pallas kernels, reduce_group(): comm_call(functools.partial(reduce_kernel, count), [f32(2, rows, width) f...  47.6 us
    pallas_call x1, Pallas kernels, ffn(): pl.pallas_call(ffn_kernel, grid=(4,), out_shape=[bf16(1024, 1024)] * 2 +...  42 us
    pallas_call x1, Pallas kernels, small_sum(): comm_call(small_sum_kernel, [jax.ShapeDtypeStruct(x.shape, x.dtype)], [pl...  28.1 us
    pallas_call x1, Pallas kernels, send_home(): comm_call(functools.partial(home_kernel, count), [jax.ShapeDtypeStruct(v....  23.1 us
    pallas_call x1, Pallas kernels, attention_back(): local_call(attention_back_kernel, [bf16(1024, 768), f32(8, 256)], [pltpu....  21.4 us
    pallas_call x2, Pallas kernels, exchange(): comm_call(kernel, outs, [DMA((3, count)), DMA((3, count)), DMA((count,))]...  19.9 us
  transfers between devices with their start and end apart: 2, of which 2 were waited for; matrix products, arithmetic and copies ran while one was open for 3% of the time, Pallas kernels for 13%

profile of v2, /device:TPU:0, one launch (start us, length us, event | category | flops | bytes accessed | tf_op | source)
XLA Modules:
  0.0 573.4 jit_solution(16293048999732156908)
XLA Ops:
  16.4 173.5 %open_phase.1 = (bf16[8,128,1024]{2,1,0:T(8,128)(2,1)}, bf16[8,128,1024]{2,1,0:T(8,128)(2,1)}, f32[8,128,128]{2,1,0:T(8,128)}, f32[8,8,128]{2,1,0:T(8,128)}, bf1...) custom-call(bf16[2,128,1024]{2,1,0:T(8,128)(2,1)} %refs_0_.1, ...), custom_call_target="tpu_custom_call" | custom-call | tf_op jit(solution)/shard_map/open_phase/pallas_call | solution.py:962
  189.9 2.7 slice_negate_fusion
  193.7 42.0 %ffn.1 = (bf16[1024,1024]{1,0:T(8,128)(2,1)}, bf16[1024,1024]{1,0:T(8,128)(2,1)}, bf16[8,1024,128]{2,1,0:T(8,128)(2,1)}, bf16[8,1024,128]{2,1,0:T(8,128)(2,1)}, bf16[8,1024,128]{2,1,0:T(8,128)(2,1)}) custom-call(bf16[1024,1024]{1,0:T(8,128)(2,1)} %bitcast.138, bf16[1024,1024]{1,0:T(8,128)(2,1)} %bitcast.132, ...), custom_call_target="tpu_custom_call" | custom-call | tf_op jit(solution)/shard_map/ffn/pallas_call | solution.py:1360
  235.7 29.1 %shard_map.213 = (f32[2,128,1024]{2,1,0:T(8,128)}, f32[2,128,1024]{2,1,0:T(8,128)}) custom-call(bf16[8,128,1024]{2,1,0:T(8,128)(2,1)} %bitcast.135, bf16[8,128,1024]{2,1,0:T(8,128)(2,1)} %bitcast.136), custom_call_target="tpu_custom_call" | custom-call | tf_op jit(solution)/shard_map/pallas_call | solution.py:1220
  269.1 18.3 %shard_map.214 = bf16[8,128,1024]{2,1,0:T(8,128)(2,1)} custom-call(bf16[2,128,1024]{2,1,0:T(8,128)(2,1)} %fusion.8.refs_0_), custom_call_target="tpu_custom_call" | custom-call | tf_op jit(solution)/shard_map/pallas_call | solution.py:1156
  287.5 2.5 convolution_convert_fusion.3.do_ref
  291.8 2.2 copy.44
  293.9 3.5 pad_maximum_fusion.3
  297.5 21.4 %shard_map.215 = (bf16[1024,768]{1,0:T(8,128)(2,1)S(1)}, f32[8,256]{1,0:T(8,128)S(1)}) custom-call(bf16[1024,256]{1,0:T(8,128)(2,1)S(1)} %copy-done, bf16[1024,256]{1,0:T(8,128)(2,1)S(1)} %copy-done.1, bf16[1024,256]{1,0:T(8,128)(2,1)S(1)} %copy-done.2, bf16[1024,256]{1,0:T(8,128)(2,1)S(1)} %convolution_convert_fusion.3.do_ref, f32[8,1024]{1,0:T(8,128)S(1)} %copy-done.4, ...), custom_call_target="tpu_custom_call" | custom-call | tf_op jit(solution)/shard_map/pallas_call | solution.py:1435
  318.9 1.9 convolution_convert_fusion.1
  326.5 1.7 pad_maximum_fusion.1
  329.8 5.4 pad_maximum_fusion
  336.6 4.6 convolution_convert_fusion
  341.1 18.5 %shard_map.216 = f32[2,128,1024]{2,1,0:T(8,128)} custom-call(bf16[8,128,1024]{2,1,0:T(8,128)(2,1)} %bitcast.134), custom_call_target="tpu_custom_call" | custom-call | tf_op jit(solution)/shard_map/pallas_call | solution.py:1220
  362.1 1.7 add_convert_fusion
  363.7 23.1 %shard_map.217 = (bf16[2,128,1024]{2,1,0:T(8,128)(2,1)}, bf16[2,128,1024]{2,1,0:T(8,128)(2,1)}) custom-call(bf16[2,128,1024]{2,1,0:T(8,128)(2,1)} %get-tuple-element.103.refs_0_, bf16[2,128,1024]{2,1,0:T(8,128)(2,1)} %get-tuple-element.102.refs_1_), custom_call_target="tpu_custom_call" | custom-call | tf_op jit(solution)/shard_map/pallas_call | solution.py:1090
  387.7 28.1 %shard_map.220 = f32[24,128]{1,0:T(8,128)} custom-call(f32[24,128]{1,0:T(8,128)} %pad_maximum_fusion.5.x_ref), custom_call_target="tpu_custom_call" | custom-call | tf_op jit(solution)/shard_map/pallas_call | solution.py:1265
  418.3 8.1 %reduce-scatter.3.cloned.1.call-done = bf16[1,1280,128]{2,1,0:T(8,128)(2,1)} async-done(((bf16[8,1280,128]{2,1,0:T(8,128)(2,1)}), bf16[1,1280,128]{2,1,0:T(8,128)(2,1)}) %reduce-scatter.3.cloned.1.call-update) | async-done | bytes 327696 | tf_op jit(solution)/shard_map/reduce_scatter | solution.py:1534
  426.4 7.1 %shard_map.218 = (bf16[4,256,128]{2,1,0:T(8,128)(2,1)}, bf16[256,128]{1,0:T(8,128)(2,1)}) custom-call(bf16[1280,128]{1,0:T(8,128)(2,1)} %bitcast.149), custom_call_target="tpu_custom_call" | custom-call | tf_op jit(solution)/shard_map/pallas_call | solution.py:1070
  436.4 110.5 %reduce-scatter.5.cloned.1.call-done = bf16[1,3072,128]{2,1,0:T(8,128)(2,1)} async-done(((bf16[8,3072,128]{2,1,0:T(8,128)(2,1)}), bf16[1,3072,128]{2,1,0:T(8,128)(2,1)}) %reduce-scatter.5.cloned.1.call-update) | async-done | bytes 786448 | tf_op jit(solution)/shard_map/reduce_scatter | solution.py:1493
  546.9 12.7 %shard_map.219 = (bf16[256,512]{1,0:T(8,128)(2,1)}, bf16[256,512]{1,0:T(8,128)(2,1)}, bf16[1024,128]{1,0:T(8,128)(2,1)}) custom-call(bf16[3072,128]{1,0:T(8,128)(2,1)} %bitcast.148), custom_call_target="tpu_custom_call" | custom-call | tf_op jit(solution)/shard_map/pallas_call | solution.py:1070
  559.6 1.8 convert_element_type.99
  561.4 1.8 convert_element_type.100
  563.2 1.8 convert_element_type.101
  (156 shorter events, 34.9 us)
Async XLA Ops:
  7.2 5.9 %copy-start.31 = (bf16[1024]{0:T(1024)(128)(2,1)S(1)}, bf16[1024]{0:T(1024)(128)(2,1)}, u32[]{:S(2)}) copy-start(bf16[1024]{0:T(1024)(128)(2,1)} %param.25) | copy-start | bytes 6148
  7.2 6.4 %copy-start.32 = (bf16[1024]{0:T(1024)(128)(2,1)S(1)}, bf16[1024]{0:T(1024)(128)(2,1)}, u32[]{:S(2)}) copy-start(bf16[1024]{0:T(1024)(128)(2,1)} %param.26) | copy-start | bytes 6148
  7.2 7.0 %copy-start.35 = (bf16[16]{0:T(256)(128)(2,1)S(1)}, bf16[16]{0:T(256)(128)(2,1)}, u32[]{:S(2)}) copy-start(bf16[16]{0:T(256)(128)(2,1)} %param.27) | copy-start | bytes 100
  7.2 419.2 %reduce-scatter.3.cloned.1.call-start = ((), (), s32[]{:S(2)}) async-start(), calls=%async_computation.2 | async-start | bytes 2949120 | tf_op jit(solution)/shard_map/reduce_scatter | solution.py:1534
  7.3 9.1 %copy-start.33 = (pred[4]{0:T(512)(128)(4,1)}, pred[4]{0:T(512)(128)(4,1)S(1)}, u32[]{:S(2)}) copy-start(pred[4]{0:T(512)(128)(4,1)S(1)} %iota_compare_fusion) | copy-start | bytes 16
  189.9 3.7 copy-start.8
  193.7 74.1 %copy-start.27 = (f32[2,128]{1,0:T(2,128)}, f32[2,128]{1,0:T(2,128)S(1)}, u32[]{:S(2)}) copy-start(f32[2,128]{1,0:T(2,128)S(1)} %add_rsqrt_fusion) | copy-start | bytes 3076
  235.7 29.1 %copy-start.24 = (f32[1024]{0:T(1024)S(1)}, f32[1024]{0:T(1024)}, u32[]{:S(2)}) copy-start(f32[1024]{0:T(1024)} %convert_element_type.84) | copy-start | bytes 12292
  266.4 2.7 copy-start.29
  267.8 19.6 %copy-start.15 = (bf16[256,1024]{1,0:T(8,128)(2,1)}, bf16[256,1024]{1,0:T(8,128)(2,1)S(1)}, u32[]{:S(2)}) copy-start(bf16[256,1024]{1,0:T(8,128)(2,1)S(1)} %pad_maximum_fusion.2) | copy-start | bytes 1572868
  269.1 18.3 %copy-start.18 = (f32[1024,3]{1,0:T(8,128)S(1)}, f32[1024,3]{1,0:T(8,128)}, u32[]{:S(2)}) copy-start(f32[1024,3]{1,0:T(8,128)} %slice.97) | copy-start | bytes 36868
  269.1 18.3 %copy-start.37 = (bf16[256,1024]{1,0:T(8,128)(2,1)S(1)}, bf16[256,1024]{1,0:T(8,128)(2,1)}, u32[]{:S(2)}) copy-start(bf16[256,1024]{1,0:T(8,128)(2,1)} %get-tuple-element.53) | copy-start | bytes 1572868
  291.7 5.7 copy-start
  291.8 5.7 copy-start.1
  291.8 5.7 copy-start.2
  291.8 5.7 copy-start.3
  291.8 5.7 copy-start.4
  291.8 5.7 copy-start.5
  297.4 21.5 %copy-start.36 = (bf16[1024,1024]{1,0:T(8,128)(2,1)S(1)}, bf16[1024,1024]{1,0:T(8,128)(2,1)}, u32[]{:S(2)}) copy-start(bf16[1024,1024]{1,0:T(8,128)(2,1)} %get-tuple-element.61) | copy-start | bytes 6291460
  328.2 218.6 %reduce-scatter.5.cloned.1.call-start = ((), (), s32[]{:S(2)}) async-start(), calls=%async_computation.3 | async-start | bytes 7077888 | tf_op jit(solution)/shard_map/reduce_scatter | solution.py:1493
  341.1 18.9 %copy-start.26 = (f32[1024]{0:T(1024)S(1)}, f32[1024]{0:T(1024)}, u32[]{:S(2)}) copy-start(f32[1024]{0:T(1024)} %convert_element_type.83) | copy-start | bytes 12292
  362.1 24.9 %copy-start.34 = (pred[4]{0:T(512)(128)(4,1)S(1)}, pred[4]{0:T(512)(128)(4,1)}, u32[]{:S(2)}) copy-start(pred[4]{0:T(512)(128)(4,1)} %copy-done.33) | copy-start | bytes 16
  434.8 130.2 %copy-start.22 = (bf16[2,128,1024]{2,1,0:T(8,128)(2,1)S(1)}, bf16[2,128,1024]{2,1,0:T(8,128)(2,1)}, u32[]{:S(2)}) copy-start(bf16[2,128,1024]{2,1,0:T(8,128)(2,1)} %get-tuple-element.137) | copy-start | bytes 1572868
  546.9 18.9 %copy-start.21 = (bf16[2,128,1024]{2,1,0:T(8,128)(2,1)S(1)}, bf16[2,128,1024]{2,1,0:T(8,128)(2,1)}, u32[]{:S(2)}) copy-start(bf16[2,128,1024]{2,1,0:T(8,128)(2,1)} %get-tuple-element.138) | copy-start | bytes 1572868
  (16 other events, 30.2 us)
Sparse Core Ops, SparseCore 0:
  328.3 98.0 reduce-scatter.2
  430.0 116.8 reduce-scatter.4

commit v3 on v0

--- a/solution.py
+++ b/solution.py
@@ -1,6 +1,10 @@
+import functools
+
 import jax
 import jax.numpy as jnp
 from jax import lax
+from jax.experimental import pallas as pl
+from jax.experimental.pallas import tpu as pltpu
 from jax.sharding import PartitionSpec as P
 
 HEADS = 16
@@ -357,6 +361,1128 @@
     )
 
 
+MESH = pl.DeviceIdType.MESH
+VM = pl.BlockSpec(memory_space=pltpu.VMEM)
+HB = pl.BlockSpec(memory_space=pl.ANY)
+SM = pl.BlockSpec(memory_space=pltpu.SMEM)
+DMA = pltpu.SemaphoreType.DMA
+NT = (((1,), (1,)), ((), ()))
+TN = (((0,), (0,)), ((), ()))
+EVERY = slice(None)
+
+
+def bf16(*shape):
+    return jax.ShapeDtypeStruct(shape, jnp.bfloat16)
+
+
+def f32(*shape):
+    return jax.ShapeDtypeStruct(shape, jnp.float32)
+
+
+def dot(a, b, dims=None, out=jnp.float32):
+    dims = (((1,), (0,)), ((), ())) if dims is None else dims
+    return lax.dot_general(a, b, dims, preferred_element_type=jnp.float32).astype(out)
+
+
+def at(dp, seq):
+    return {"dp": dp, "seq": seq}
+
+
+def place():
+    return lax.axis_index("dp"), lax.axis_index("seq")
+
+
+def ring(i):
+    return i + 1 - 2 * lax.rem(i, 2), lax.rem(i + 2, 4)
+
+
+def owned(i, s):
+    return 4 * lax.rem(i, 2) + 2 * s + i // 2
+
+
+def keeper(j):
+    return 2 * lax.rem(j, 2) + j // 4
+
+
+def send(src, dst, send_sem, recv_sem, peer):
+    return pltpu.make_async_remote_copy(
+        src_ref=src,
+        dst_ref=dst,
+        send_sem=send_sem,
+        recv_sem=recv_sem,
+        device_id=peer,
+        device_id_type=MESH,
+    )
+
+
+def landed(ref, sem):
+    pltpu.make_async_copy(ref, ref, sem).wait()
+
+
+def meet(peers, home=False):
+    i, j = place()
+    barrier = pltpu.get_barrier_semaphore()
+    for peer in peers:
+        pl.semaphore_signal(barrier, inc=1, device_id=peer, device_id_type=MESH)
+    if home:
+        target, stays = keeper(j), keeper(j) == i
+        for s in (0, 1):
+
+            @pl.when(jnp.logical_not(stays & (owned(i, s) == j)))
+            def _():
+                pl.semaphore_signal(
+                    barrier, inc=1, device_id=at(target, owned(i, s)), device_id_type=MESH
+                )
+
+        pl.semaphore_wait(barrier, len(peers) + jnp.where(stays, 1, 2))
+    else:
+        pl.semaphore_wait(barrier, len(peers))
+
+
+def dp_peers():
+    i, j = place()
+    return [at(lax.rem(i + step, 4), j) for step in (1, 2, 3)]
+
+
+def seq_peers():
+    i, j = place()
+    z, y = j // 2, lax.rem(j, 2)
+    return [at(i, 2 * lax.rem(z + step, 4) + y) for step in (1, 2, 3)] + [at(i, 2 * z + 1 - y)]
+
+
+class Home:
+    def __init__(self, ins, outs, sems, slotted):
+        self.ins, self.outs, self.slotted = ins, outs, slotted
+        self.send_sem, self.recv_sem = sems
+
+    @staticmethod
+    def sems(count):
+        return [DMA((count, 2)), DMA((count, 2))]
+
+    def target(self, a, s):
+        i, _ = place()
+        return self.outs[a].at[s if self.slotted else owned(i, s)]
+
+    def start(self, a, s):
+        i, j = place()
+        slot = lax.rem(j // 2, 2)
+        src, dst = self.ins[a].at[s], self.outs[a].at[slot if self.slotted else j]
+        here = (keeper(j) == i) & (owned(i, s) == j)
+
+        @pl.when(jnp.logical_not(here))
+        def _():
+            peer = at(keeper(j), owned(i, s))
+            send(src, dst, self.send_sem.at[a, s], self.recv_sem.at[a, slot], peer).start()
+
+        @pl.when(here)
+        def _():
+            pltpu.make_async_copy(src, dst, self.recv_sem.at[a, slot]).start()
+
+    def wait(self, a, s):
+        landed(self.target(a, s), self.recv_sem.at[a, s])
+
+    def finish(self, a):
+        i, j = place()
+        for s in (0, 1):
+
+            @pl.when(jnp.logical_not((keeper(j) == i) & (owned(i, s) == j)))
+            def _():
+                landed(self.ins[a].at[s], self.send_sem.at[a, s])
+
+
+class GroupGather:
+    def __init__(self, outs, sems):
+        self.outs = outs
+        self.s_core, self.r_core, self.s_x, self.r_x, self.s_on, self.r_on = sems
+
+    @staticmethod
+    def sems(count):
+        return [DMA((count, 2))] * 6
+
+    def push(self, a, s):
+        i, j = place()
+        core, across = ring(i)
+        block = self.outs[a].at[owned(i, s)]
+        send(block, block, self.s_x.at[a, s], self.r_x.at[a, s], at(across, j)).start()
+        send(block, block, self.s_core.at[a, s], self.r_core.at[a, s], at(core, j)).start()
+
+    def relay(self, a, s):
+        i, j = place()
+        core, across = ring(i)
+        block = self.outs[a].at[owned(across, s)]
+        landed(block, self.r_x.at[a, s])
+        send(block, block, self.s_on.at[a, s], self.r_on.at[a, s], at(core, j)).start()
+
+    def finish(self, a):
+        i, _ = place()
+        core, _ = ring(i)
+        for s in (0, 1):
+            landed(self.outs[a].at[owned(core, s)], self.r_core.at[a, s])
+            landed(self.outs[a].at[owned(lax.rem(core + 2, 4), s)], self.r_on.at[a, s])
+        for s in (0, 1):
+            for sem in (self.s_x, self.s_core, self.s_on):
+                landed(self.outs[a].at[s], sem.at[a, s])
+
+
+class GroupSum:
+    def __init__(self, parts, buffers, sems):
+        self.parts = parts
+        self.near, self.far = buffers
+        self.s_core, self.r_core, self.s_x, self.r_x = sems
+
+    @staticmethod
+    def buffers():
+        block = (128, 1024)
+        return [pltpu.VMEM((2, 2) + block, jnp.bfloat16), pltpu.VMEM((2,) + block, jnp.bfloat16)]
+
+    @staticmethod
+    def sems():
+        return [DMA((2, 2)), DMA((2, 2)), DMA((2,)), DMA((2,))]
+
+    def start(self, s):
+        i, j = place()
+        core, _ = ring(i)
+        for side, owner in ((0, lax.rem(core + 2, 4)), (1, core)):
+            send(
+                self.parts.at[owned(owner, s)],
+                self.near.at[side, s],
+                self.s_core.at[side, s],
+                self.r_core.at[side, s],
+                at(core, j),
+            ).start()
+
+    def cross(self, s):
+        i, j = place()
+        _, across = ring(i)
+        landed(self.near.at[0, s], self.r_core.at[0, s])
+        both = self.parts[owned(across, s)].astype(jnp.float32)
+        both = both + self.near[0, s].astype(jnp.float32)
+        self.near[0, s] = both.astype(jnp.bfloat16)
+        send(
+            self.near.at[0, s], self.far.at[s], self.s_x.at[s], self.r_x.at[s], at(across, j)
+        ).start()
+
+    def total(self, s):
+        i, _ = place()
+        landed(self.near.at[1, s], self.r_core.at[1, s])
+        both = self.parts[owned(i, s)].astype(jnp.float32) + self.near[1, s].astype(jnp.float32)
+        landed(self.far.at[s], self.r_x.at[s])
+        return both + self.far[s].astype(jnp.float32)
+
+    def finish(self):
+        for s in (0, 1):
+            landed(self.near.at[0, s], self.s_x.at[s])
+            for side in (0, 1):
+                landed(self.near.at[side, s], self.s_core.at[side, s])
+
+
+class Exchange:
+    def __init__(self, pieces, sems):
+        self.pieces = pieces
+        self.send_sem, self.recv_sem, self.own_sem = sems
+        self.copies = []
+
+    @staticmethod
+    def sems(count):
+        return [DMA((3, count)), DMA((3, count)), DMA((count,))]
+
+    def start(self):
+        i, j = place()
+        for step in (2, 3, 1):
+            other = lax.rem(i + step, 4)
+            for index, (src, dst) in enumerate(self.pieces(i, other)):
+                copy = send(
+                    src,
+                    dst,
+                    self.send_sem.at[step - 1, index],
+                    self.recv_sem.at[step - 1, index],
+                    at(other, j),
+                )
+                copy.start()
+                self.copies.append(copy)
+        for index, (src, dst) in enumerate(self.pieces(i, i)):
+            copy = pltpu.make_async_copy(src, dst, self.own_sem.at[index])
+            copy.start()
+            self.copies.append(copy)
+
+    def wait(self):
+        for copy in self.copies:
+            copy.wait()
+
+
+class SeqGather:
+    def __init__(self, full, chunks, sems):
+        self.full, self.chunks = full, chunks
+        self.s_z, self.r_z, self.s_y, self.r_y = sems
+
+    @staticmethod
+    def sems(count):
+        return [DMA((count, 3)), DMA((count, 3)), DMA((count, 4)), DMA((count, 4))]
+
+    def block(self, chunk, z, y):
+        start, size = self.chunks[chunk]
+        return self.full.at[2 * z + y, pl.ds(start, size)]
+
+    def start(self, chunk):
+        i, j = place()
+        z, y = j // 2, lax.rem(j, 2)
+        own = self.block(chunk, z, y)
+        for dz in (2, 1, 3):
+            peer = at(i, 2 * lax.rem(z + dz, 4) + y)
+            send(own, own, self.s_z.at[chunk, dz - 1], self.r_z.at[chunk, dz - 1], peer).start()
+        send(own, own, self.s_y.at[chunk, 0], self.r_y.at[chunk, 0], at(i, 2 * z + 1 - y)).start()
+
+    def forward(self, chunk, dz):
+        i, j = place()
+        z, y = j // 2, lax.rem(j, 2)
+        block = self.block(chunk, lax.rem(z + 4 - dz, 4), y)
+        landed(block, self.r_z.at[chunk, dz - 1])
+        peer = at(i, 2 * z + 1 - y)
+        send(block, block, self.s_y.at[chunk, dz], self.r_y.at[chunk, dz], peer).start()
+
+    def arrived(self, chunk, dz):
+        _, j = place()
+        z, y = j // 2, lax.rem(j, 2)
+        landed(self.block(chunk, lax.rem(z + 4 - dz, 4), 1 - y), self.r_y.at[chunk, dz])
+
+    def drain(self, chunk):
+        _, j = place()
+        own = self.block(chunk, j // 2, lax.rem(j, 2))
+        for dz in (0, 1, 2, 3):
+            landed(own, self.s_y.at[chunk, dz])
+            if dz:
+                landed(own, self.s_z.at[chunk, dz - 1])
+
+    def finish(self, chunk):
+        for dz in (0, 1, 2, 3):
+            self.arrived(chunk, dz)
+        self.drain(chunk)
+
+
+class SeqSum:
+    def __init__(self, parts, chunks, scratch):
+        self.parts, self.chunks = parts, chunks
+        self.near, self.far = scratch[:2]
+        self.s_y, self.r_y, self.s_z, self.r_z = scratch[2:]
+
+    @staticmethod
+    def scratch(rows, count):
+        return [
+            pltpu.VMEM((4, rows, 128), jnp.bfloat16),
+            pltpu.VMEM((3, rows, 128), jnp.bfloat16),
+            DMA((count, 4)),
+            DMA((count, 4)),
+            DMA((count, 3)),
+            DMA((count, 3)),
+        ]
+
+    def start(self, chunk, dz):
+        i, j = place()
+        z, y = j // 2, lax.rem(j, 2)
+        rows = pl.ds(*self.chunks[chunk])
+        send(
+            self.parts.at[2 * lax.rem(z + dz, 4) + 1 - y, rows],
+            self.near.at[dz, rows],
+            self.s_y.at[chunk, dz],
+            self.r_y.at[chunk, dz],
+            at(i, 2 * z + 1 - y),
+        ).start()
+
+    def each(self, chunk, body):
+        start, size = self.chunks[chunk]
+
+        @pl.loop(0, size // 256)
+        def _(t):
+            body(pl.ds(pl.multiple_of(start + t * 256, 256), 256))
+
+    def cross(self, chunk, dz):
+        i, j = place()
+        z, y = j // 2, lax.rem(j, 2)
+        rows = pl.ds(*self.chunks[chunk])
+        target = lax.rem(z + dz, 4)
+        landed(self.near.at[dz, rows], self.r_y.at[chunk, dz])
+
+        def add(part):
+            both = self.parts[2 * target + y, part, :].astype(jnp.float32)
+            both = both + self.near[dz, part, :].astype(jnp.float32)
+            self.near[dz, part, :] = both.astype(jnp.bfloat16)
+
+        self.each(chunk, add)
+        send(
+            self.near.at[dz, rows],
+            self.far.at[dz - 1, rows],
+            self.s_z.at[chunk, dz - 1],
+            self.r_z.at[chunk, dz - 1],
+            at(i, 2 * target + y),
+        ).start()
+
+    def finish(self, chunk):
+        _, j = place()
+        rows = pl.ds(*self.chunks[chunk])
+        landed(self.near.at[0, rows], self.r_y.at[chunk, 0])
+        for dz in (1, 2, 3):
+            landed(self.far.at[dz - 1, rows], self.r_z.at[chunk, dz - 1])
+
+        def add(part):
+            total = self.parts[j, part, :].astype(jnp.float32)
+            total = total + self.near[0, part, :].astype(jnp.float32)
+            for dz in (1, 2, 3):
+                total = total + self.far[dz - 1, part, :].astype(jnp.float32)
+            self.near[0, part, :] = total.astype(jnp.bfloat16)
+
+        self.each(chunk, add)
+
+    def drain(self, chunk):
+        rows = pl.ds(*self.chunks[chunk])
+        for dz in (0, 1, 2, 3):
+            landed(self.near.at[dz, rows], self.s_y.at[chunk, dz])
+            if dz:
+                landed(self.near.at[dz, rows], self.s_z.at[chunk, dz - 1])
+
+
+class SmallSum:
+    def __init__(self, value, scratch):
+        self.value = value
+        self.stages, self.sems = scratch[:3], scratch[3:]
+
+    @staticmethod
+    def scratch(shape):
+        return [pltpu.VMEM((count,) + shape, jnp.float32) for count in (4, 4, 2)] + [
+            DMA((count,)) for count in (3, 3, 3, 3, 1, 1)
+        ]
+
+    def run(self):
+        i, j = place()
+        z, y = j // 2, lax.rem(j, 2)
+        rounds = (
+            (i, dp_peers()),
+            (z, seq_peers()[:3]),
+            (y, seq_peers()[3:]),
+        )
+        total = self.value[...]
+        for stage, (spot, peers) in enumerate(rounds):
+            held = self.stages[stage]
+            held[spot] = total
+            for step, peer in enumerate(peers):
+                send(
+                    held.at[spot],
+                    held.at[spot],
+                    self.sems[2 * stage].at[step],
+                    self.sems[2 * stage + 1].at[step],
+                    peer,
+                ).start()
+            for step in range(len(peers)):
+                landed(held.at[0], self.sems[2 * stage + 1].at[step])
+                landed(held.at[0], self.sems[2 * stage].at[step])
+            total = held[0]
+            for index in range(1, held.shape[0]):
+                total = total + held[index]
+        return total
+
+
+def swap_halves(x):
+    lane = lax.broadcasted_iota(jnp.int32, x.shape, 1)
+    width = x.shape[1]
+    return jnp.where(lane % 64 < 32, pltpu.roll(x, width - 32, 1), pltpu.roll(x, 32, 1))
+
+
+def angle_tables(table):
+    lane = lax.broadcasted_iota(jnp.int32, table.shape, 1)
+    by_32, by_64, by_96 = (pltpu.roll(table, shift, 1) for shift in (32, 64, 96))
+    first, second, third = lane < 32, lane < 64, lane < 96
+    cos_t = jnp.where(first, table, jnp.where(second, by_32, jnp.where(third, by_64, by_96)))
+    sin_t = jnp.where(first, -by_96, jnp.where(second, table, jnp.where(third, -by_32, by_64)))
+    return cos_t, sin_t
+
+
+SLOTS = (
+    (0, 1, 2, 4, 5, 6, 8, 9, 10, 12, 13, 14),
+    (0, 2, 3, 4, 6, 7, 8, 10, 11, 12, 14, 15),
+)
+
+
+def attention_pieces(packed, w_out, dst):
+    def pieces(me, other):
+        _, j = place()
+        spot = lax.rem(other + 2 * lax.rem(j, 2), 4)
+        return [
+            (packed.at[spot], dst.at[j, pl.ds(256 * me, 256)]),
+            (w_out.at[pl.ds(64 * other, 64)], dst.at[j, pl.ds(1024 + 64 * me, 64)]),
+        ]
+
+    return pieces
+
+
+def ffn_pieces(w_gate, w_up, w_down, dst):
+    def pieces(me, other):
+        _, j = place()
+        columns = pl.ds(pl.multiple_of(128 * other, 128), 128)
+        pairs = [
+            (w_gate.at[:, columns], dst.at[j, pl.ds(256 * me, 256)]),
+            (w_up.at[:, columns], dst.at[j, pl.ds(1024 + 256 * me, 256)]),
+        ]
+        for half in (0, 1):
+            pairs.append(
+                (
+                    w_down.at[pl.ds(512 * half + 128 * other, 128)],
+                    dst.at[j, pl.ds(2048 + 256 * me + 128 * half, 128)],
+                )
+            )
+        return pairs
+
+    return pieces
+
+
+def head_weights(full, wh_ref, wm_ref, low_half):
+    def column(m, rows):
+        first, second = SLOTS[0][m], SLOTS[1][m]
+        one = full[first // 2, rows, 64 * (first % 2) : 64 * (first % 2) + 64]
+        two = full[second // 2, rows, 64 * (second % 2) : 64 * (second % 2) + 64]
+        return jnp.where(low_half, one, two)
+
+    @pl.loop(0, 4)
+    def _(t):
+        rows = pl.ds(pl.multiple_of(t * 256, 256), 256)
+        for m in range(0, 12, 2):
+            wh_ref[rows, 64 * m : 64 * m + 128] = jnp.concatenate(
+                [column(m, rows), column(m + 1, rows)], axis=1
+            )
+
+    for b in range(8):
+        wm_ref[:, 128 * b : 128 * b + 128] = full[b, 1024:1280, :]
+
+
+def norm_rows(hidden):
+    return lax.rsqrt(jnp.mean(hidden * hidden, axis=1, keepdims=True) + EPSILON)
+
+
+def return_attention(src, g_qkv, g_out):
+    def pieces(me, other):
+        _, j = place()
+        spot = lax.rem(me + 2 * lax.rem(j, 2), 4)
+        return [
+            (src.at[pl.ds(256 * other, 256)], g_qkv.at[spot]),
+            (src.at[pl.ds(1024 + 64 * other, 64)], g_out.at[pl.ds(64 * me, 64)]),
+        ]
+
+    return pieces
+
+
+def return_ffn(src, g_gate, g_up, g_down):
+    def pieces(me, other):
+        columns = pl.ds(pl.multiple_of(128 * me, 128), 128)
+        pairs = [
+            (src.at[pl.ds(256 * other, 256)], g_gate.at[:, columns]),
+            (src.at[pl.ds(1024 + 256 * other, 256)], g_up.at[:, columns]),
+        ]
+        for half in (0, 1):
+            pairs.append(
+                (
+                    src.at[pl.ds(2048 + 256 * other + 128 * half, 128)],
+                    g_down.at[pl.ds(512 * half + 128 * me, 128)],
+                )
+            )
+        return pairs
+
+    return pieces
+
+
+def back_rows(grad_in, hidden, inv_rms):
+    mean = jnp.mean(grad_in * hidden, axis=1, keepdims=True)
+    return inv_rms * grad_in - hidden * (inv_rms * inv_rms * inv_rms * mean)
+
+
+def slot_columns(grads, slot, low_half):
+    picks = []
+    for row in SLOTS:
+        if slot in row:
+            m = row.index(slot)
+            picks.append(grads[:, 64 * m : 64 * m + 64])
+        else:
+            picks.append(jnp.zeros((grads.shape[0], 64), jnp.float32))
+    return jnp.where(low_half, picks[0], picks[1])
+
+
+FFN_CHUNKS = ((2048, 1024), (0, 2048))
+GRAD_CHUNKS = ((0, 2048), (2048, 1024))
+ATTENTION_CHUNKS = ((0, 1024), (1024, 256))
+ARRIVAL = (2, 1, 3)
+
+
+def wide(ref, first, rows):
+    return jnp.concatenate([ref[first, rows, :], ref[first + 1, rows, :]], axis=1)
+
+
+def store_wide(ref, first, rows, value):
+    ref[first, rows, :] = value[:, :128]
+    ref[first + 1, rows, :] = value[:, 128:]
+
+
+def two(ref, t, cols=slice(None)):
+    value = ref[pl.ds(2 * t, 2), :, cols]
+    return value.reshape(256, value.shape[2])
+
+
+def layer_kernel(*refs):
+    (tok, cot, tab, idr, packed, w_out, w_gate, w_up, w_down, gain_one, gain_two, bias), refs = (
+        refs[:12],
+        refs[12:],
+    )
+    (output, input_grad, g_gate, g_up, g_down, g_qkv, g_out, small_out), refs = refs[:8], refs[8:]
+    (
+        tok_all, cot_all, tab_all, idr_all, tok_own, attn_all, wh_ref, wm_ref, q_ref, k_ref, v_ref,
+        o_ref, lse_ref, rows_ref, part, mid_ref, a2_all, turned, ffn_all, ffn_g, hidden_s, dgate_s,
+        dup_s, e2_ref, dq_acc, dk_acc, dv_acc, out_own, in_own, dbias, small,
+        r_gate, r_up, r_down, r_qkv, r_out,
+    ), refs = refs[:36], refs[36:]
+    home_in, refs = refs[:2], refs[2:]
+    home_out, refs = refs[:2], refs[2:]
+    gather_in, refs = refs[:6], refs[6:]
+    gather_a2, refs = refs[:6], refs[6:]
+    gather_ez, refs = refs[:6], refs[6:]
+    buffers, refs = refs[:2], refs[2:]
+    out_buffers, refs = refs[:2], refs[2:]
+    sum_sems, refs = [refs[4 * n : 4 * n + 4] for n in range(4)], refs[16:]
+    spread_a, spread_f, back_a, back_f = [refs[3 * n : 3 * n + 3] for n in range(4)]
+    refs = refs[12:]
+    chain_a, chain_f, refs = refs[:4], refs[4:8], refs[8:]
+    fold_f, fold_a, refs = refs[:6], refs[6:12], refs[12:]
+    small_scratch = refs
+
+    i, j = place()
+    z, y = j // 2, lax.rem(j, 2)
+    mine_first = 2 * (1 - lax.rem(i, 2))
+    low_half = i < 2
+
+    def turn(u):
+        return lax.rem(mine_first + u, 4)
+
+    ez_all, dqkv_ref, do_ref, out_part = dgate_s, dup_s, hidden_s, turned
+    home = Home((tok, tab, idr, cot), (tok_all, tab_all, idr_all, cot_all), home_in, False)
+    group = GroupGather((tok_all, tab_all, idr_all, cot_all), gather_in)
+    spread = Exchange(attention_pieces(packed, w_out, attn_all), spread_a)
+    spread_ffn = Exchange(ffn_pieces(w_gate, w_up, w_down, ffn_all), spread_f)
+    attn_w = SeqGather(attn_all, ((0, 1280),), chain_a)
+    ffn_w = SeqGather(ffn_all, FFN_CHUNKS, chain_f)
+    branch = GroupSum(part, buffers, sum_sems[0])
+    second = GroupGather((a2_all,), gather_a2)
+    da_sum = GroupSum(part, buffers, sum_sems[1])
+    out_sum = GroupSum(out_part, out_buffers, sum_sems[2])
+    da1_sum = GroupSum(part, buffers, sum_sems[3])
+    third = GroupGather((ez_all,), gather_ez)
+    leave = Home((out_own, in_own), (output, input_grad), home_out, True)
+    ffn_fold = SeqSum(ffn_g, GRAD_CHUNKS, fold_f)
+    attn_fold = SeqSum(attn_all, ATTENTION_CHUNKS, fold_a)
+    ffn_back = Exchange(return_ffn(fold_f[0].at[0], r_gate, r_up, r_down), back_f)
+    attn_back = Exchange(return_attention(fold_a[0].at[0], r_qkv, r_out), back_a)
+
+    meet(dp_peers() + seq_peers(), home=True)
+    for a in (0, 1, 2):
+        for s in (0, 1):
+            home.start(a, s)
+    spread.start()
+    spread_ffn.start()
+    spread.wait()
+    attn_w.start(0)
+    for a in (0, 1, 2):
+        for s in (0, 1):
+            home.wait(a, s)
+            group.push(a, s)
+    spread_ffn.wait()
+    ffn_w.start(0)
+    for s in (0, 1):
+        home.start(3, s)
+    ffn_w.start(1)
+    for s in (0, 1):
+        tok_own[s] = tok_all[owned(i, s)]
+    for a in (0, 1, 2):
+        for s in (0, 1):
+            group.relay(a, s)
+    for a in (0, 1, 2):
+        group.finish(a)
+        home.finish(a)
+    for b in range(8):
+        rows_ref[:, 128 * b : 128 * b + 128] = idr_all[b]
+
+    @pl.loop(0, 8)
+    def _(b):
+        hidden = tok_all[b].astype(jnp.float32)
+        tok_all[b] = (hidden * norm_rows(hidden) * gain_one[...]).astype(jnp.bfloat16)
+
+    a1_all = tok_all
+    for dz in ARRIVAL:
+        attn_w.forward(0, dz)
+    attn_w.finish(0)
+    head_weights(attn_all, wh_ref, wm_ref, low_half)
+
+    @pl.loop(0, 4)
+    def _(t):
+        rows = pl.ds(pl.multiple_of(t * 256, 256), 256)
+        proj = dot(two(a1_all, t), wh_ref[...])
+        cos_t, sin_t = angle_tables(two(tab_all, t))
+        for pair in (0, 1):
+            cols = slice(128 * pair, 128 * pair + 128)
+            for base, out in ((0, q_ref), (256, k_ref)):
+                x = proj[:, base + 128 * pair : base + 128 * pair + 128]
+                out[rows, cols] = (x * cos_t + swap_halves(x) * sin_t).astype(jnp.bfloat16)
+        v_ref[rows, :] = proj[:, 512:768].astype(jnp.bfloat16)
+
+    @pl.loop(0, 4)
+    def _(u):
+        t = turn(u)
+        start = pl.multiple_of(t * 256, 256)
+        rows = pl.ds(start, 256)
+        columns = two(tab_all, t)
+        seg_q, var_q = columns[:, 64:65], columns[:, 65:66]
+        code_k, var_k = rows_ref[0:1, :], rows_ref[1:2, :]
+        row = start + lax.broadcasted_iota(jnp.int32, (256, 1024), 0)
+        col = lax.broadcasted_iota(jnp.int32, (256, 1024), 1)
+        allowed = ((seg_q == code_k) & (jnp.abs(row - col) <= WINDOW)) | (row == col)
+        masked = jnp.where(allowed, 0.0, NEGATIVE)
+        same = jnp.where(var_q == var_k, 1.0, 0.0)
+        stats = jnp.zeros((256, 128), jnp.float32)
+        lane = lax.broadcasted_iota(jnp.int32, (256, 128), 1)
+        for h in range(4):
+            cols = slice(64 * h, 64 * h + 64)
+            scores = dot(q_ref[rows, cols] * 0.125, k_ref[:, cols], NT)
+            scores = scores + bias[h] * same + masked
+            top = jnp.max(scores, axis=1, keepdims=True)
+            weight = jnp.exp(scores - top)
+            total = jnp.sum(weight, axis=1, keepdims=True)
+            mixed = dot(weight.astype(jnp.bfloat16), v_ref[:, cols])
+            o_ref[rows, cols] = (mixed / total).astype(jnp.bfloat16)
+            stats = jnp.where(lane == h, top + jnp.log(total), stats)
+        lse_ref[:, rows] = stats.T[:8]
+        part[pl.ds(2 * t, 2)] = dot(o_ref[rows, :], wm_ref[...], out=jnp.bfloat16).reshape(2, 128, 1024)
+        for s in (0, 1):
+
+            @pl.when(u == s)
+            def _():
+                branch.start(s)
+
+            @pl.when(u == s + 2)
+            def _():
+                branch.cross(s)
+
+        @pl.when(u == 1)
+        def _():
+            for dz in ARRIVAL:
+                ffn_w.forward(0, dz)
+
+    for s in (0, 1):
+        home.wait(3, s)
+        group.push(3, s)
+    for s in (0, 1):
+        block = owned(i, s)
+        mid = tok_own[s].astype(jnp.float32) + branch.total(s)
+        mid_ref[s] = mid
+        a2_all[block] = (mid * norm_rows(mid) * gain_two[...]).astype(jnp.bfloat16)
+        second.push(0, s)
+    branch.finish()
+    ffn_w.forward(1, 2)
+    for s in (0, 1):
+        group.relay(3, s)
+    for s in (0, 1):
+        second.relay(0, s)
+    ffn_w.forward(1, 1)
+    group.finish(3)
+    home.finish(3)
+    second.finish(0)
+    ffn_w.finish(0)
+
+    @pl.loop(0, 4)
+    def _(t):
+        for d in range(4):
+            turned[2 * d : 2 * d + 2, :, pl.ds(pl.multiple_of(256 * t, 256), 256)] = (
+                two(a2_all, t, slice(256 * d, 256 * d + 256)).T.reshape(2, 128, 256)
+            )
+
+    def unit(dz):
+        f = lax.rem(z + 4 - dz, 4)
+        cols = pl.ds(pl.multiple_of(256 * f, 256), 256)
+        wg, wu = wide(ffn_all, 2 * f, slice(0, 1024)), wide(ffn_all, 2 * f, slice(1024, 2048))
+        down = pl.ds(pl.multiple_of(2048 + 256 * f, 256), 256)
+        wd = jnp.concatenate([ffn_all[b, down, :] for b in range(8)], axis=1)
+
+        @pl.loop(0, 4)
+        def _(t):
+            a, g = two(a2_all, t), two(cot_all, t)
+            gate, up, dh = dot(a, wg), dot(a, wu), dot(g, wd, NT)
+            sig = 1.0 / (1.0 + jnp.exp(-gate))
+            gate_sig = gate * sig
+            into = (pl.ds(2 * t, 2), slice(None), cols)
+            hidden_s[into] = (gate_sig * up).astype(jnp.bfloat16).reshape(2, 128, 256)
+            dgate = dh * up * (sig + gate_sig * (1.0 - sig))
+            dgate_s[into] = dgate.astype(jnp.bfloat16).reshape(2, 128, 256)
+            dup_s[into] = (dh * gate_sig).astype(jnp.bfloat16).reshape(2, 128, 256)
+
+        @pl.loop(0, 4)
+        def _(d):
+            rows = pl.ds(pl.multiple_of(d * 256, 256), 256)
+            rows_up = pl.ds(pl.multiple_of(1024 + d * 256, 256), 256)
+            a_t = two(turned, d)
+            dgate, dup = dgate_s[:, :, cols].reshape(1024, 256), dup_s[:, :, cols].reshape(1024, 256)
+            store_wide(ffn_g, 2 * f, rows, dot(a_t, dgate, out=jnp.bfloat16))
+            store_wide(ffn_g, 2 * f, rows_up, dot(a_t, dup, out=jnp.bfloat16))
+
+        h_t = hidden_s[:, :, cols].reshape(1024, 256).T
+        for d in range(4):
+            g = cot_all[:, :, 256 * d : 256 * d + 256].reshape(1024, 256)
+            store_wide(ffn_g, 2 * d, down, dot(h_t, g, out=jnp.bfloat16))
+
+    @pl.loop(0, 4)
+    def _(step):
+        dz = jnp.where(step == 1, 2, jnp.where(step == 2, 1, step))
+        for n, here in enumerate((0, 2, 1, 3)):
+
+            @pl.when(step == n)
+            def _():
+                if n == 3:
+                    ffn_w.forward(1, 3)
+                ffn_w.arrived(1, here)
+
+        unit(dz)
+        for n, there in enumerate((0, 2, 3, 1)):
+
+            @pl.when(step == n)
+            def _():
+                ffn_fold.start(0, there)
+
+    for dz in (2, 3, 1, 0):
+        ffn_fold.start(1, dz)
+    ffn_w.drain(1)
+
+    def product(left, t, first_row):
+        total = None
+        for p in range(4):
+            piece = dot(
+                two(left, t, slice(256 * p, 256 * p + 256)),
+                wide(ffn_all, 2 * p, slice(first_row, first_row + 1024)),
+                NT,
+            )
+            total = piece if total is None else total + piece
+        return total
+
+    @pl.loop(0, 4)
+    def _(u):
+        t = turn(u)
+        value = product(dgate_s, t, 0) + product(dup_s, t, 1024)
+        part[pl.ds(2 * t, 2)] = value.astype(jnp.bfloat16).reshape(2, 128, 1024)
+        for s in (0, 1):
+
+            @pl.when(u == s)
+            def _():
+                da_sum.start(s)
+
+            @pl.when(u == s + 2)
+            def _():
+                da_sum.cross(s)
+
+    @pl.loop(0, 4)
+    def _(u):
+        t = turn(u)
+        hidden = two(hidden_s, t)
+        for d in range(4):
+            w = wide(ffn_all, 2 * d, slice(2048, 3072))
+            out_part[pl.ds(2 * t, 2), :, 256 * d : 256 * d + 256] = dot(
+                hidden, w, out=jnp.bfloat16
+            ).reshape(2, 128, 256)
+        for s in (0, 1):
+
+            @pl.when(u == s)
+            def _():
+                out_sum.start(s)
+
+    gain_rows = jnp.zeros((1, 1024), jnp.float32)
+    for s in (0, 1):
+        mid = mid_ref[s]
+        inv = norm_rows(mid)
+        da2 = da_sum.total(s)
+        gain_rows = gain_rows + jnp.sum(da2 * (mid * inv), axis=0, keepdims=True)
+        e2 = cot_all[owned(i, s)].astype(jnp.float32) + back_rows(da2 * gain_two[...], mid, inv)
+        e2_ref[s] = e2
+        ez_all[owned(i, s)] = e2.astype(jnp.bfloat16)
+        third.push(0, s)
+    for b in range(8):
+        small[8 + b : 9 + b, :] = gain_rows[:, 128 * b : 128 * b + 128]
+    for s in (0, 1):
+        out_sum.cross(s)
+    da_sum.finish()
+    ffn_fold.cross(0, 2)
+    for s in (0, 1):
+        third.relay(0, s)
+    third.finish(0)
+
+    @pl.loop(0, 4)
+    def _(t):
+        do_ref[pl.ds(2 * t, 2), :, 0:256] = dot(two(ez_all, t), wm_ref[...], NT, jnp.bfloat16).reshape(
+            2, 128, 256
+        )
+
+    for d in range(4):
+        ez = ez_all[:, :, 256 * d : 256 * d + 256].reshape(1024, 256)
+        store_wide(attn_all, 2 * d, slice(1024, 1280), dot(o_ref[...], ez, TN, jnp.bfloat16))
+    for dz in (2, 3, 1, 0):
+        attn_fold.start(1, dz)
+    ffn_fold.cross(0, 3)
+    for s in (0, 1):
+        out_own[s] = (mid_ref[s] + out_sum.total(s)).astype(jnp.bfloat16)
+        leave.start(0, s)
+
+    def unturn(acc, base, t, rows):
+        cos_t, sin_t = angle_tables(two(tab_all, t))
+        for pair in (0, 1):
+            g = acc[rows, 128 * pair : 128 * pair + 128]
+            dqkv_ref[pl.ds(2 * t, 2), :, base + 128 * pair : base + 128 * pair + 128] = (
+                (g * cos_t - swap_halves(g) * sin_t).astype(jnp.bfloat16).reshape(2, 128, 128)
+            )
+
+    dk_acc[...] = jnp.zeros_like(dk_acc)
+    dv_acc[...] = jnp.zeros_like(dv_acc)
+    dbias[...] = jnp.zeros_like(dbias)
+
+    @pl.loop(0, 4)
+    def _(t):
+        start = pl.multiple_of(t * 256, 256)
+        rows = pl.ds(start, 256)
+        columns = tab_all[...].reshape(1024, 128)
+        var_k, code_k = columns[:, 65:66], columns[:, 66:67]
+        pair = idr_all[pl.ds(2 * t, 2)]
+        label = jnp.concatenate([pair[0], pair[1]], axis=1)
+        seg_q, var_q = label[2:3, :], label[1:2, :]
+        row = lax.broadcasted_iota(jnp.int32, (1024, 256), 0)
+        col = start + lax.broadcasted_iota(jnp.int32, (1024, 256), 1)
+        allowed = ((seg_q == code_k) & (jnp.abs(row - col) <= WINDOW)) | (row == col)
+        masked = jnp.where(allowed, 0.0, NEGATIVE)
+        same = jnp.where(var_q == var_k, 1.0, 0.0)
+        for h in range(4):
+            cols = slice(64 * h, 64 * h + 64)
+            q_h, k_h, v_h = q_ref[rows, cols] * 0.125, k_ref[:, cols], v_ref[:, cols]
+            do_h = two(do_ref, t, cols)
+            scores = dot(k_h, q_h, NT) + bias[h] * same + masked
+            prob = jnp.exp(scores - lse_ref[h : h + 1, rows])
+            dv_acc[:, cols] += dot(prob.astype(jnp.bfloat16), do_h)
+            dprob = dot(v_h, do_h, NT)
+            mean = jnp.sum(prob * dprob, axis=0, keepdims=True)
+            dscore = (prob * (dprob - mean)).astype(jnp.bfloat16)
+            dbias[h : h + 1, :] += jnp.sum(dscore.astype(jnp.float32) * same, axis=0, keepdims=True)
+            dk_acc[:, cols] += dot(dscore, q_h)
+            dq_acc[:, cols] = dot(dscore, k_h, TN) * 0.125
+
+        unturn(dq_acc, 0, t, slice(None))
+
+        @pl.when(t == 0)
+        def _():
+            ffn_fold.cross(0, 1)
+
+        @pl.when(t == 2)
+        def _():
+            ffn_fold.cross(1, 2)
+
+    @pl.loop(0, 4)
+    def _(t):
+        rows = pl.ds(pl.multiple_of(t * 256, 256), 256)
+        unturn(dk_acc, 256, t, rows)
+        dqkv_ref[pl.ds(2 * t, 2), :, 512:768] = (
+            dv_acc[rows, :].astype(jnp.bfloat16).reshape(2, 128, 256)
+        )
+
+    for d in range(4):
+        block = slice(256 * d, 256 * d + 256)
+        grads = dot(
+            a1_all[:, :, block].reshape(1024, 256), dqkv_ref[:, :, 0:768].reshape(1024, 768), TN
+        )
+        for b in range(8):
+            attn_all[b, block, :] = jnp.concatenate(
+                [slot_columns(grads, 2 * b + e, low_half) for e in (0, 1)], axis=1
+            ).astype(jnp.bfloat16)
+    for dz in (2, 3, 1, 0):
+        attn_fold.start(0, dz)
+    for dz in (3, 1):
+        ffn_fold.cross(1, dz)
+
+    @pl.loop(0, 4)
+    def _(u):
+        t = turn(u)
+        part[pl.ds(2 * t, 2)] = dot(
+            two(dqkv_ref, t, slice(0, 768)), wh_ref[...], NT, jnp.bfloat16
+        ).reshape(2, 128, 1024)
+        for s in (0, 1):
+
+            @pl.when(u == s)
+            def _():
+                da1_sum.start(s)
+
+            @pl.when(u == s + 2)
+            def _():
+                da1_sum.cross(s)
+
+    for dz in (2, 3, 1):
+        attn_fold.cross(1, dz)
+    gain_rows = jnp.zeros((1, 1024), jnp.float32)
+    for s in (0, 1):
+        hidden = tok_own[s].astype(jnp.float32)
+        inv = norm_rows(hidden)
+        da1 = da1_sum.total(s)
+        gain_rows = gain_rows + jnp.sum(da1 * (hidden * inv), axis=0, keepdims=True)
+        grad = e2_ref[s] + back_rows(da1 * gain_one[...], hidden, inv)
+        in_own[s] = grad.astype(jnp.bfloat16)
+        leave.start(1, s)
+    for b in range(8):
+        small[b : b + 1, :] = gain_rows[:, 128 * b : 128 * b + 128]
+    lane = lax.broadcasted_iota(jnp.int32, (8, 128), 1)
+    line = lax.broadcasted_iota(jnp.int32, (8, 128), 0)
+    bias_row = jnp.zeros((8, 128), jnp.float32)
+    for h in range(4):
+        value = jnp.sum(dbias[h : h + 1, :], axis=1, keepdims=True)
+        bias_row = jnp.where((line == 0) & (lane == 4 * h + i), value, bias_row)
+    small[16:24, :] = bias_row
+
+    for chunk in (0, 1):
+        ffn_fold.finish(chunk)
+    ffn_back.start()
+    small_out[...] = SmallSum(small, small_scratch).run()
+    for dz in (2, 3, 1):
+        attn_fold.cross(0, dz)
+    ffn_back.wait()
+    g_gate[...] = r_gate[...].astype(jnp.float32)
+    g_up[...] = r_up[...].astype(jnp.float32)
+    g_down[...] = r_down[...].astype(jnp.float32)
+    for chunk in (1, 0):
+        attn_fold.finish(chunk)
+    attn_back.start()
+    out_sum.finish()
+    da1_sum.finish()
+    for a in (0, 1):
+        for s in (0, 1):
+            leave.wait(a, s)
+        leave.finish(a)
+    for chunk in (0, 1):
+        ffn_fold.drain(chunk)
+        attn_fold.drain(chunk)
+    attn_back.wait()
+    g_qkv[...] = r_qkv[...].astype(jnp.float32)
+    g_out[...] = r_out[...].astype(jnp.float32)
+
+
+def layer(arrays):
+    def vmem(dtype, *shape):
+        return pltpu.VMEM(shape, dtype)
+
+    low, full = jnp.bfloat16, jnp.float32
+    blocks = vmem(low, 8, 128, 1024)
+    own = vmem(low, 2, 128, 1024)
+    heads = vmem(low, 1024, 256)
+    grads = vmem(full, 1024, 256)
+    return pl.pallas_call(
+        layer_kernel,
+        out_shape=[
+            bf16(2, 128, 1024),
+            bf16(2, 128, 1024),
+            f32(256, 512),
+            f32(256, 512),
+            f32(1024, 128),
+            f32(4, 256, 128),
+            f32(256, 128),
+            f32(24, 128),
+        ],
+        in_specs=[HB, HB, VM, VM, VM, VM, HB, HB, HB, VM, VM, SM],
+        out_specs=[HB] * 2 + [VM] * 6,
+        scratch_shapes=[
+            blocks,
+            blocks,
+            vmem(full, 8, 128, 128),
+            vmem(full, 8, 8, 128),
+            own,
+            vmem(low, 8, 1280, 128),
+            vmem(low, 1024, 768),
+            vmem(low, 256, 1024),
+            heads,
+            heads,
+            heads,
+            heads,
+            vmem(full, 8, 1024),
+            vmem(full, 8, 1024),
+            blocks,
+            vmem(full, 2, 128, 1024),
+            blocks,
+            blocks,
+            vmem(low, 8, 3072, 128),
+            vmem(low, 8, 3072, 128),
+            blocks,
+            blocks,
+            blocks,
+            vmem(full, 2, 128, 1024),
+            vmem(full, 256, 256),
+            grads,
+            grads,
+            own,
+            own,
+            vmem(full, 8, 256),
+            vmem(full, 24, 128),
+            vmem(low, 256, 512),
+            vmem(low, 256, 512),
+            vmem(low, 1024, 128),
+            vmem(low, 4, 256, 128),
+            vmem(low, 256, 128),
+        ]
+        + Home.sems(4)
+        + Home.sems(2)
+        + GroupGather.sems(4)
+        + GroupGather.sems(1)
+        + GroupGather.sems(1)
+        + GroupSum.buffers()
+        + GroupSum.buffers()
+        + GroupSum.sems() * 4
+        + Exchange.sems(2)
+        + Exchange.sems(4)
+        + Exchange.sems(2)
+        + Exchange.sems(4)
+        + SeqGather.sems(1)
+        + SeqGather.sems(2)
+        + SeqSum.scratch(3072, 2)
+        + SeqSum.scratch(1280, 2)
+        + SmallSum.scratch((24, 128)),
+        compiler_params=pltpu.CompilerParams(
+            collective_id=1, has_side_effects=True, vmem_limit_bytes=67_043_328
+        ),
+        name="layer",
+    )(*arrays)
+
+
+def on_group(
+    tokens, segment_ids, variate_ids, time_ids, pad_mask, cotangent,
+    w_qkv, w_out, w_gate, w_up, w_down, gain_attn, gain_ffn, variate_bias,
+):
+    i = lax.axis_index("dp")
+    gain_one = gain_attn.astype(jnp.float32)[None]
+    gain_two = gain_ffn.astype(jnp.float32)[None]
+    packed = jnp.pad(w_qkv, ((0, 0), (0, 128))).reshape(256, 2, 4, 64)
+    packed = packed.transpose(2, 0, 1, 3).reshape(4, 256, 128)
+    frequency = jnp.exp(-jnp.log(10000.0) * jnp.arange(32, dtype=jnp.float32) / 32)
+    angles = time_ids.astype(jnp.float32)[..., None] * frequency
+    code_ids = jnp.where(pad_mask == 1, segment_ids, -1)
+    labels = jnp.stack([segment_ids, variate_ids, code_ids], axis=-1).astype(jnp.float32)
+    tables = jnp.concatenate(
+        [jnp.cos(angles), jnp.sin(angles), labels, jnp.zeros((2, 128, 61), jnp.float32)], axis=-1
+    )
+    label_rows = jnp.stack([code_ids, variate_ids, segment_ids] + [segment_ids] * 5, axis=1)
+    bias = jnp.where(
+        jnp.arange(4)[None, :] == i, variate_bias.astype(jnp.float32).reshape(4, 4), 0.0
+    ).sum(axis=1)
+    output, input_grad, g_gate, g_up, g_down, g_qkv, g_out, small = layer(
+        [
+            tokens, cotangent, tables, label_rows.astype(jnp.float32), packed, w_out, w_gate, w_up, w_down,
+            gain_one, gain_two, bias,
+        ]
+    )
+    g_qkv = g_qkv.reshape(4, 256, 2, 64).transpose(1, 2, 0, 3).reshape(256, 512)[:, :384]
+    small = small.reshape(3, 1024)
+    return (
+        output, input_grad, g_qkv, g_out, g_gate, g_up, g_down, small[0], small[1], small[2, :16],
+    )
+
+
 def solution(mesh):
     in_specs = (
         P("dp", "seq", None),
@@ -386,6 +1512,7 @@
         P(),
         P(),
     )
+    grouped = mesh.shape["dp"] == 4 and mesh.shape["seq"] == 8
     return jax.shard_map(
-        on_device, mesh=mesh, in_specs=in_specs, out_specs=out_specs, check_vma=False
-    )
+        on_group if grouped else on_device, mesh=mesh, in_specs=in_specs, out_specs=out_specs, check_vma=False
+    )

time: 2230 us -> 371 us (0.17)
  waiting for transfers between devices: 1630 us -> 0 us
  Pallas kernels: 0 us -> 348 us
  starting transfers between devices: 201 us -> 0 us
  matrix products: 168 us -> 0 us
  other arithmetic: 65.9 us -> 4.45 us
  blocking collectives: 59.5 us -> 0 us
  local copies, waits for them, and re-layouts: 70.1 us -> 13.8 us
    reduce_scatter x10 -> x0, waiting for transfers between devices: 1110 us -> none  [the longest x1 281 us: reduce_last(): lax.psum_scatter(grads_full[4], 'seq', scatter_dimension=1, tiled=True)]
    pallas_call x0 -> x1, Pallas kernels: none -> 348 us  [layer(): pl.pallas_call(layer_kernel, out_shape=[bf16(2, 128, 1024), bf16(2, 128,...]
    all_gather x8 -> x0, waiting for transfers between devices: 286 us -> none  [the longest x1 119 us: fetch_weights(): lax.all_gather(row_blocks[4], 'seq', axis=1, tiled=True)]
    ppermute x48 -> x0, waiting for transfers between devices: 236 us -> none  [passed_along(): return lax.ppermute(block, axis, route)]
    ppermute x48 -> x0, starting transfers between devices: 200 us -> none  [passed_along(): return lax.ppermute(block, axis, route)]
    dot_general x37 -> x0, matrix products: 168 us -> none  [the longest x2 18.6 us: on_device(): jnp.einsum('td,fd->tf', grad_ffn, weights[4], preferred_element_type=jnp....]
    psum x1 -> x0, blocking collectives: 39.5 us -> none  [on_device(): lax.psum((bias_total, gain_one_total, gain_two_total), ('dp', 'seq'))]
    slice x19 -> x1, local copies, waits for them, and re-layouts: 38.1 us -> 0.03 us  [on_group(): g_qkv.reshape(4, 256, 2, 64).transpose(1, 2, 0, 3).reshape(256, 512)]
  transfers between devices with their start and end apart: 66 -> 0, of which waited for: 32 -> 0; matrix products, arithmetic and copies ran while one was open for 10% -> 0% of each run, Pallas kernels for 0% -> 0%
where the time goes in v3:
time: 371 us; the launch traced here: 367 us
  Pallas kernels  348 us (94%)
  local copies, waits for them, and re-layouts  13.8 us (4%)
  other arithmetic  4.45 us (1%)
    pallas_call x1, Pallas kernels, layer(): pl.pallas_call(layer_kernel, out_shape=[bf16(2, 128, 1024), bf16(2, 128,...  348 us
    unnamed x36, local copies, waits for them, and re-layouts  9.39 us

profile of v3, /device:TPU:0, one launch (start us, length us, event | category | flops | bytes accessed | tf_op | source)
XLA Modules:
  0.0 366.7 jit_solution(8776848850239961843)
XLA Ops:
  0.6 0.7 convert_element_type.14
  1.3 0.5 multiply_cosine_fusion
  2.0 0.5 copy-done.7
  2.6 0.7 copy-done.9
  3.5 0.8 maximum_maximum_fusion.refs_2_
  4.3 0.6 convert_element_type.16.refs_3_
  5.1 0.8 copy.30.refs_4_
  6.0 0.6 copy-done.13
  6.7 0.6 select_reduce_fusion.refs_11_
  7.4 0.6 broadcast_in_dim.41
  8.0 0.6 broadcast_in_dim.40
  8.6 347.7 %layer.1 = (bf16[2,128,1024]{2,1,0:T(8,128)(2,1)}, bf16[2,128,1024]{2,1,0:T(8,128)(2,1)}, f32[256,512]{1,0:T(8,128)}, f32[256,512]{1,0:T(8,128)}, f32[1024,128]{...) custom-call(bf16[2,128,1024]{2,1,0:T(8,128)(2,1)} %refs_0_.1, ...), custom_call_target="tpu_custom_call" | custom-call | tf_op jit(solution)/shard_map/layer/pallas_call | solution.py:1377
  356.3 1.3 slice_bitcast_fusion
  357.7 0.5 slice_bitcast_fusion.2
  358.2 1.2 copy.31
  359.5 0.9 copy.33
  360.6 0.8 copy.40
  361.3 0.4 copy-done.3
  361.8 0.8 copy.41
  362.8 0.7 copy.42
  363.4 0.8 copy.43
  364.7 0.8 copy.44
  365.5 0.4 copy-done
  365.9 0.8 copy.45
  (38 shorter events, 1.6 us)
Async XLA Ops:
  1.3 0.7 copy-start.12
  1.9 0.7 copy-start.7
  2.6 0.7 copy-start.9
  3.5 1.4 copy-start.5
  5.1 2.9 copy-start.11
  6.0 0.7 copy-start.13
  6.7 0.7 copy-start.10
  356.3 1.4 copy-start.8
  359.5 1.0 copy-start.4
  360.6 1.2 copy-start.3
  361.8 1.0 copy-start.6
  361.8 1.7 copy-start.2
  363.4 1.2 copy-start.1
  364.7 1.2 copy-start

commit v4 on v3

--- a/solution.py
+++ b/solution.py
@@ -610,14 +610,27 @@
             copy.wait()
 
 
+ARRIVAL = ((1, 2, 3), (2, 0, 3), (1, 3, 0), (2, 1, 0))
+LEAVING = ((2, 3, 1), (0, 2, 3), (3, 1, 0), (1, 0, 2))
+
+
+def pick(table, z, n):
+    row = [entry[n] for entry in table]
+    return jnp.where(z == 0, row[0], jnp.where(z == 1, row[1], jnp.where(z == 2, row[2], row[3])))
+
+
+def inner(z):
+    return (z == 1) | (z == 2)
+
+
 class SeqGather:
     def __init__(self, full, chunks, sems):
         self.full, self.chunks = full, chunks
-        self.s_z, self.r_z, self.s_y, self.r_y = sems
+        self.s_z, self.r_z, self.s_on, self.s_y, self.r_y = sems
 
     @staticmethod
     def sems(count):
-        return [DMA((count, 3)), DMA((count, 3)), DMA((count, 4)), DMA((count, 4))]
+        return [DMA((count, 2)), DMA((count, 4)), DMA((count, 4)), DMA((count, 4)), DMA((count, 4))]
 
     def block(self, chunk, z, y):
         start, size = self.chunks[chunk]
@@ -627,35 +640,59 @@
         i, j = place()
         z, y = j // 2, lax.rem(j, 2)
         own = self.block(chunk, z, y)
-        for dz in (2, 1, 3):
-            peer = at(i, 2 * lax.rem(z + dz, 4) + y)
-            send(own, own, self.s_z.at[chunk, dz - 1], self.r_z.at[chunk, dz - 1], peer).start()
-        send(own, own, self.s_y.at[chunk, 0], self.r_y.at[chunk, 0], at(i, 2 * z + 1 - y)).start()
-
-    def forward(self, chunk, dz):
+        first, second = pick(((2, 1), (2, 0), (1, 3), (1, 2)), z, 0), pick(
+            ((2, 1), (2, 0), (1, 3), (1, 2)), z, 1
+        )
+        for n, target in enumerate((first, second)):
+            peer = at(i, 2 * target + y)
+            send(own, own, self.s_z.at[chunk, n], self.r_z.at[chunk, z], peer).start()
+        send(own, own, self.s_y.at[chunk, z], self.r_y.at[chunk, z], at(i, 2 * z + 1 - y)).start()
+
+    def forward(self, chunk, n):
         i, j = place()
         z, y = j // 2, lax.rem(j, 2)
-        block = self.block(chunk, lax.rem(z + 4 - dz, 4), y)
-        landed(block, self.r_z.at[chunk, dz - 1])
+        source = pick(ARRIVAL, z, n)
+        block = self.block(chunk, source, y)
+        landed(block, self.r_z.at[chunk, source])
+
+        @pl.when(inner(z) & (source // 2 != z // 2) | inner(z) & inner(source))
+        def _():
+            send(
+                block,
+                block,
+                self.s_on.at[chunk, source],
+                self.r_z.at[chunk, source],
+                at(i, 2 * jnp.where(z == 1, 0, 3) + y),
+            ).start()
+
         peer = at(i, 2 * z + 1 - y)
-        send(block, block, self.s_y.at[chunk, dz], self.r_y.at[chunk, dz], peer).start()
-
-    def arrived(self, chunk, dz):
+        send(block, block, self.s_y.at[chunk, source], self.r_y.at[chunk, source], peer).start()
+
+    def arrived(self, chunk, source):
         _, j = place()
-        z, y = j // 2, lax.rem(j, 2)
-        landed(self.block(chunk, lax.rem(z + 4 - dz, 4), 1 - y), self.r_y.at[chunk, dz])
+        y = lax.rem(j, 2)
+        landed(self.block(chunk, source, 1 - y), self.r_y.at[chunk, source])
 
     def drain(self, chunk):
         _, j = place()
-        own = self.block(chunk, j // 2, lax.rem(j, 2))
-        for dz in (0, 1, 2, 3):
-            landed(own, self.s_y.at[chunk, dz])
-            if dz:
-                landed(own, self.s_z.at[chunk, dz - 1])
+        z = j // 2
+        own = self.block(chunk, z, lax.rem(j, 2))
+        for n in (0, 1):
+            landed(own, self.s_z.at[chunk, n])
+        landed(own, self.s_y.at[chunk, z])
+        for n in (0, 1, 2):
+            source = pick(ARRIVAL, z, n)
+            landed(own, self.s_y.at[chunk, source])
+
+            @pl.when(inner(z) & (source // 2 != z // 2) | inner(z) & inner(source))
+            def _():
+                landed(own, self.s_on.at[chunk, source])
 
     def finish(self, chunk):
-        for dz in (0, 1, 2, 3):
-            self.arrived(chunk, dz)
+        _, j = place()
+        self.arrived(chunk, j // 2)
+        for n in (0, 1, 2):
+            self.arrived(chunk, pick(ARRIVAL, j // 2, n))
         self.drain(chunk)
 
 
@@ -669,24 +706,29 @@
     def scratch(rows, count):
         return [
             pltpu.VMEM((4, rows, 128), jnp.bfloat16),
-            pltpu.VMEM((3, rows, 128), jnp.bfloat16),
+            pltpu.VMEM((4, rows, 128), jnp.bfloat16),
             DMA((count, 4)),
             DMA((count, 4)),
-            DMA((count, 3)),
-            DMA((count, 3)),
+            DMA((count, 4)),
+            DMA((count, 4)),
         ]
 
-    def start(self, chunk, dz):
+    def start(self, chunk, row):
         i, j = place()
         z, y = j // 2, lax.rem(j, 2)
         rows = pl.ds(*self.chunks[chunk])
         send(
-            self.parts.at[2 * lax.rem(z + dz, 4) + 1 - y, rows],
-            self.near.at[dz, rows],
-            self.s_y.at[chunk, dz],
-            self.r_y.at[chunk, dz],
+            self.parts.at[2 * row + 1 - y, rows],
+            self.near.at[row, rows],
+            self.s_y.at[chunk, row],
+            self.r_y.at[chunk, row],
             at(i, 2 * z + 1 - y),
         ).start()
+
+    def start_rest(self, chunk):
+        z = lax.axis_index("seq") // 2
+        for n in (0, 1, 2):
+            self.start(chunk, pick(LEAVING, z, n))
 
     def each(self, chunk, body):
         start, size = self.chunks[chunk]
@@ -695,49 +737,74 @@
         def _(t):
             body(pl.ds(pl.multiple_of(start + t * 256, 256), 256))
 
-    def cross(self, chunk, dz):
+    def cross(self, chunk, n):
         i, j = place()
         z, y = j // 2, lax.rem(j, 2)
         rows = pl.ds(*self.chunks[chunk])
-        target = lax.rem(z + dz, 4)
-        landed(self.near.at[dz, rows], self.r_y.at[chunk, dz])
+        row = pick(LEAVING, z, n)
+        landed(self.near.at[row, rows], self.r_y.at[chunk, row])
 
         def add(part):
-            both = self.parts[2 * target + y, part, :].astype(jnp.float32)
-            both = both + self.near[dz, part, :].astype(jnp.float32)
-            self.near[dz, part, :] = both.astype(jnp.bfloat16)
-
-        self.each(chunk, add)
+            both = self.parts[2 * row + y, part, :].astype(jnp.float32)
+            both = both + self.near[row, part, :].astype(jnp.float32)
+            self.near[row, part, :] = both.astype(jnp.bfloat16)
+
+        def add_more(part):
+            both = self.parts[2 * row + y, part, :].astype(jnp.float32)
+            both = both + self.near[row, part, :].astype(jnp.float32)
+            both = both + self.far[2 + lax.rem(row, 2), part, :].astype(jnp.float32)
+            self.near[row, part, :] = both.astype(jnp.bfloat16)
+
+        if n == 0:
+            self.each(chunk, add)
+        else:
+
+            @pl.when(inner(z))
+            def _():
+                held = 2 + lax.rem(row, 2)
+                landed(self.far.at[held, rows], self.r_z.at[chunk, held])
+                self.each(chunk, add_more)
+
+            @pl.when(jnp.logical_not(inner(z)))
+            def _():
+                self.each(chunk, add)
+
+        beside = jnp.where(z == 0, 1, 2)
+        target = jnp.where(inner(z), row, beside)
+        spot = jnp.where(target == row, z // 2, 2 + lax.rem(row, 2))
         send(
-            self.near.at[dz, rows],
-            self.far.at[dz - 1, rows],
-            self.s_z.at[chunk, dz - 1],
-            self.r_z.at[chunk, dz - 1],
+            self.near.at[row, rows],
+            self.far.at[spot, rows],
+            self.s_z.at[chunk, row],
+            self.r_z.at[chunk, spot],
             at(i, 2 * target + y),
         ).start()
 
     def finish(self, chunk):
         _, j = place()
+        z = j // 2
         rows = pl.ds(*self.chunks[chunk])
-        landed(self.near.at[0, rows], self.r_y.at[chunk, 0])
-        for dz in (1, 2, 3):
-            landed(self.far.at[dz - 1, rows], self.r_z.at[chunk, dz - 1])
+        landed(self.near.at[z, rows], self.r_y.at[chunk, z])
+        for spot in (0, 1):
+            landed(self.far.at[spot, rows], self.r_z.at[chunk, spot])
 
         def add(part):
             total = self.parts[j, part, :].astype(jnp.float32)
-            total = total + self.near[0, part, :].astype(jnp.float32)
-            for dz in (1, 2, 3):
-                total = total + self.far[dz - 1, part, :].astype(jnp.float32)
-            self.near[0, part, :] = total.astype(jnp.bfloat16)
+            total = total + self.near[z, part, :].astype(jnp.float32)
+            for spot in (0, 1):
+                total = total + self.far[spot, part, :].astype(jnp.float32)
+            self.near[z, part, :] = total.astype(jnp.bfloat16)
 
         self.each(chunk, add)
 
     def drain(self, chunk):
+        z = lax.axis_index("seq") // 2
         rows = pl.ds(*self.chunks[chunk])
-        for dz in (0, 1, 2, 3):
-            landed(self.near.at[dz, rows], self.s_y.at[chunk, dz])
-            if dz:
-                landed(self.near.at[dz, rows], self.s_z.at[chunk, dz - 1])
+        landed(self.near.at[z, rows], self.s_y.at[chunk, z])
+        for n in (0, 1, 2):
+            row = pick(LEAVING, z, n)
+            landed(self.near.at[row, rows], self.s_y.at[chunk, row])
+            landed(self.near.at[row, rows], self.s_z.at[chunk, row])
 
 
 class SmallSum:
@@ -751,32 +818,32 @@
             DMA((count,)) for count in (3, 3, 3, 3, 1, 1)
         ]
 
-    def run(self):
+    def round(self, stage):
         i, j = place()
         z, y = j // 2, lax.rem(j, 2)
-        rounds = (
-            (i, dp_peers()),
-            (z, seq_peers()[:3]),
-            (y, seq_peers()[3:]),
-        )
-        total = self.value[...]
-        for stage, (spot, peers) in enumerate(rounds):
-            held = self.stages[stage]
-            held[spot] = total
-            for step, peer in enumerate(peers):
-                send(
-                    held.at[spot],
-                    held.at[spot],
-                    self.sems[2 * stage].at[step],
-                    self.sems[2 * stage + 1].at[step],
-                    peer,
-                ).start()
-            for step in range(len(peers)):
-                landed(held.at[0], self.sems[2 * stage + 1].at[step])
-                landed(held.at[0], self.sems[2 * stage].at[step])
-            total = held[0]
-            for index in range(1, held.shape[0]):
-                total = total + held[index]
+        return ((i, dp_peers()), (z, seq_peers()[:3]), (y, seq_peers()[3:]))[stage]
+
+    def start(self, stage):
+        spot, peers = self.round(stage)
+        held = self.stages[stage]
+        held[spot] = self.value[...] if stage == 0 else self.total(stage - 1)
+        for step, peer in enumerate(peers):
+            send(
+                held.at[spot],
+                held.at[spot],
+                self.sems[2 * stage].at[step],
+                self.sems[2 * stage + 1].at[step],
+                peer,
+            ).start()
+
+    def total(self, stage):
+        held = self.stages[stage]
+        for step in range(held.shape[0] - 1):
+            landed(held.at[0], self.sems[2 * stage + 1].at[step])
+            landed(held.at[0], self.sems[2 * stage].at[step])
+        total = held[0]
+        for index in range(1, held.shape[0]):
+            total = total + held[index]
         return total
 
 
@@ -906,7 +973,6 @@
 FFN_CHUNKS = ((2048, 1024), (0, 2048))
 GRAD_CHUNKS = ((0, 2048), (2048, 1024))
 ATTENTION_CHUNKS = ((0, 1024), (1024, 256))
-ARRIVAL = (2, 1, 3)
 
 
 def wide(ref, first, rows):
@@ -945,9 +1011,9 @@
     sum_sems, refs = [refs[4 * n : 4 * n + 4] for n in range(4)], refs[16:]
     spread_a, spread_f, back_a, back_f = [refs[3 * n : 3 * n + 3] for n in range(4)]
     refs = refs[12:]
-    chain_a, chain_f, refs = refs[:4], refs[4:8], refs[8:]
+    chain_a, chain_f, refs = refs[:5], refs[5:10], refs[10:]
     fold_f, fold_a, refs = refs[:6], refs[6:12], refs[12:]
-    small_scratch = refs
+    small_scratch, out_sem = refs[:-1], refs[-1]
 
     i, j = place()
     z, y = j // 2, lax.rem(j, 2)
@@ -973,14 +1039,14 @@
     leave = Home((out_own, in_own), (output, input_grad), home_out, True)
     ffn_fold = SeqSum(ffn_g, GRAD_CHUNKS, fold_f)
     attn_fold = SeqSum(attn_all, ATTENTION_CHUNKS, fold_a)
-    ffn_back = Exchange(return_ffn(fold_f[0].at[0], r_gate, r_up, r_down), back_f)
-    attn_back = Exchange(return_attention(fold_a[0].at[0], r_qkv, r_out), back_a)
+    ffn_back = Exchange(return_ffn(fold_f[0].at[z], r_gate, r_up, r_down), back_f)
+    attn_back = Exchange(return_attention(fold_a[0].at[z], r_qkv, r_out), back_a)
 
     meet(dp_peers() + seq_peers(), home=True)
+    spread.start()
     for a in (0, 1, 2):
         for s in (0, 1):
             home.start(a, s)
-    spread.start()
     spread_ffn.start()
     spread.wait()
     attn_w.start(0)
@@ -988,13 +1054,15 @@
         for s in (0, 1):
             home.wait(a, s)
             group.push(a, s)
+    for s in (0, 1):
+        tok_own[s] = tok_all[owned(i, s)]
+    for n in (0, 1, 2):
+        attn_w.forward(0, n)
+    for s in (0, 1):
+        home.start(3, s)
     spread_ffn.wait()
     ffn_w.start(0)
-    for s in (0, 1):
-        home.start(3, s)
     ffn_w.start(1)
-    for s in (0, 1):
-        tok_own[s] = tok_all[owned(i, s)]
     for a in (0, 1, 2):
         for s in (0, 1):
             group.relay(a, s)
@@ -1010,8 +1078,6 @@
         tok_all[b] = (hidden * norm_rows(hidden) * gain_one[...]).astype(jnp.bfloat16)
 
     a1_all = tok_all
-    for dz in ARRIVAL:
-        attn_w.forward(0, dz)
     attn_w.finish(0)
     head_weights(attn_all, wh_ref, wm_ref, low_half)
 
@@ -1064,14 +1130,23 @@
             def _():
                 branch.cross(s)
 
-        @pl.when(u == 1)
+        @pl.when(u == 0)
         def _():
-            for dz in ARRIVAL:
-                ffn_w.forward(0, dz)
-
-    for s in (0, 1):
-        home.wait(3, s)
-        group.push(3, s)
+            for s in (0, 1):
+                home.wait(3, s)
+                group.push(3, s)
+
+        @pl.when(u == 3)
+        def _():
+            for s in (0, 1):
+                group.relay(3, s)
+
+        for n in (0, 1, 2):
+
+            @pl.when(u == n + 1)
+            def _():
+                ffn_w.forward(0, n)
+
     for s in (0, 1):
         block = owned(i, s)
         mid = tok_own[s].astype(jnp.float32) + branch.total(s)
@@ -1079,12 +1154,9 @@
         a2_all[block] = (mid * norm_rows(mid) * gain_two[...]).astype(jnp.bfloat16)
         second.push(0, s)
     branch.finish()
-    ffn_w.forward(1, 2)
-    for s in (0, 1):
-        group.relay(3, s)
+    ffn_w.forward(1, 0)
     for s in (0, 1):
         second.relay(0, s)
-    ffn_w.forward(1, 1)
     group.finish(3)
     home.finish(3)
     second.finish(0)
@@ -1097,8 +1169,7 @@
                 two(a2_all, t, slice(256 * d, 256 * d + 256)).T.reshape(2, 128, 256)
             )
 
-    def unit(dz):
-        f = lax.rem(z + 4 - dz, 4)
+    def unit(f):
         cols = pl.ds(pl.multiple_of(256 * f, 256), 256)
         wg, wu = wide(ffn_all, 2 * f, slice(0, 1024)), wide(ffn_all, 2 * f, slice(1024, 2048))
         down = pl.ds(pl.multiple_of(2048 + 256 * f, 256), 256)
@@ -1132,24 +1203,25 @@
 
     @pl.loop(0, 4)
     def _(step):
-        dz = jnp.where(step == 1, 2, jnp.where(step == 2, 1, step))
-        for n, here in enumerate((0, 2, 1, 3)):
-
-            @pl.when(step == n)
+        f = z
+        for n in (0, 1, 2):
+            f = jnp.where(step == n + 1, pick(ARRIVAL, z, n), f)
+        ffn_w.arrived(1, f)
+        for n in (1, 2):
+
+            @pl.when(step == n - 1)
             def _():
-                if n == 3:
-                    ffn_w.forward(1, 3)
-                ffn_w.arrived(1, here)
-
-        unit(dz)
-        for n, there in enumerate((0, 2, 3, 1)):
-
-            @pl.when(step == n)
-            def _():
-                ffn_fold.start(0, there)
-
-    for dz in (2, 3, 1, 0):
-        ffn_fold.start(1, dz)
+                ffn_w.forward(1, n)
+
+        unit(f)
+
+        @pl.when(step > 0)
+        def _():
+            ffn_fold.start(0, f)
+
+    ffn_fold.start_rest(1)
+    ffn_fold.start(0, z)
+    ffn_fold.start(1, z)
     ffn_w.drain(1)
 
     def product(left, t, first_row):
@@ -1205,13 +1277,14 @@
         third.push(0, s)
     for b in range(8):
         small[8 + b : 9 + b, :] = gain_rows[:, 128 * b : 128 * b + 128]
+    da_sum.finish()
+    ffn_fold.cross(0, 0)
     for s in (0, 1):
         out_sum.cross(s)
-    da_sum.finish()
-    ffn_fold.cross(0, 2)
     for s in (0, 1):
         third.relay(0, s)
     third.finish(0)
+    ffn_fold.cross(0, 1)
 
     @pl.loop(0, 4)
     def _(t):
@@ -1222,9 +1295,8 @@
     for d in range(4):
         ez = ez_all[:, :, 256 * d : 256 * d + 256].reshape(1024, 256)
         store_wide(attn_all, 2 * d, slice(1024, 1280), dot(o_ref[...], ez, TN, jnp.bfloat16))
-    for dz in (2, 3, 1, 0):
-        attn_fold.start(1, dz)
-    ffn_fold.cross(0, 3)
+    attn_fold.start_rest(1)
+    attn_fold.start(1, z)
     for s in (0, 1):
         out_own[s] = (mid_ref[s] + out_sum.total(s)).astype(jnp.bfloat16)
         leave.start(0, s)
@@ -1273,11 +1345,19 @@
 
         @pl.when(t == 0)
         def _():
-            ffn_fold.cross(0, 1)
+            ffn_fold.cross(1, 0)
+
+        @pl.when(t == 1)
+        def _():
+            ffn_fold.cross(0, 2)
 
         @pl.when(t == 2)
         def _():
-            ffn_fold.cross(1, 2)
+            ffn_fold.cross(1, 1)
+
+        @pl.when(t == 3)
+        def _():
+            attn_fold.cross(1, 0)
 
     @pl.loop(0, 4)
     def _(t):
@@ -1296,10 +1376,8 @@
             attn_all[b, block, :] = jnp.concatenate(
                 [slot_columns(grads, 2 * b + e, low_half) for e in (0, 1)], axis=1
             ).astype(jnp.bfloat16)
-    for dz in (2, 3, 1, 0):
-        attn_fold.start(0, dz)
-    for dz in (3, 1):
-        ffn_fold.cross(1, dz)
+    attn_fold.start_rest(0)
+    attn_fold.start(0, z)
 
     @pl.loop(0, 4)
     def _(u):
@@ -1317,8 +1395,13 @@
             def _():
                 da1_sum.cross(s)
 
-    for dz in (2, 3, 1):
-        attn_fold.cross(1, dz)
+    ffn_fold.cross(1, 2)
+    attn_fold.cross(1, 1)
+    attn_fold.cross(0, 0)
+    attn_fold.cross(1, 2)
+    for chunk in (0, 1):
+        ffn_fold.finish(chunk)
+    ffn_back.start()
     gain_rows = jnp.zeros((1, 1024), jnp.float32)
     for s in (0, 1):
         hidden = tok_own[s].astype(jnp.float32)
@@ -1327,7 +1410,6 @@
         gain_rows = gain_rows + jnp.sum(da1 * (hidden * inv), axis=0, keepdims=True)
         grad = e2_ref[s] + back_rows(da1 * gain_one[...], hidden, inv)
         in_own[s] = grad.astype(jnp.bfloat16)
-        leave.start(1, s)
     for b in range(8):
         small[b : b + 1, :] = gain_rows[:, 128 * b : 128 * b + 128]
     lane = lax.broadcasted_iota(jnp.int32, (8, 128), 1)
@@ -1337,20 +1419,33 @@
         value = jnp.sum(dbias[h : h + 1, :], axis=1, keepdims=True)
         bias_row = jnp.where((line == 0) & (lane == 4 * h + i), value, bias_row)
     small[16:24, :] = bias_row
-
-    for chunk in (0, 1):
-        ffn_fold.finish(chunk)
-    ffn_back.start()
-    small_out[...] = SmallSum(small, small_scratch).run()
-    for dz in (2, 3, 1):
-        attn_fold.cross(0, dz)
-    ffn_back.wait()
-    g_gate[...] = r_gate[...].astype(jnp.float32)
-    g_up[...] = r_up[...].astype(jnp.float32)
-    g_down[...] = r_down[...].astype(jnp.float32)
+    small_sum = SmallSum(small, small_scratch)
+    small_sum.start(0)
+    attn_fold.cross(0, 1)
+    attn_fold.cross(0, 2)
+    small_sum.start(1)
+    for s in (0, 1):
+        leave.start(1, s)
     for chunk in (1, 0):
         attn_fold.finish(chunk)
     attn_back.start()
+    small_sum.start(2)
+    ffn_back.wait()
+    copies = []
+    for start, source, target in ((0, r_gate, g_gate), (512, r_up, g_up)):
+        for half in (0, 1):
+            cols = slice(256 * half, 256 * half + 256)
+            rows = slice(start + 256 * half, start + 256 * half + 256)
+            dv_acc[rows, :] = source[:, cols].astype(jnp.float32)
+            copies.append((dv_acc.at[rows], target.at[:, cols]))
+    dk_acc[:, 0:128] = r_down[...].astype(jnp.float32)
+    copies.append((dk_acc.at[:, 0:128], g_down))
+    copies = [
+        pltpu.make_async_copy(src, dst, out_sem.at[index]) for index, (src, dst) in enumerate(copies)
+    ]
+    for copy in copies:
+        copy.start()
+    small_out[...] = small_sum.total(2)
     out_sum.finish()
     da1_sum.finish()
     for a in (0, 1):
@@ -1363,6 +1458,8 @@
     attn_back.wait()
     g_qkv[...] = r_qkv[...].astype(jnp.float32)
     g_out[...] = r_out[...].astype(jnp.float32)
+    for copy in copies:
+        copy.wait()
 
 
 def layer(arrays):
@@ -1387,7 +1484,7 @@
             f32(24, 128),
         ],
         in_specs=[HB, HB, VM, VM, VM, VM, HB, HB, HB, VM, VM, SM],
-        out_specs=[HB] * 2 + [VM] * 6,
+        out_specs=[HB] * 5 + [VM] * 3,
         scratch_shapes=[
             blocks,
             blocks,
@@ -1442,7 +1539,8 @@
         + SeqGather.sems(2)
         + SeqSum.scratch(3072, 2)
         + SeqSum.scratch(1280, 2)
-        + SmallSum.scratch((24, 128)),
+        + SmallSum.scratch((24, 128))
+        + [DMA((5,))],
         compiler_params=pltpu.CompilerParams(
             collective_id=1, has_side_effects=True, vmem_limit_bytes=67_043_328
         ),

time: 371 us -> 296 us (0.80)
  Pallas kernels: 348 us -> 276 us
    pallas_call x1, Pallas kernels: 348 us -> 276 us  [layer(): pl.pallas_call(layer_kernel, out_shape=[bf16(2, 128, 1024), bf16(2, 128,...]
where the time goes in v4:
time: 296 us; the launch traced here: 295 us
  Pallas kernels  276 us (93%)
  local copies, waits for them, and re-layouts  13.8 us (5%)
  other arithmetic  4.45 us (2%)
    pallas_call x1, Pallas kernels, layer(): pl.pallas_call(layer_kernel, out_shape=[bf16(2, 128, 1024), bf16(2, 128,...  276 us
    unnamed x36, local copies, waits for them, and re-layouts  9.39 us

profile of v4, /device:TPU:0, one launch (start us, length us, event | category | flops | bytes accessed | tf_op | source)
XLA Modules:
  0.0 294.7 jit_solution(1032655460701694888)
XLA Ops:
  0.6 0.7 convert_element_type.14
  1.3 0.5 multiply_cosine_fusion
  2.0 0.5 copy-done.7
  2.6 0.7 copy-done.9
  3.5 0.8 maximum_maximum_fusion.refs_2_
  4.3 0.6 convert_element_type.16.refs_3_
  5.1 0.8 copy.30.refs_4_
  6.0 0.6 copy-done.13
  6.7 0.6 select_reduce_fusion.refs_11_
  7.4 0.6 broadcast_in_dim.41
  8.0 0.6 broadcast_in_dim.40
  8.6 275.7 %layer.1 = (bf16[2,128,1024]{2,1,0:T(8,128)(2,1)}, bf16[2,128,1024]{2,1,0:T(8,128)(2,1)}, f32[256,512]{1,0:T(8,128)}, f32[256,512]{1,0:T(8,128)}, f32[1024,128]{...) custom-call(bf16[2,128,1024]{2,1,0:T(8,128)(2,1)} %refs_0_.1, ...), custom_call_target="tpu_custom_call" | custom-call | tf_op jit(solution)/shard_map/layer/pallas_call | solution.py:1474
  284.3 1.3 slice_bitcast_fusion
  285.6 0.5 slice_bitcast_fusion.2
  286.1 1.2 copy.31
  287.5 0.9 copy.33
  288.5 0.8 copy.40
  289.3 0.4 copy-done.3
  289.7 0.8 copy.41
  290.7 0.7 copy.42
  291.4 0.8 copy.43
  292.6 0.8 copy.44
  293.4 0.4 copy-done
  293.9 0.8 copy.45
  (38 shorter events, 1.6 us)
Async XLA Ops:
  1.3 0.7 copy-start.12
  1.9 0.7 copy-start.7
  2.6 0.7 copy-start.9
  3.5 1.4 copy-start.5
  5.1 2.9 copy-start.11
  6.0 0.7 copy-start.13
  6.7 0.7 copy-start.10
  284.3 1.4 copy-start.8
  287.5 1.0 copy-start.4
  288.5 1.2 copy-start.3
  289.7 1.0 copy-start.6
  289.7 1.7 copy-start.2
  291.4 1.2 copy-start.1
  292.6 1.2 copy-start

commit v5 on v4

--- a/solution.py
+++ b/solution.py
@@ -384,12 +384,21 @@
     return lax.dot_general(a, b, dims, preferred_element_type=jnp.float32).astype(out)
 
 
-def at(dp, seq):
-    return {"dp": dp, "seq": seq}
+def at(i, j):
+    return {"dp": 2 * lax.rem(j, 2) + lax.rem(i, 2), "seq": 2 * (j // 2) + i // 2}
 
 
 def place():
-    return lax.axis_index("dp"), lax.axis_index("seq")
+    dp, seq = lax.axis_index("dp"), lax.axis_index("seq")
+    return 2 * lax.rem(seq, 2) + lax.rem(dp, 2), 2 * (seq // 2) + dp // 2
+
+
+def row_block(i, j):
+    return 2 * lax.rem(j, 2) + lax.rem(i, 2)
+
+
+def column_block(i, j):
+    return 2 * (j // 2) + i // 2
 
 
 def ring(i):
@@ -400,8 +409,12 @@
     return 4 * lax.rem(i, 2) + 2 * s + i // 2
 
 
-def keeper(j):
-    return 2 * lax.rem(j, 2) + j // 4
+def keeper(i, j):
+    return 2 * (i // 2) + j // 4
+
+
+def taker(i, j, s):
+    return 4 * lax.rem(i, 2) + 2 * s + lax.rem(j, 2)
 
 
 def send(src, dst, send_sem, recv_sem, peer):
@@ -425,13 +438,13 @@
     for peer in peers:
         pl.semaphore_signal(barrier, inc=1, device_id=peer, device_id_type=MESH)
     if home:
-        target, stays = keeper(j), keeper(j) == i
+        target, stays = keeper(i, j), keeper(i, j) == i
         for s in (0, 1):
 
-            @pl.when(jnp.logical_not(stays & (owned(i, s) == j)))
+            @pl.when(jnp.logical_not(stays & (taker(i, j, s) == j)))
             def _():
                 pl.semaphore_signal(
-                    barrier, inc=1, device_id=at(target, owned(i, s)), device_id_type=MESH
+                    barrier, inc=1, device_id=at(target, taker(i, j, s)), device_id_type=MESH
                 )
 
         pl.semaphore_wait(barrier, len(peers) + jnp.where(stays, 1, 2))
@@ -466,12 +479,12 @@
     def start(self, a, s):
         i, j = place()
         slot = lax.rem(j // 2, 2)
-        src, dst = self.ins[a].at[s], self.outs[a].at[slot if self.slotted else j]
-        here = (keeper(j) == i) & (owned(i, s) == j)
+        src, dst = self.ins[a].at[s], self.outs[a].at[slot if self.slotted else column_block(i, j)]
+        here = (keeper(i, j) == i) & (taker(i, j, s) == j)
 
         @pl.when(jnp.logical_not(here))
         def _():
-            peer = at(keeper(j), owned(i, s))
+            peer = at(keeper(i, j), taker(i, j, s))
             send(src, dst, self.send_sem.at[a, s], self.recv_sem.at[a, slot], peer).start()
 
         @pl.when(here)
@@ -485,7 +498,7 @@
         i, j = place()
         for s in (0, 1):
 
-            @pl.when(jnp.logical_not((keeper(j) == i) & (owned(i, s) == j)))
+            @pl.when(jnp.logical_not((keeper(i, j) == i) & (taker(i, j, s) == j)))
             def _():
                 landed(self.ins[a].at[s], self.send_sem.at[a, s])
 
@@ -513,12 +526,22 @@
         landed(block, self.r_x.at[a, s])
         send(block, block, self.s_on.at[a, s], self.r_on.at[a, s], at(core, j)).start()
 
-    def finish(self, a):
-        i, _ = place()
-        core, _ = ring(i)
+    def near(self, a):
+        core, _ = ring(place()[0])
         for s in (0, 1):
             landed(self.outs[a].at[owned(core, s)], self.r_core.at[a, s])
+
+    def beyond(self, a):
+        core, _ = ring(place()[0])
+        for s in (0, 1):
             landed(self.outs[a].at[owned(lax.rem(core + 2, 4), s)], self.r_on.at[a, s])
+
+    def finish(self, a):
+        self.near(a)
+        self.beyond(a)
+        self.sent(a)
+
+    def sent(self, a):
         for s in (0, 1):
             for sem in (self.s_x, self.s_core, self.s_on):
                 landed(self.outs[a].at[s], sem.at[a, s])
@@ -576,11 +599,14 @@
                 landed(self.near.at[side, s], self.s_core.at[side, s])
 
 
+def when(condition):
+    return (lambda body: body()) if condition is None else pl.when(condition)
+
+
 class Exchange:
     def __init__(self, pieces, sems):
         self.pieces = pieces
         self.send_sem, self.recv_sem, self.own_sem = sems
-        self.copies = []
 
     @staticmethod
     def sems(count):
@@ -590,28 +616,49 @@
         i, j = place()
         for step in (2, 3, 1):
             other = lax.rem(i + step, 4)
-            for index, (src, dst) in enumerate(self.pieces(i, other)):
-                copy = send(
-                    src,
-                    dst,
-                    self.send_sem.at[step - 1, index],
-                    self.recv_sem.at[step - 1, index],
-                    at(other, j),
-                )
-                copy.start()
-                self.copies.append(copy)
-        for index, (src, dst) in enumerate(self.pieces(i, i)):
-            copy = pltpu.make_async_copy(src, dst, self.own_sem.at[index])
-            copy.start()
-            self.copies.append(copy)
+            for index, (src, dst, sends, _) in enumerate(self.pieces(i, other)):
+
+                @when(sends)
+                def _():
+                    send(
+                        src,
+                        dst,
+                        self.send_sem.at[step - 1, index],
+                        self.recv_sem.at[step - 1, index],
+                        at(other, j),
+                    ).start()
+
+        for index, (src, dst, sends, _) in enumerate(self.pieces(i, i)):
+
+            @when(sends)
+            def _():
+                pltpu.make_async_copy(src, dst, self.own_sem.at[index]).start()
 
     def wait(self):
-        for copy in self.copies:
-            copy.wait()
+        i, _ = place()
+        for step in (2, 3, 1):
+            there, source = lax.rem(i + step, 4), lax.rem(i + 4 - step, 4)
+            for index, (src, _, sends, _) in enumerate(self.pieces(i, there)):
+
+                @when(sends)
+                def _():
+                    landed(src, self.send_sem.at[step - 1, index])
+
+            for index, (src, _, _, gets) in enumerate(self.pieces(i, source)):
+
+                @when(gets)
+                def _():
+                    landed(src, self.recv_sem.at[step - 1, index])
+
+        for index, (src, _, sends, _) in enumerate(self.pieces(i, i)):
+
+            @when(sends)
+            def _():
+                landed(src, self.own_sem.at[index])
 
 
 ARRIVAL = ((1, 2, 3), (2, 0, 3), (1, 3, 0), (2, 1, 0))
-LEAVING = ((2, 3, 1), (0, 2, 3), (3, 1, 0), (1, 0, 2))
+LEAVING = ((1, 2, 3), (0, 2, 3), (3, 1, 0), (2, 1, 0))
 
 
 def pick(table, z, n):
@@ -624,187 +671,172 @@
 
 
 class SeqGather:
-    def __init__(self, full, chunks, sems):
-        self.full, self.chunks = full, chunks
+    def __init__(self, blocks, sems):
+        self.blocks = blocks
         self.s_z, self.r_z, self.s_on, self.s_y, self.r_y = sems
 
     @staticmethod
     def sems(count):
         return [DMA((count, 2)), DMA((count, 4)), DMA((count, 4)), DMA((count, 4)), DMA((count, 4))]
 
-    def block(self, chunk, z, y):
-        start, size = self.chunks[chunk]
-        return self.full.at[2 * z + y, pl.ds(start, size)]
-
-    def start(self, chunk):
+    def relays(self, source):
+        z = place()[1] // 2
+        return inner(z) & ((source // 2 != z // 2) | inner(source))
+
+    def start_z(self, chunk):
         i, j = place()
-        z, y = j // 2, lax.rem(j, 2)
-        own = self.block(chunk, z, y)
-        first, second = pick(((2, 1), (2, 0), (1, 3), (1, 2)), z, 0), pick(
-            ((2, 1), (2, 0), (1, 3), (1, 2)), z, 1
-        )
-        for n, target in enumerate((first, second)):
-            peer = at(i, 2 * target + y)
+        z, x = j // 2, lax.rem(j, 2)
+        own = self.blocks[chunk](z, x)
+        targets = [pick(((2, 1), (2, 0), (1, 3), (1, 2)), z, n) for n in (0, 1)]
+        for n, target in enumerate(targets):
+            peer = at(i, 2 * target + x)
             send(own, own, self.s_z.at[chunk, n], self.r_z.at[chunk, z], peer).start()
-        send(own, own, self.s_y.at[chunk, z], self.r_y.at[chunk, z], at(i, 2 * z + 1 - y)).start()
+
+    def start_y(self, chunk):
+        i, j = place()
+        z, x = j // 2, lax.rem(j, 2)
+        own = self.blocks[chunk](z, x)
+        peer = at(i, 2 * z + 1 - x)
+        send(own, own, self.s_y.at[chunk, z], self.r_y.at[chunk, z], peer).start()
+
+    def relayed(self, chunk):
+        _, j = place()
+        z, x = j // 2, lax.rem(j, 2)
+        own = self.blocks[chunk](z, x)
+        for n in (0, 1):
+            landed(own, self.s_z.at[chunk, n])
+        for n in (0, 1, 2):
+            source = pick(ARRIVAL, z, n)
+
+            @pl.when(self.relays(source))
+            def _():
+                landed(own, self.s_on.at[chunk, source])
 
     def forward(self, chunk, n):
         i, j = place()
-        z, y = j // 2, lax.rem(j, 2)
+        z, x = j // 2, lax.rem(j, 2)
         source = pick(ARRIVAL, z, n)
-        block = self.block(chunk, source, y)
+        block = self.blocks[chunk](source, x)
         landed(block, self.r_z.at[chunk, source])
 
-        @pl.when(inner(z) & (source // 2 != z // 2) | inner(z) & inner(source))
+        @pl.when(self.relays(source))
         def _():
+            peer = at(i, 2 * jnp.where(z == 1, 0, 3) + x)
             send(
-                block,
-                block,
-                self.s_on.at[chunk, source],
-                self.r_z.at[chunk, source],
-                at(i, 2 * jnp.where(z == 1, 0, 3) + y),
+                block, block, self.s_on.at[chunk, source], self.r_z.at[chunk, source], peer
             ).start()
 
-        peer = at(i, 2 * z + 1 - y)
+        peer = at(i, 2 * z + 1 - x)
         send(block, block, self.s_y.at[chunk, source], self.r_y.at[chunk, source], peer).start()
 
     def arrived(self, chunk, source):
-        _, j = place()
-        y = lax.rem(j, 2)
-        landed(self.block(chunk, source, 1 - y), self.r_y.at[chunk, source])
+        x = lax.rem(place()[1], 2)
+        landed(self.blocks[chunk](source, 1 - x), self.r_y.at[chunk, source])
 
     def drain(self, chunk):
         _, j = place()
-        z = j // 2
-        own = self.block(chunk, z, lax.rem(j, 2))
-        for n in (0, 1):
-            landed(own, self.s_z.at[chunk, n])
+        z, x = j // 2, lax.rem(j, 2)
+        own = self.blocks[chunk](z, x)
         landed(own, self.s_y.at[chunk, z])
         for n in (0, 1, 2):
-            source = pick(ARRIVAL, z, n)
-            landed(own, self.s_y.at[chunk, source])
-
-            @pl.when(inner(z) & (source // 2 != z // 2) | inner(z) & inner(source))
+            landed(own, self.s_y.at[chunk, pick(ARRIVAL, z, n)])
+
+    def finish(self, chunk):
+        z = place()[1] // 2
+        self.arrived(chunk, z)
+        for n in (0, 1, 2):
+            self.arrived(chunk, pick(ARRIVAL, z, n))
+        self.drain(chunk)
+
+
+class SeqSum:
+    def __init__(self, parts, near, far, sems):
+        self.parts, self.near, self.far = parts, near, far
+        self.s_y, self.r_y, self.s_z, self.r_z = sems
+
+    @staticmethod
+    def sems(count):
+        return [DMA((count, 4)) for _ in range(4)]
+
+    def start(self, chunk, row):
+        i, j = place()
+        z, x = j // 2, lax.rem(j, 2)
+        send(
+            self.parts[chunk](row, 1 - x),
+            self.near[chunk](row),
+            self.s_y.at[chunk, row],
+            self.r_y.at[chunk, row],
+            at(i, 2 * z + 1 - x),
+        ).start()
+
+    def start_rest(self, chunk):
+        z = place()[1] // 2
+        for n in (0, 1, 2):
+            self.start(chunk, pick(LEAVING, z, n))
+
+    def add(self, target, terms):
+        if len(target.shape) == 3:
+            for e in range(target.shape[0]):
+                self.add(target.at[e], [term.at[e] for term in terms])
+            return
+        rows = target.shape[0]
+        step = min(256, rows)
+
+        @pl.loop(0, rows // step)
+        def _(t):
+            part = pl.ds(pl.multiple_of(t * step, step), step)
+            total = target[part, :].astype(jnp.float32)
+            for term in terms:
+                total = total + term[part, :].astype(jnp.float32)
+            target[part, :] = total.astype(jnp.bfloat16)
+
+    def cross(self, chunk, n):
+        i, j = place()
+        z, x = j // 2, lax.rem(j, 2)
+        row = pick(LEAVING, z, n)
+        held = 2 + lax.rem(row, 2)
+        near, own, far = self.near[chunk](row), self.parts[chunk](row, x), self.far[chunk](held)
+        landed(near, self.r_y.at[chunk, row])
+        if n == 0:
+            self.add(near, (own,))
+        else:
+
+            @pl.when(inner(z))
             def _():
-                landed(own, self.s_on.at[chunk, source])
+                landed(far, self.r_z.at[chunk, held])
+                self.add(near, (own, far))
+
+            @pl.when(jnp.logical_not(inner(z)))
+            def _():
+                self.add(near, (own,))
+
+        target = jnp.where(inner(z), row, jnp.where(z == 0, 1, 2))
+        spot = jnp.where(target == row, z // 2, held)
+        send(
+            near,
+            self.far[chunk](spot),
+            self.s_z.at[chunk, row],
+            self.r_z.at[chunk, spot],
+            at(i, 2 * target + x),
+        ).start()
 
     def finish(self, chunk):
         _, j = place()
-        self.arrived(chunk, j // 2)
-        for n in (0, 1, 2):
-            self.arrived(chunk, pick(ARRIVAL, j // 2, n))
-        self.drain(chunk)
-
-
-class SeqSum:
-    def __init__(self, parts, chunks, scratch):
-        self.parts, self.chunks = parts, chunks
-        self.near, self.far = scratch[:2]
-        self.s_y, self.r_y, self.s_z, self.r_z = scratch[2:]
-
-    @staticmethod
-    def scratch(rows, count):
-        return [
-            pltpu.VMEM((4, rows, 128), jnp.bfloat16),
-            pltpu.VMEM((4, rows, 128), jnp.bfloat16),
-            DMA((count, 4)),
-            DMA((count, 4)),
-            DMA((count, 4)),
-            DMA((count, 4)),
-        ]
-
-    def start(self, chunk, row):
-        i, j = place()
-        z, y = j // 2, lax.rem(j, 2)
-        rows = pl.ds(*self.chunks[chunk])
-        send(
-            self.parts.at[2 * row + 1 - y, rows],
-            self.near.at[row, rows],
-            self.s_y.at[chunk, row],
-            self.r_y.at[chunk, row],
-            at(i, 2 * z + 1 - y),
-        ).start()
-
-    def start_rest(self, chunk):
-        z = lax.axis_index("seq") // 2
-        for n in (0, 1, 2):
-            self.start(chunk, pick(LEAVING, z, n))
-
-    def each(self, chunk, body):
-        start, size = self.chunks[chunk]
-
-        @pl.loop(0, size // 256)
-        def _(t):
-            body(pl.ds(pl.multiple_of(start + t * 256, 256), 256))
-
-    def cross(self, chunk, n):
-        i, j = place()
-        z, y = j // 2, lax.rem(j, 2)
-        rows = pl.ds(*self.chunks[chunk])
-        row = pick(LEAVING, z, n)
-        landed(self.near.at[row, rows], self.r_y.at[chunk, row])
-
-        def add(part):
-            both = self.parts[2 * row + y, part, :].astype(jnp.float32)
-            both = both + self.near[row, part, :].astype(jnp.float32)
-            self.near[row, part, :] = both.astype(jnp.bfloat16)
-
-        def add_more(part):
-            both = self.parts[2 * row + y, part, :].astype(jnp.float32)
-            both = both + self.near[row, part, :].astype(jnp.float32)
-            both = both + self.far[2 + lax.rem(row, 2), part, :].astype(jnp.float32)
-            self.near[row, part, :] = both.astype(jnp.bfloat16)
-
-        if n == 0:
-            self.each(chunk, add)
-        else:
-
-            @pl.when(inner(z))
-            def _():
-                held = 2 + lax.rem(row, 2)
-                landed(self.far.at[held, rows], self.r_z.at[chunk, held])
-                self.each(chunk, add_more)
-
-            @pl.when(jnp.logical_not(inner(z)))
-            def _():
-                self.each(chunk, add)
-
-        beside = jnp.where(z == 0, 1, 2)
-        target = jnp.where(inner(z), row, beside)
-        spot = jnp.where(target == row, z // 2, 2 + lax.rem(row, 2))
-        send(
-            self.near.at[row, rows],
-            self.far.at[spot, rows],
-            self.s_z.at[chunk, row],
-            self.r_z.at[chunk, spot],
-            at(i, 2 * target + y),
-        ).start()
-
-    def finish(self, chunk):
+        z, x = j // 2, lax.rem(j, 2)
+        near, far = self.near[chunk](z), [self.far[chunk](spot) for spot in (0, 1)]
+        landed(near, self.r_y.at[chunk, z])
+        for spot in (0, 1):
+            landed(far[spot], self.r_z.at[chunk, spot])
+        self.add(near, (self.parts[chunk](z, x), *far))
+
+    def drain(self, chunk):
         _, j = place()
-        z = j // 2
-        rows = pl.ds(*self.chunks[chunk])
-        landed(self.near.at[z, rows], self.r_y.at[chunk, z])
-        for spot in (0, 1):
-            landed(self.far.at[spot, rows], self.r_z.at[chunk, spot])
-
-        def add(part):
-            total = self.parts[j, part, :].astype(jnp.float32)
-            total = total + self.near[z, part, :].astype(jnp.float32)
-            for spot in (0, 1):
-                total = total + self.far[spot, part, :].astype(jnp.float32)
-            self.near[z, part, :] = total.astype(jnp.bfloat16)
-
-        self.each(chunk, add)
-
-    def drain(self, chunk):
-        z = lax.axis_index("seq") // 2
-        rows = pl.ds(*self.chunks[chunk])
-        landed(self.near.at[z, rows], self.s_y.at[chunk, z])
+        z, x = j // 2, lax.rem(j, 2)
+        for row in range(4):
+            landed(self.near[chunk](row), self.s_y.at[chunk, row])
         for n in (0, 1, 2):
             row = pick(LEAVING, z, n)
-            landed(self.near.at[row, rows], self.s_y.at[chunk, row])
-            landed(self.near.at[row, rows], self.s_z.at[chunk, row])
+            landed(self.near[chunk](row), self.s_z.at[chunk, row])
 
 
 class SmallSum:
@@ -862,20 +894,58 @@
     return cos_t, sin_t
 
 
-SLOTS = (
-    (0, 1, 2, 4, 5, 6, 8, 9, 10, 12, 13, 14),
-    (0, 2, 3, 4, 6, 7, 8, 10, 11, 12, 14, 15),
-)
-
-
-def attention_pieces(packed, w_out, dst):
+def first_slice(i, b, second=0):
+    return jnp.minimum((6 * b - i + 3) // 4 + second, 11)
+
+
+def local_slice(i, b, second=0):
+    return jnp.minimum(lax.rem(i + 2 * lax.rem(b, 2), 4) + 4 * second, 5)
+
+
+def has_second(i, b):
+    return lax.rem(i + 2 * lax.rem(b, 2), 4) < 2
+
+
+def spot(index, size):
+    return pl.ds(pl.multiple_of(size * index, size), size)
+
+
+def attention_pieces(turned_qkv, w_out, heads, outs):
     def pieces(me, other):
         _, j = place()
-        spot = lax.rem(other + 2 * lax.rem(j, 2), 4)
-        return [
-            (packed.at[spot], dst.at[j, pl.ds(256 * me, 256)]),
-            (w_out.at[pl.ds(64 * other, 64)], dst.at[j, pl.ds(1024 + 64 * me, 64)]),
-        ]
+        b, rows = column_block(me, j), row_block(me, j)
+        found = [(w_out.at[spot(other, 64)], outs.at[b, spot(rows, 64)], None, None)]
+        for second in (0, 1):
+            found.append(
+                (
+                    turned_qkv.at[spot(local_slice(other, b, second), 64)],
+                    heads.at[spot(first_slice(other, b, second), 64), spot(rows, 256)],
+                    has_second(other, b) if second else None,
+                    has_second(me, column_block(other, j)) if second else None,
+                )
+            )
+        return found
+
+    return pieces
+
+
+def return_attention(heads, outs, g_qkv, g_out):
+    def pieces(me, other):
+        _, j = place()
+        b = column_block(other, j)
+        side, half = other // 2, lax.rem(other, 2)
+        found = [(outs.at[side, spot(half, 64)], g_out.at[spot(me, 64)], None, None)]
+        for second in (0, 1):
+            held = jnp.minimum(first_slice(me, b, second) - 3 * (j // 2), 2)
+            found.append(
+                (
+                    heads.at[spot(held, 64), spot(half, 256)],
+                    g_qkv.at[spot(local_slice(me, b, second), 64)],
+                    has_second(me, b) if second else None,
+                    has_second(other, column_block(me, j)) if second else None,
+                )
+            )
+        return found
 
     return pieces
 
@@ -883,75 +953,52 @@
 def ffn_pieces(w_gate, w_up, w_down, dst):
     def pieces(me, other):
         _, j = place()
-        columns = pl.ds(pl.multiple_of(128 * other, 128), 128)
-        pairs = [
-            (w_gate.at[:, columns], dst.at[j, pl.ds(256 * me, 256)]),
-            (w_up.at[:, columns], dst.at[j, pl.ds(1024 + 256 * me, 256)]),
+        b, rows = column_block(me, j), row_block(me, j)
+        return [
+            (w_gate.at[:, spot(other, 128)], dst.at[b, spot(rows, 256)], None, None),
+            (w_up.at[:, spot(other, 128)], dst.at[b, spot(4 + rows, 256)], None, None),
+        ] + [
+            (
+                w_down.at[spot(4 * half + other, 128)],
+                dst.at[b, spot(16 + 2 * rows + half, 128)],
+                None,
+                None,
+            )
+            for half in (0, 1)
         ]
-        for half in (0, 1):
-            pairs.append(
-                (
-                    w_down.at[pl.ds(512 * half + 128 * other, 128)],
-                    dst.at[j, pl.ds(2048 + 256 * me + 128 * half, 128)],
-                )
+
+    return pieces
+
+
+def return_ffn(src, g_gate, g_up, g_down):
+    def pieces(me, other):
+        side, part = other // 2, lax.rem(other, 2)
+        return [
+            (src.at[0, side, spot(part, 256)], g_gate.at[:, spot(me, 128)], None, None),
+            (src.at[1, side, spot(part, 256)], g_up.at[:, spot(me, 128)], None, None),
+        ] + [
+            (
+                src.at[2, side, spot(2 * part + half, 128)],
+                g_down.at[spot(4 * half + me, 128)],
+                None,
+                None,
             )
-        return pairs
+            for half in (0, 1)
+        ]
 
     return pieces
 
 
-def head_weights(full, wh_ref, wm_ref, low_half):
-    def column(m, rows):
-        first, second = SLOTS[0][m], SLOTS[1][m]
-        one = full[first // 2, rows, 64 * (first % 2) : 64 * (first % 2) + 64]
-        two = full[second // 2, rows, 64 * (second % 2) : 64 * (second % 2) + 64]
-        return jnp.where(low_half, one, two)
-
-    @pl.loop(0, 4)
-    def _(t):
-        rows = pl.ds(pl.multiple_of(t * 256, 256), 256)
-        for m in range(0, 12, 2):
-            wh_ref[rows, 64 * m : 64 * m + 128] = jnp.concatenate(
-                [column(m, rows), column(m + 1, rows)], axis=1
-            )
-
-    for b in range(8):
-        wm_ref[:, 128 * b : 128 * b + 128] = full[b, 1024:1280, :]
+def position_table(labels):
+    lane = lax.broadcasted_iota(jnp.int32, (128, 128), 1)
+    frequency = jnp.exp(-jnp.log(10000.0) * (lane % 32).astype(jnp.float32) / 32)
+    angle = labels[:, 3:4] * frequency
+    rest = jnp.where(lane == 64, labels[:, 2:3], jnp.where(lane == 65, labels[:, 1:2], labels[:, 0:1]))
+    return jnp.where(lane < 32, jnp.cos(angle), jnp.where(lane < 64, jnp.sin(angle), rest))
 
 
 def norm_rows(hidden):
     return lax.rsqrt(jnp.mean(hidden * hidden, axis=1, keepdims=True) + EPSILON)
-
-
-def return_attention(src, g_qkv, g_out):
-    def pieces(me, other):
-        _, j = place()
-        spot = lax.rem(me + 2 * lax.rem(j, 2), 4)
-        return [
-            (src.at[pl.ds(256 * other, 256)], g_qkv.at[spot]),
-            (src.at[pl.ds(1024 + 64 * other, 64)], g_out.at[pl.ds(64 * me, 64)]),
-        ]
-
-    return pieces
-
-
-def return_ffn(src, g_gate, g_up, g_down):
-    def pieces(me, other):
-        columns = pl.ds(pl.multiple_of(128 * me, 128), 128)
-        pairs = [
-            (src.at[pl.ds(256 * other, 256)], g_gate.at[:, columns]),
-            (src.at[pl.ds(1024 + 256 * other, 256)], g_up.at[:, columns]),
-        ]
-        for half in (0, 1):
-            pairs.append(
-                (
-                    src.at[pl.ds(2048 + 256 * other + 128 * half, 128)],
-                    g_down.at[pl.ds(512 * half + 128 * me, 128)],
-                )
-            )
-        return pairs
-
-    return pieces
 
 
 def back_rows(grad_in, hidden, inv_rms):
@@ -959,20 +1006,8 @@
     return inv_rms * grad_in - hidden * (inv_rms * inv_rms * inv_rms * mean)
 
 
-def slot_columns(grads, slot, low_half):
-    picks = []
-    for row in SLOTS:
-        if slot in row:
-            m = row.index(slot)
-            picks.append(grads[:, 64 * m : 64 * m + 64])
-        else:
-            picks.append(jnp.zeros((grads.shape[0], 64), jnp.float32))
-    return jnp.where(low_half, picks[0], picks[1])
-
-
-FFN_CHUNKS = ((2048, 1024), (0, 2048))
-GRAD_CHUNKS = ((0, 2048), (2048, 1024))
-ATTENTION_CHUNKS = ((0, 1024), (1024, 256))
+FFN_CHUNKS = (2048, 0, 1024)
+GRAD_CHUNKS = (0, 1024, 2048)
 
 
 def wide(ref, first, rows):
@@ -990,17 +1025,17 @@
 
 
 def layer_kernel(*refs):
-    (tok, cot, tab, idr, packed, w_out, w_gate, w_up, w_down, gain_one, gain_two, bias), refs = (
-        refs[:12],
-        refs[12:],
-    )
-    (output, input_grad, g_gate, g_up, g_down, g_qkv, g_out, small_out), refs = refs[:8], refs[8:]
     (
-        tok_all, cot_all, tab_all, idr_all, tok_own, attn_all, wh_ref, wm_ref, q_ref, k_ref, v_ref,
-        o_ref, lse_ref, rows_ref, part, mid_ref, a2_all, turned, ffn_all, ffn_g, hidden_s, dgate_s,
-        dup_s, e2_ref, dq_acc, dk_acc, dv_acc, out_own, in_own, dbias, small,
-        r_gate, r_up, r_down, r_qkv, r_out,
-    ), refs = refs[:36], refs[36:]
+        tok, cot, segments, variates, times, pads, w_qkv, w_out, w_gate, w_up, w_down,
+        gain_attn, gain_ffn, bias_all,
+    ), refs = refs[:14], refs[14:]
+    (output, input_grad, r_gate, r_up, r_down, r_qkv, r_out, small_out), refs = refs[:8], refs[8:]
+    (
+        tok_all, cot_all, tab_all, idr_all, tok_own, heads_w, out_w, heads_g, out_g, wm_ref, q_ref,
+        k_ref, v_ref, o_ref, lse_ref, rows_ref, part, mid_ref, a2_all, turned, ffn_all, ffn_g,
+        hidden_s, dgate_s, dup_s, e2_ref, dq_acc, dk_acc, dv_acc, out_own, in_own, dbias, small,
+        near_f, far_f, near_q, far_q, near_o, far_o, idr, turned_qkv,
+    ), refs = refs[:41], refs[41:]
     home_in, refs = refs[:2], refs[2:]
     home_out, refs = refs[:2], refs[2:]
     gather_in, refs = refs[:6], refs[6:]
@@ -1012,24 +1047,33 @@
     spread_a, spread_f, back_a, back_f = [refs[3 * n : 3 * n + 3] for n in range(4)]
     refs = refs[12:]
     chain_a, chain_f, refs = refs[:5], refs[5:10], refs[10:]
-    fold_f, fold_a, refs = refs[:6], refs[6:12], refs[12:]
-    small_scratch, out_sem = refs[:-1], refs[-1]
+    fold_f, fold_a, refs = refs[:4], refs[4:8], refs[8:]
+    small_scratch = refs
 
     i, j = place()
     z, y = j // 2, lax.rem(j, 2)
     mine_first = 2 * (1 - lax.rem(i, 2))
-    low_half = i < 2
 
     def turn(u):
         return lax.rem(mine_first + u, 4)
 
-    ez_all, dqkv_ref, do_ref, out_part = dgate_s, dup_s, hidden_s, turned
-    home = Home((tok, tab, idr, cot), (tok_all, tab_all, idr_all, cot_all), home_in, False)
-    group = GroupGather((tok_all, tab_all, idr_all, cot_all), gather_in)
-    spread = Exchange(attention_pieces(packed, w_out, attn_all), spread_a)
+    ez_all, dqkv_ref, out_part = dgate_s, dup_s, turned
+    home = Home((tok, idr, cot), (tok_all, idr_all, cot_all), home_in, False)
+    group = GroupGather((tok_all, idr_all, cot_all), gather_in)
+    spread = Exchange(attention_pieces(turned_qkv, w_out, heads_w, out_w), spread_a)
     spread_ffn = Exchange(ffn_pieces(w_gate, w_up, w_down, ffn_all), spread_f)
-    attn_w = SeqGather(attn_all, ((0, 1280),), chain_a)
-    ffn_w = SeqGather(ffn_all, FFN_CHUNKS, chain_f)
+
+    def heads_block(ref):
+        return lambda row, side: ref.at[spot(row, 192), spot(side, 512)]
+
+    def outs_block(ref):
+        return lambda row, side: ref.at[spot(row, 2), spot(side, 128)]
+
+    def ffn_block(ref, start):
+        return lambda row, side: ref.at[spot(row, 2), spot(start // 512 + side, 512)]
+
+    attn_w = SeqGather((heads_block(heads_w), outs_block(out_w)), chain_a)
+    ffn_w = SeqGather([ffn_block(ffn_all, start) for start in FFN_CHUNKS], chain_f)
     branch = GroupSum(part, buffers, sum_sems[0])
     second = GroupGather((a2_all,), gather_a2)
     da_sum = GroupSum(part, buffers, sum_sems[1])
@@ -1037,36 +1081,68 @@
     da1_sum = GroupSum(part, buffers, sum_sems[3])
     third = GroupGather((ez_all,), gather_ez)
     leave = Home((out_own, in_own), (output, input_grad), home_out, True)
-    ffn_fold = SeqSum(ffn_g, GRAD_CHUNKS, fold_f)
-    attn_fold = SeqSum(attn_all, ATTENTION_CHUNKS, fold_a)
-    ffn_back = Exchange(return_ffn(fold_f[0].at[z], r_gate, r_up, r_down), back_f)
-    attn_back = Exchange(return_attention(fold_a[0].at[z], r_qkv, r_out), back_a)
-
+    ffn_fold = SeqSum(
+        [ffn_block(ffn_g, start) for start in GRAD_CHUNKS],
+        [lambda row, chunk=chunk: near_f.at[row, chunk] for chunk in (0, 1, 2)],
+        [lambda held, chunk=chunk: far_f.at[held, chunk] for chunk in (0, 1, 2)],
+        fold_f,
+    )
+    attn_fold = SeqSum(
+        (heads_block(heads_g), outs_block(out_g)),
+        (lambda row: near_q.at[row], lambda row: near_o.at[row]),
+        (lambda held: far_q.at[held], lambda held: far_o.at[held]),
+        fold_a,
+    )
+    ffn_back = Exchange(return_ffn(near_f.at[z], r_gate, r_up, r_down), back_f)
+    attn_back = Exchange(return_attention(near_q.at[z], near_o.at[z], r_qkv, r_out), back_a)
+
+    turned_qkv[...] = w_qkv[...].T
+    for s in (0, 1):
+        label = [ref[s : s + 1, :] for ref in (segments, variates, times, pads)]
+        lines = (jnp.where(label[3] == 1, label[0], -1), label[1], label[0], label[2])
+        for line, value in enumerate(lines):
+            idr[s, line : line + 1, :] = value.astype(jnp.float32)
+        idr[s, 4:8, :] = jnp.zeros((4, 128), jnp.float32)
+    gain_one, gain_two = gain_attn[...].astype(jnp.float32), gain_ffn[...].astype(jnp.float32)
+    sixteen = lax.broadcasted_iota(jnp.int32, (1, 16), 1)
+    bias = [
+        jnp.sum(
+            jnp.where(sixteen == 4 * h + i, bias_all[...].astype(jnp.float32), 0.0),
+            axis=1,
+            keepdims=True,
+        )
+        for h in range(4)
+    ]
     meet(dp_peers() + seq_peers(), home=True)
     spread.start()
-    for a in (0, 1, 2):
+    for a in (0, 1):
         for s in (0, 1):
             home.start(a, s)
-    spread_ffn.start()
     spread.wait()
-    attn_w.start(0)
-    for a in (0, 1, 2):
+    for chunk in (0, 1):
+        attn_w.start_z(chunk)
+    for chunk in (0, 1):
+        attn_w.start_y(chunk)
+    for a in (0, 1):
         for s in (0, 1):
             home.wait(a, s)
             group.push(a, s)
+    spread_ffn.start()
     for s in (0, 1):
         tok_own[s] = tok_all[owned(i, s)]
     for n in (0, 1, 2):
-        attn_w.forward(0, n)
-    for s in (0, 1):
-        home.start(3, s)
-    spread_ffn.wait()
-    ffn_w.start(0)
-    ffn_w.start(1)
-    for a in (0, 1, 2):
+        for chunk in (0, 1):
+            attn_w.forward(chunk, n)
+    for a in (0, 1):
         for s in (0, 1):
             group.relay(a, s)
-    for a in (0, 1, 2):
+    for chunk in (0, 1):
+        attn_w.relayed(chunk)
+    spread_ffn.wait()
+    ffn_w.start_z(0)
+    for s in (0, 1):
+        home.start(2, s)
+    for a in (0, 1):
         group.finish(a)
         home.finish(a)
     for b in range(8):
@@ -1075,16 +1151,21 @@
     @pl.loop(0, 8)
     def _(b):
         hidden = tok_all[b].astype(jnp.float32)
-        tok_all[b] = (hidden * norm_rows(hidden) * gain_one[...]).astype(jnp.bfloat16)
+        tok_all[b] = (hidden * norm_rows(hidden) * gain_one).astype(jnp.bfloat16)
+        tab_all[b] = position_table(idr_all[b].T)
 
     a1_all = tok_all
-    attn_w.finish(0)
-    head_weights(attn_all, wh_ref, wm_ref, low_half)
+    for chunk in (0, 1):
+        attn_w.finish(chunk)
+    for chunk in (0, 1, 2):
+        ffn_w.start_y(chunk)
+    for b in range(8):
+        wm_ref[:, 128 * b : 128 * b + 128] = out_w[b]
 
     @pl.loop(0, 4)
     def _(t):
         rows = pl.ds(pl.multiple_of(t * 256, 256), 256)
-        proj = dot(two(a1_all, t), wh_ref[...])
+        proj = dot(two(a1_all, t), heads_w[...], NT)
         cos_t, sin_t = angle_tables(two(tab_all, t))
         for pair in (0, 1):
             cols = slice(128 * pair, 128 * pair + 128)
@@ -1132,35 +1213,39 @@
 
         @pl.when(u == 0)
         def _():
+            for n in (0, 1, 2):
+                ffn_w.forward(0, n)
+            ffn_w.start_z(1)
+
+        @pl.when(u == 1)
+        def _():
             for s in (0, 1):
-                home.wait(3, s)
-                group.push(3, s)
+                home.wait(2, s)
+                group.push(2, s)
 
         @pl.when(u == 3)
         def _():
             for s in (0, 1):
-                group.relay(3, s)
-
-        for n in (0, 1, 2):
-
-            @pl.when(u == n + 1)
-            def _():
-                ffn_w.forward(0, n)
+                group.relay(2, s)
+            for n in (0, 1, 2):
+                ffn_w.forward(1, n)
+            ffn_w.start_z(2)
 
     for s in (0, 1):
         block = owned(i, s)
         mid = tok_own[s].astype(jnp.float32) + branch.total(s)
         mid_ref[s] = mid
-        a2_all[block] = (mid * norm_rows(mid) * gain_two[...]).astype(jnp.bfloat16)
+        a2_all[block] = (mid * norm_rows(mid) * gain_two).astype(jnp.bfloat16)
         second.push(0, s)
     branch.finish()
-    ffn_w.forward(1, 0)
     for s in (0, 1):
         second.relay(0, s)
-    group.finish(3)
-    home.finish(3)
+    group.finish(2)
+    home.finish(2)
     second.finish(0)
     ffn_w.finish(0)
+    for n in (0, 1):
+        ffn_w.forward(2, n)
 
     @pl.loop(0, 4)
     def _(t):
@@ -1206,23 +1291,33 @@
         f = z
         for n in (0, 1, 2):
             f = jnp.where(step == n + 1, pick(ARRIVAL, z, n), f)
+        @pl.when(step == 1)
+        def _():
+            ffn_w.forward(2, 2)
+
         ffn_w.arrived(1, f)
-        for n in (1, 2):
-
-            @pl.when(step == n - 1)
-            def _():
-                ffn_w.forward(1, n)
-
+        ffn_w.arrived(2, f)
         unit(f)
 
         @pl.when(step > 0)
         def _():
             ffn_fold.start(0, f)
-
-    ffn_fold.start_rest(1)
-    ffn_fold.start(0, z)
-    ffn_fold.start(1, z)
-    ffn_w.drain(1)
+            ffn_fold.start(1, f)
+
+    for chunk in (0, 1, 2):
+        ffn_w.relayed(chunk)
+    for chunk in (1, 2):
+        ffn_w.drain(chunk)
+
+    def at_end(chunk, n):
+        @pl.when(jnp.logical_not(inner(z)))
+        def _():
+            ffn_fold.cross(chunk, n)
+
+    def at_inner(chunk, n):
+        @pl.when(inner(z))
+        def _():
+            ffn_fold.cross(chunk, n)
 
     def product(left, t, first_row):
         total = None
@@ -1265,74 +1360,78 @@
             def _():
                 out_sum.start(s)
 
+    at_end(0, 0), at_end(1, 0)
     gain_rows = jnp.zeros((1, 1024), jnp.float32)
     for s in (0, 1):
         mid = mid_ref[s]
         inv = norm_rows(mid)
         da2 = da_sum.total(s)
         gain_rows = gain_rows + jnp.sum(da2 * (mid * inv), axis=0, keepdims=True)
-        e2 = cot_all[owned(i, s)].astype(jnp.float32) + back_rows(da2 * gain_two[...], mid, inv)
+        e2 = cot_all[owned(i, s)].astype(jnp.float32) + back_rows(da2 * gain_two, mid, inv)
         e2_ref[s] = e2
         ez_all[owned(i, s)] = e2.astype(jnp.bfloat16)
         third.push(0, s)
     for b in range(8):
         small[8 + b : 9 + b, :] = gain_rows[:, 128 * b : 128 * b + 128]
     da_sum.finish()
-    ffn_fold.cross(0, 0)
+    ffn_fold.start_rest(2)
+    at_inner(0, 0), at_inner(1, 0)
+    at_end(0, 1), at_end(1, 1)
     for s in (0, 1):
         out_sum.cross(s)
-    for s in (0, 1):
-        third.relay(0, s)
-    third.finish(0)
-    ffn_fold.cross(0, 1)
-
-    @pl.loop(0, 4)
-    def _(t):
-        do_ref[pl.ds(2 * t, 2), :, 0:256] = dot(two(ez_all, t), wm_ref[...], NT, jnp.bfloat16).reshape(
-            2, 128, 256
-        )
-
-    for d in range(4):
-        ez = ez_all[:, :, 256 * d : 256 * d + 256].reshape(1024, 256)
-        store_wide(attn_all, 2 * d, slice(1024, 1280), dot(o_ref[...], ez, TN, jnp.bfloat16))
-    attn_fold.start_rest(1)
-    attn_fold.start(1, z)
-    for s in (0, 1):
-        out_own[s] = (mid_ref[s] + out_sum.total(s)).astype(jnp.bfloat16)
-        leave.start(0, s)
-
-    def unturn(acc, base, t, rows):
-        cos_t, sin_t = angle_tables(two(tab_all, t))
-        for pair in (0, 1):
-            g = acc[rows, 128 * pair : 128 * pair + 128]
-            dqkv_ref[pl.ds(2 * t, 2), :, base + 128 * pair : base + 128 * pair + 128] = (
-                (g * cos_t - swap_halves(g) * sin_t).astype(jnp.bfloat16).reshape(2, 128, 128)
-            )
+    third.near(0)
+
+    def unturn(acc, base, blocks, rows):
+        for block, part_rows in zip(blocks, rows):
+            cos_t, sin_t = angle_tables(tab_all[block])
+            for pair in (0, 1):
+                g = acc[part_rows, 128 * pair : 128 * pair + 128]
+                dqkv_ref[block, :, base + 128 * pair : base + 128 * pair + 128] = (
+                    g * cos_t - swap_halves(g) * sin_t
+                ).astype(jnp.bfloat16)
 
     dk_acc[...] = jnp.zeros_like(dk_acc)
     dv_acc[...] = jnp.zeros_like(dv_acc)
     dbias[...] = jnp.zeros_like(dbias)
 
     @pl.loop(0, 4)
-    def _(t):
-        start = pl.multiple_of(t * 256, 256)
-        rows = pl.ds(start, 256)
+    def _(u):
+        @pl.when(u == 2)
+        def _():
+            third.relay(0, 0)
+            third.relay(0, 1)
+            third.beyond(0)
+            for d in range(4):
+                ez = ez_all[:, :, 256 * d : 256 * d + 256].reshape(1024, 256)
+                store_wide(out_g, 2 * d, slice(None), dot(o_ref[...], ez, TN, jnp.bfloat16))
+            attn_fold.start_rest(1)
+
+        b = 2 * lax.rem(u, 2) + jnp.where(u < 2, i // 2, 1 - i // 2)
+        upper = b + 4
+        rows = pl.ds(pl.multiple_of(128 * b, 128), 128)
+        rows_up = pl.ds(pl.multiple_of(128 * upper, 128), 128)
+
+        def both(ref, cols):
+            return jnp.concatenate([ref[rows, cols], ref[rows_up, cols]], axis=0)
+
+        do = dot(jnp.concatenate([ez_all[b], ez_all[upper]], axis=0), wm_ref[...], NT, jnp.bfloat16)
         columns = tab_all[...].reshape(1024, 128)
         var_k, code_k = columns[:, 65:66], columns[:, 66:67]
-        pair = idr_all[pl.ds(2 * t, 2)]
-        label = jnp.concatenate([pair[0], pair[1]], axis=1)
+        label = jnp.concatenate([idr_all[b], idr_all[upper]], axis=1)
+        log_sum = jnp.concatenate([lse_ref[:, rows], lse_ref[:, rows_up]], axis=1)
         seg_q, var_q = label[2:3, :], label[1:2, :]
         row = lax.broadcasted_iota(jnp.int32, (1024, 256), 0)
-        col = start + lax.broadcasted_iota(jnp.int32, (1024, 256), 1)
+        lane = lax.broadcasted_iota(jnp.int32, (1024, 256), 1)
+        col = 128 * b + jnp.where(lane < 128, lane, lane + 384)
         allowed = ((seg_q == code_k) & (jnp.abs(row - col) <= WINDOW)) | (row == col)
         masked = jnp.where(allowed, 0.0, NEGATIVE)
         same = jnp.where(var_q == var_k, 1.0, 0.0)
         for h in range(4):
             cols = slice(64 * h, 64 * h + 64)
-            q_h, k_h, v_h = q_ref[rows, cols] * 0.125, k_ref[:, cols], v_ref[:, cols]
-            do_h = two(do_ref, t, cols)
+            q_h, k_h, v_h = both(q_ref, cols) * 0.125, k_ref[:, cols], v_ref[:, cols]
+            do_h = do[:, cols]
             scores = dot(k_h, q_h, NT) + bias[h] * same + masked
-            prob = jnp.exp(scores - lse_ref[h : h + 1, rows])
+            prob = jnp.exp(scores - log_sum[h : h + 1, :])
             dv_acc[:, cols] += dot(prob.astype(jnp.bfloat16), do_h)
             dprob = dot(v_h, do_h, NT)
             mean = jnp.sum(prob * dprob, axis=0, keepdims=True)
@@ -1341,49 +1440,56 @@
             dk_acc[:, cols] += dot(dscore, q_h)
             dq_acc[:, cols] = dot(dscore, k_h, TN) * 0.125
 
-        unturn(dq_acc, 0, t, slice(None))
-
-        @pl.when(t == 0)
+        unturn(dq_acc, 0, (b, upper), (slice(0, 128), slice(128, 256)))
+
+        @pl.when(u == 0)
         def _():
-            ffn_fold.cross(1, 0)
-
-        @pl.when(t == 1)
+            at_end(0, 2), at_end(1, 2)
+
+        @pl.when(u == 1)
         def _():
-            ffn_fold.cross(0, 2)
-
-        @pl.when(t == 2)
+            at_inner(0, 1), at_inner(1, 1)
+            ffn_fold.cross(2, 0)
+
+        @pl.when(u == 2)
         def _():
-            ffn_fold.cross(1, 1)
-
-        @pl.when(t == 3)
+            at_inner(0, 2), at_inner(1, 2)
+            at_end(2, 1), at_end(2, 2)
+            ffn_fold.start(0, z)
+
+        @pl.when(u == 3)
         def _():
-            attn_fold.cross(1, 0)
+            at_inner(2, 1)
 
     @pl.loop(0, 4)
     def _(t):
         rows = pl.ds(pl.multiple_of(t * 256, 256), 256)
-        unturn(dk_acc, 256, t, rows)
+        unturn(
+            dk_acc,
+            256,
+            (2 * t, 2 * t + 1),
+            [pl.ds(pl.multiple_of(t * 256 + 128 * e, 128), 128) for e in (0, 1)],
+        )
         dqkv_ref[pl.ds(2 * t, 2), :, 512:768] = (
             dv_acc[rows, :].astype(jnp.bfloat16).reshape(2, 128, 256)
         )
 
-    for d in range(4):
+    for d in range(3):
         block = slice(256 * d, 256 * d + 256)
-        grads = dot(
-            a1_all[:, :, block].reshape(1024, 256), dqkv_ref[:, :, 0:768].reshape(1024, 768), TN
-        )
-        for b in range(8):
-            attn_all[b, block, :] = jnp.concatenate(
-                [slot_columns(grads, 2 * b + e, low_half) for e in (0, 1)], axis=1
-            ).astype(jnp.bfloat16)
+        heads_g[block, :] = dot(
+            dqkv_ref[:, :, block].reshape(1024, 256), a1_all[...].reshape(1024, 1024), TN, jnp.bfloat16
+        )
+    at_inner(2, 2)
     attn_fold.start_rest(0)
-    attn_fold.start(0, z)
+    for s in (0, 1):
+        out_own[s] = (mid_ref[s] + out_sum.total(s)).astype(jnp.bfloat16)
+        leave.start(0, s)
 
     @pl.loop(0, 4)
     def _(u):
         t = turn(u)
         part[pl.ds(2 * t, 2)] = dot(
-            two(dqkv_ref, t, slice(0, 768)), wh_ref[...], NT, jnp.bfloat16
+            two(dqkv_ref, t, slice(0, 768)), heads_w[...], out=jnp.bfloat16
         ).reshape(2, 128, 1024)
         for s in (0, 1):
 
@@ -1395,21 +1501,29 @@
             def _():
                 da1_sum.cross(s)
 
-    ffn_fold.cross(1, 2)
-    attn_fold.cross(1, 1)
-    attn_fold.cross(0, 0)
-    attn_fold.cross(1, 2)
-    for chunk in (0, 1):
-        ffn_fold.finish(chunk)
-    ffn_back.start()
+    third.sent(0)
+    for chunk in (1, 2):
+        ffn_fold.start(chunk, z)
+    for chunk in (1, 0):
+        attn_fold.start(chunk, z)
+    for chunk in (1, 0):
+        attn_fold.cross(chunk, 0)
+
+    @pl.when(jnp.logical_not(inner(z)))
+    def _():
+        for n in (1, 2):
+            for chunk in (1, 0):
+                attn_fold.cross(chunk, n)
+
     gain_rows = jnp.zeros((1, 1024), jnp.float32)
     for s in (0, 1):
         hidden = tok_own[s].astype(jnp.float32)
         inv = norm_rows(hidden)
         da1 = da1_sum.total(s)
         gain_rows = gain_rows + jnp.sum(da1 * (hidden * inv), axis=0, keepdims=True)
-        grad = e2_ref[s] + back_rows(da1 * gain_one[...], hidden, inv)
+        grad = e2_ref[s] + back_rows(da1 * gain_one, hidden, inv)
         in_own[s] = grad.astype(jnp.bfloat16)
+        leave.start(1, s)
     for b in range(8):
         small[b : b + 1, :] = gain_rows[:, 128 * b : 128 * b + 128]
     lane = lax.broadcasted_iota(jnp.int32, (8, 128), 1)
@@ -1421,30 +1535,22 @@
     small[16:24, :] = bias_row
     small_sum = SmallSum(small, small_scratch)
     small_sum.start(0)
-    attn_fold.cross(0, 1)
-    attn_fold.cross(0, 2)
+
+    @pl.when(inner(z))
+    def _():
+        for n in (1, 2):
+            for chunk in (1, 0):
+                attn_fold.cross(chunk, n)
+
+    for chunk in (0, 1, 2):
+        ffn_fold.finish(chunk)
+    ffn_back.start()
     small_sum.start(1)
-    for s in (0, 1):
-        leave.start(1, s)
     for chunk in (1, 0):
         attn_fold.finish(chunk)
     attn_back.start()
     small_sum.start(2)
     ffn_back.wait()
-    copies = []
-    for start, source, target in ((0, r_gate, g_gate), (512, r_up, g_up)):
-        for half in (0, 1):
-            cols = slice(256 * half, 256 * half + 256)
-            rows = slice(start + 256 * half, start + 256 * half + 256)
-            dv_acc[rows, :] = source[:, cols].astype(jnp.float32)
-            copies.append((dv_acc.at[rows], target.at[:, cols]))
-    dk_acc[:, 0:128] = r_down[...].astype(jnp.float32)
-    copies.append((dk_acc.at[:, 0:128], g_down))
-    copies = [
-        pltpu.make_async_copy(src, dst, out_sem.at[index]) for index, (src, dst) in enumerate(copies)
-    ]
-    for copy in copies:
-        copy.start()
     small_out[...] = small_sum.total(2)
     out_sum.finish()
     da1_sum.finish()
@@ -1452,14 +1558,11 @@
         for s in (0, 1):
             leave.wait(a, s)
         leave.finish(a)
+    for chunk in (0, 1, 2):
+        ffn_fold.drain(chunk)
     for chunk in (0, 1):
-        ffn_fold.drain(chunk)
         attn_fold.drain(chunk)
     attn_back.wait()
-    g_qkv[...] = r_qkv[...].astype(jnp.float32)
-    g_out[...] = r_out[...].astype(jnp.float32)
-    for copy in copies:
-        copy.wait()
 
 
 def layer(arrays):
@@ -1476,23 +1579,25 @@
         out_shape=[
             bf16(2, 128, 1024),
             bf16(2, 128, 1024),
-            f32(256, 512),
-            f32(256, 512),
-            f32(1024, 128),
-            f32(4, 256, 128),
-            f32(256, 128),
+            bf16(256, 512),
+            bf16(256, 512),
+            bf16(1024, 128),
+            bf16(384, 256),
+            bf16(256, 128),
             f32(24, 128),
         ],
-        in_specs=[HB, HB, VM, VM, VM, VM, HB, HB, HB, VM, VM, SM],
-        out_specs=[HB] * 5 + [VM] * 3,
+        in_specs=[HB, HB] + [VM] * 6 + [HB] * 3 + [VM] * 3,
+        out_specs=[HB] * 7 + [VM],
         scratch_shapes=[
             blocks,
             blocks,
             vmem(full, 8, 128, 128),
             vmem(full, 8, 8, 128),
             own,
-            vmem(low, 8, 1280, 128),
-            vmem(low, 1024, 768),
+            vmem(low, 768, 1024),
+            vmem(low, 8, 256, 128),
+            vmem(low, 768, 1024),
+            vmem(low, 8, 256, 128),
             vmem(low, 256, 1024),
             heads,
             heads,
@@ -1517,30 +1622,32 @@
             own,
             vmem(full, 8, 256),
             vmem(full, 24, 128),
-            vmem(low, 256, 512),
-            vmem(low, 256, 512),
-            vmem(low, 1024, 128),
-            vmem(low, 4, 256, 128),
-            vmem(low, 256, 128),
+            vmem(low, 4, 3, 2, 512, 128),
+            vmem(low, 4, 3, 2, 512, 128),
+            vmem(low, 4, 192, 512),
+            vmem(low, 4, 192, 512),
+            vmem(low, 4, 2, 128, 128),
+            vmem(low, 4, 2, 128, 128),
+            vmem(full, 2, 8, 128),
+            vmem(low, 384, 256),
         ]
-        + Home.sems(4)
+        + Home.sems(3)
         + Home.sems(2)
-        + GroupGather.sems(4)
+        + GroupGather.sems(3)
         + GroupGather.sems(1)
         + GroupGather.sems(1)
         + GroupSum.buffers()
         + GroupSum.buffers()
         + GroupSum.sems() * 4
-        + Exchange.sems(2)
+        + Exchange.sems(3)
         + Exchange.sems(4)
-        + Exchange.sems(2)
+        + Exchange.sems(3)
         + Exchange.sems(4)
-        + SeqGather.sems(1)
         + SeqGather.sems(2)
-        + SeqSum.scratch(3072, 2)
-        + SeqSum.scratch(1280, 2)
-        + SmallSum.scratch((24, 128))
-        + [DMA((5,))],
+        + SeqGather.sems(3)
+        + SeqSum.sems(3)
+        + SeqSum.sems(2)
+        + SmallSum.scratch((24, 128)),
         compiler_params=pltpu.CompilerParams(
             collective_id=1, has_side_effects=True, vmem_limit_bytes=67_043_328
         ),
@@ -1548,37 +1655,52 @@
     )(*arrays)
 
 
+def finish_kernel(*refs):
+    (out_in, grad_in, gate, up, down, qkv, out, small), refs = refs[:8], refs[8:]
+    output, input_grad, g_qkv, g_out, g_gate, g_up, g_down, one, two_, bias = refs
+    output[...] = out_in[...]
+    input_grad[...] = grad_in[...]
+    g_qkv[...] = qkv[...].astype(jnp.float32).T
+    for target, source in ((g_out, out), (g_gate, gate), (g_up, up), (g_down, down)):
+        target[...] = source[...].astype(jnp.float32)
+    one[...] = small[0:8, :]
+    two_[...] = small[8:16, :]
+    bias[...] = small[16:17, 0:16]
+
+
+def finish(arrays):
+    return pl.pallas_call(
+        finish_kernel,
+        out_shape=[
+            bf16(2, 128, 1024),
+            bf16(2, 128, 1024),
+            f32(256, 384),
+            f32(256, 128),
+            f32(256, 512),
+            f32(256, 512),
+            f32(1024, 128),
+            f32(8, 128),
+            f32(8, 128),
+            f32(1, 16),
+        ],
+        in_specs=[VM] * 8,
+        out_specs=[VM] * 10,
+        name="finish",
+    )(*arrays)
+
+
 def on_group(
     tokens, segment_ids, variate_ids, time_ids, pad_mask, cotangent,
     w_qkv, w_out, w_gate, w_up, w_down, gain_attn, gain_ffn, variate_bias,
 ):
-    i = lax.axis_index("dp")
-    gain_one = gain_attn.astype(jnp.float32)[None]
-    gain_two = gain_ffn.astype(jnp.float32)[None]
-    packed = jnp.pad(w_qkv, ((0, 0), (0, 128))).reshape(256, 2, 4, 64)
-    packed = packed.transpose(2, 0, 1, 3).reshape(4, 256, 128)
-    frequency = jnp.exp(-jnp.log(10000.0) * jnp.arange(32, dtype=jnp.float32) / 32)
-    angles = time_ids.astype(jnp.float32)[..., None] * frequency
-    code_ids = jnp.where(pad_mask == 1, segment_ids, -1)
-    labels = jnp.stack([segment_ids, variate_ids, code_ids], axis=-1).astype(jnp.float32)
-    tables = jnp.concatenate(
-        [jnp.cos(angles), jnp.sin(angles), labels, jnp.zeros((2, 128, 61), jnp.float32)], axis=-1
-    )
-    label_rows = jnp.stack([code_ids, variate_ids, segment_ids] + [segment_ids] * 5, axis=1)
-    bias = jnp.where(
-        jnp.arange(4)[None, :] == i, variate_bias.astype(jnp.float32).reshape(4, 4), 0.0
-    ).sum(axis=1)
-    output, input_grad, g_gate, g_up, g_down, g_qkv, g_out, small = layer(
+    results = layer(
         [
-            tokens, cotangent, tables, label_rows.astype(jnp.float32), packed, w_out, w_gate, w_up, w_down,
-            gain_one, gain_two, bias,
+            tokens, cotangent, segment_ids, variate_ids, time_ids, pad_mask, w_qkv, w_out, w_gate, w_up,
+            w_down, gain_attn[None], gain_ffn[None], variate_bias[None],
         ]
     )
-    g_qkv = g_qkv.reshape(4, 256, 2, 64).transpose(1, 2, 0, 3).reshape(256, 512)[:, :384]
-    small = small.reshape(3, 1024)
-    return (
-        output, input_grad, g_qkv, g_out, g_gate, g_up, g_down, small[0], small[1], small[2, :16],
-    )
+    *large, one, two_, bias_grad = finish(results)
+    return (*large, one.reshape(1024), two_.reshape(1024), bias_grad.reshape(16))
 
 
 def solution(mesh):

time: 296 us -> 251 us (0.85)
  Pallas kernels: 276 us -> 248 us
  local copies, waits for them, and re-layouts: 13.8 us -> 1.88 us
  other arithmetic: 4.45 us -> 0 us
    pallas_call x1, Pallas kernels: 276 us -> 245 us  [layer(): pl.pallas_call(layer_kernel, out_shape=[bf16(2, 128, 1024), bf16(2, 128,...]
    unnamed x36 -> x2, local copies, waits for them, and re-layouts: 9.39 us -> 0.01 us
    pallas_call x0 -> x1, Pallas kernels: none -> 3.26 us  [finish(): pl.pallas_call(finish_kernel, out_shape=[bf16(2, 128, 1024), bf16(2, 128,...]
where the time goes in v5:
time: 251 us
  Pallas kernels  248 us (99%)
    pallas_call x1, Pallas kernels, layer(): pl.pallas_call(layer_kernel, out_shape=[bf16(2, 128, 1024), bf16(2, 128,...  245 us

profile of v5, /device:TPU:0, one launch (start us, length us, event | category | flops | bytes accessed | tf_op | source)
XLA Modules:
  0.0 250.8 jit_solution(3085577873888291956)
XLA Ops:
  0.6 0.0 copy-start
  0.7 1.3 broadcast_in_dim.9.refs_11_
  1.9 0.0 copy-done
  1.9 0.6 broadcast_in_dim.10.refs_12_
  2.5 245.0 %layer.1 = (bf16[2,128,1024]{2,1,0:T(8,128)(2,1)}, bf16[2,128,1024]{2,1,0:T(8,128)(2,1)}, bf16[256,512]{1,0:T(8,128)(2,1)}, bf16[256,512]{1,0:T(8,128)(2,1)}, bf...) custom-call(bf16[2,128,1024]{2,1,0:T(8,128)(2,1)} %refs_0_.1, ...), custom_call_target="tpu_custom_call" | custom-call | tf_op jit(solution)/shard_map/layer/pallas_call | solution.py:1577
  247.5 3.3 %finish.1 = (bf16[2,128,1024]{2,1,0:T(8,128)(2,1)}, bf16[2,128,1024]{2,1,0:T(8,128)(2,1)}, f32[256,384]{1,0:T(8,128)}, f32[256,128]{1,0:T(8,128)}, f32[256,512]{...) custom-call(bf16[2,128,1024]{2,1,0:T(8,128)(2,1)} %get-tuple-element, ...), custom_call_target="tpu_custom_call" | custom-call | tf_op jit(solution)/shard_map/finish/pallas_call | solution.py:1672
Async XLA Ops:
  0.6 1.3 copy-start

commit v6 on v5

--- a/solution.py
+++ b/solution.py
@@ -729,6 +729,13 @@
         peer = at(i, 2 * z + 1 - x)
         send(block, block, self.s_y.at[chunk, source], self.r_y.at[chunk, source], peer).start()
 
+    def forward_at(self, inside, chunk, n):
+        z = place()[1] // 2
+
+        @pl.when(inner(z) if inside else jnp.logical_not(inner(z)))
+        def _():
+            self.forward(chunk, n)
+
     def arrived(self, chunk, source):
         x = lax.rem(place()[1], 2)
         landed(self.blocks[chunk](source, 1 - x), self.r_y.at[chunk, source])
@@ -1103,7 +1110,8 @@
         for line, value in enumerate(lines):
             idr[s, line : line + 1, :] = value.astype(jnp.float32)
         idr[s, 4:8, :] = jnp.zeros((4, 128), jnp.float32)
-    gain_one, gain_two = gain_attn[...].astype(jnp.float32), gain_ffn[...].astype(jnp.float32)
+    gain_one = gain_attn[...].astype(jnp.float32).reshape(1, 1024)
+    gain_two = gain_ffn[...].astype(jnp.float32).reshape(1, 1024)
     sixteen = lax.broadcasted_iota(jnp.int32, (1, 16), 1)
     bias = [
         jnp.sum(
@@ -1213,23 +1221,29 @@
 
         @pl.when(u == 0)
         def _():
-            for n in (0, 1, 2):
-                ffn_w.forward(0, n)
+            ffn_w.forward(0, 0)
             ffn_w.start_z(1)
+            ffn_w.forward_at(True, 0, 1)
+            ffn_w.forward_at(True, 0, 2)
 
         @pl.when(u == 1)
         def _():
             for s in (0, 1):
                 home.wait(2, s)
                 group.push(2, s)
+            ffn_w.forward_at(False, 0, 1)
+
+        @pl.when(u == 2)
+        def _():
+            ffn_w.forward_at(False, 0, 2)
+            ffn_w.forward(1, 0)
+            ffn_w.start_z(2)
 
         @pl.when(u == 3)
         def _():
             for s in (0, 1):
                 group.relay(2, s)
-            for n in (0, 1, 2):
-                ffn_w.forward(1, n)
-            ffn_w.start_z(2)
+            ffn_w.forward_at(True, 1, 1)
 
     for s in (0, 1):
         block = owned(i, s)
@@ -1238,8 +1252,11 @@
         a2_all[block] = (mid * norm_rows(mid) * gain_two).astype(jnp.bfloat16)
         second.push(0, s)
     branch.finish()
+    ffn_w.forward_at(True, 1, 2)
+    ffn_w.forward_at(False, 1, 1)
     for s in (0, 1):
         second.relay(0, s)
+    ffn_w.forward_at(False, 1, 2)
     group.finish(2)
     home.finish(2)
     second.finish(0)
@@ -1696,7 +1713,7 @@
     results = layer(
         [
             tokens, cotangent, segment_ids, variate_ids, time_ids, pad_mask, w_qkv, w_out, w_gate, w_up,
-            w_down, gain_attn[None], gain_ffn[None], variate_bias[None],
+            w_down, gain_attn, gain_ffn, variate_bias[None],
         ]
     )
     *large, one, two_, bias_grad = finish(results)

time: 251 us -> 241 us (0.960)
  Pallas kernels: 248 us -> 241 us
    pallas_call x1, Pallas kernels: 245 us -> 237 us  [layer(): pl.pallas_call(layer_kernel, out_shape=[bf16(2, 128, 1024), bf16(2, 128,...]
where the time goes in v6:
time: 241 us
  Pallas kernels  241 us (100%)
    pallas_call x1, Pallas kernels, layer(): pl.pallas_call(layer_kernel, out_shape=[bf16(2, 128, 1024), bf16(2, 128,...  237 us

profile of v6, /device:TPU:0, one launch (start us, length us, event | category | flops | bytes accessed | tf_op | source)
XLA Modules:
  0.0 241.3 jit_solution(17166361449062663422)
XLA Ops:
  0.6 237.3 %layer.1 = (bf16[2,128,1024]{2,1,0:T(8,128)(2,1)}, bf16[2,128,1024]{2,1,0:T(8,128)(2,1)}, bf16[256,512]{1,0:T(8,128)(2,1)}, bf16[256,512]{1,0:T(8,128)(2,1)}, bf...) custom-call(bf16[2,128,1024]{2,1,0:T(8,128)(2,1)} %refs_0_.1, ...), custom_call_target="tpu_custom_call" | custom-call | tf_op jit(solution)/shard_map/layer/pallas_call | solution.py:1594
  238.0 3.3 %finish.1 = (bf16[2,128,1024]{2,1,0:T(8,128)(2,1)}, bf16[2,128,1024]{2,1,0:T(8,128)(2,1)}, f32[256,384]{1,0:T(8,128)}, f32[256,128]{1,0:T(8,128)}, f32[256,512]{...) custom-call(bf16[2,128,1024]{2,1,0:T(8,128)(2,1)} %get-tuple-element, ...), custom_call_target="tpu_custom_call" | custom-call | tf_op jit(solution)/shard_map/finish/pallas_call | solution.py:1689
